TPU v7x, 256 devices: a whole 4x4x8 slice. The times are simulated.
256 devices in a mesh: virt: 2 (over y_lo), occ: 16 (over z, y_hi), aux: 8 (over x, core).
Axes of the slice: x: 4, y: 4 (y_hi: 2, y_lo: 2; y = y_hi * 2 + y_lo), z: 8, core: 2. Of those that a mesh axis runs over, the one named last changes fastest.
Arguments:
- three_index: bfloat16 [16384, 16, 1536], P('aux', 'occ', 'virt'), may hold values from -0.59765625 to 0.59765625
- occupied_energy: bfloat16 [16], P('occ'), may hold values from -2 to -0.5
- virtual_energy: float32 [1536], P('virt'), may hold values from 0.2 to 3
Outputs:
- density: bfloat16 [16384, 16, 1536], P('aux', 'occ', 'virt')
All inputs are finite; a program needn't handle non-finite values.
Results may differ from a plain program's by a relative error of at most 0.0046.
Values may be sent and summed in bfloat16 or wider, within the bound.
No kernel may reach another device: no remote copies, remote signals or barrier semaphores. Data moves between devices by JAX's collectives and lax.ppermute only.
A program may use at most 64 MiB of HBM per device.

v0:
```python
import jax
import jax.numpy as jnp
from jax import lax
from jax.sharding import Mesh
from jax.sharding import PartitionSpec as P

AUX = ("aux_0", "aux_1")


spin_scale = 1.2


def cut_along(value, dim, length):
    before, after = (value.shape[:dim], value.shape[dim + 1 :])
    return jnp.moveaxis(value.reshape(*before, length, -1, *after), dim, 0)


def sent_and_summed(value, axis, dim):
    length = lax.axis_size(axis)
    blocks = lax.all_to_all(cut_along(value, dim, length), axis, 0, 0, tiled=True)
    return jnp.sum(blocks, axis=0)


def cut_rows(length, count):
    unit = 8 if length >= 8 * count else 1
    return [length // unit * k // count * unit for k in range(1, count)]


def all_blocks(value, axes, order):
    blocks = value[None]
    for k in order:
        blocks = lax.all_gather(blocks, axes[k], axis=0, tiled=True)
    current = [lax.axis_size(axes[k]) for k in reversed(order)]
    blocks = blocks.reshape(*current, *value.shape)
    turned = sorted(range(len(order)), key=lambda place: order[len(order) - 1 - place])
    return blocks.transpose(*turned, *range(len(order), blocks.ndim)).reshape(-1, *value.shape)


def in_order(blocks, dim):
    dims = list(blocks.shape[1:])
    dims[dim] *= blocks.shape[0]
    return jnp.moveaxis(blocks, 0, dim).reshape(dims)


def spread_gather(value, axes, dim):
    numbers = list(range(len(axes)))[::-1]
    cut = value.shape.index(max(value.shape[:-1] or value.shape))
    edges = [0, *cut_rows(value.shape[cut], len(axes)), value.shape[cut]]
    gathered = []
    for k, (start, end) in enumerate(zip(edges, edges[1:])):
        if end > start:
            piece = lax.slice_in_dim(value, start, end, axis=cut)
            gathered.append(all_blocks(piece, axes, numbers[k:] + numbers[:k]))
    return in_order(jnp.concatenate(gathered, axis=cut + 1), dim)


def shifted(block, axis, distance):
    devices = range(lax.axis_size(axis))
    route = [((i - distance) % len(devices), i) for i in devices]
    return lax.ppermute(block, axis, route)


def level_matrix(virtual_energy, left_occupied, right_occupied):
    left_levels = (virtual_energy[None, :] - left_occupied.astype(jnp.float32)[:, None]).reshape(-1)
    right_levels = (virtual_energy[None, :] - right_occupied.astype(jnp.float32)[:, None]).reshape(
        -1
    )
    return left_levels[:, None] + right_levels[None, :]


def amplitudes(own_block, far_block, own_energy, far_energy, virtual_energy):
    columns = own_block.shape[1]
    share_rows = columns // lax.axis_size(AUX)
    shared = sent_and_summed(
        lax.dot_general(
            own_block, far_block, (((0,), (0,)), ((), ())), preferred_element_type=jnp.float32
        ),
        AUX,
        0,
    )
    first_row = lax.axis_index(AUX) * share_rows
    denominator = lax.dynamic_slice_in_dim(
        level_matrix(virtual_energy, own_energy, far_energy), first_row, share_rows, 0
    )
    amplitude_rows = (spin_scale * shared / denominator).astype(jnp.bfloat16)
    return spread_gather(amplitude_rows, AUX, 0)


def on_device(three_index, occupied_energy, virtual_energy):
    aux_rows, occ_rows, slab_size = three_index.shape
    own_block = three_index.reshape(aux_rows, occ_rows * slab_size)
    first_index, first_energy = shifted((three_index, occupied_energy), "occ", 1)
    second_index, second_energy = shifted((three_index, occupied_energy), "occ", 2)
    first_block = first_index.reshape(aux_rows, occ_rows * slab_size)
    second_block = second_index.reshape(aux_rows, occ_rows * slab_size)
    later_one = shifted(own_block, "occ", -1)
    later_two = shifted(own_block, "occ", -2)
    first_amplitude = amplitudes(
        own_block, first_block, occupied_energy, first_energy, virtual_energy
    )
    accumulated = lax.dot_general(
        first_block, first_amplitude, (((1,), (1,)), ((), ())), preferred_element_type=jnp.float32
    )
    arrived_one = shifted(first_amplitude, "occ", -1)
    accumulated = accumulated + jnp.dot(later_one, arrived_one, preferred_element_type=jnp.float32)
    second_amplitude = amplitudes(
        own_block, second_block, occupied_energy, second_energy, virtual_energy
    )
    accumulated = accumulated + lax.dot_general(
        second_block, second_amplitude, (((1,), (1,)), ((), ())), preferred_element_type=jnp.float32
    )
    arrived_two = shifted(second_amplitude, "occ", -2)
    accumulated = accumulated + jnp.dot(later_two, arrived_two, preferred_element_type=jnp.float32)
    return accumulated.astype(jnp.bfloat16).reshape(aux_rows, occ_rows, slab_size)


def solution(mesh):
    torus = Mesh(
        mesh.devices.reshape(mesh.shape["virt"], mesh.shape["occ"], 4, 2),
        ("virt", "occ", "aux_0", "aux_1"),
    )
    placed = (P(AUX, "occ", "virt"), P("occ"), P("virt"))
    return jax.shard_map(
        on_device, mesh=torus, in_specs=placed, out_specs=P(AUX, "occ", "virt"), check_vma=False
    )
```

profile of v0, /device:TPU:98, one launch (start us, length us, event | category | flops | bytes accessed | tf_op | source)
XLA Modules:
  0.0 354.2 jit_solution(5099378030142497002)
XLA Ops:
  0.0 3.2 collective-permute-start
  3.2 3.1 collective-permute-start.4
  6.3 3.2 copy.13
  9.6 64.1 %collective-permute-done = bf16[2048,1,768]{2,0,1:T(8,128)(2,1)} collective-permute-done((bf16[2048,1,768]{2,0,1:T(8,128)(2,1)}, bf16[2048,1,768]{2,0,1:T(8,128)(2,1)}, u32[]{:S(2)}, u32[]{:S(2)}) %collective-permute-start) | collective-permute-done | bytes 3145760 | tf_op jit(solution)/shard_map/ppermute | solution.py:60
  73.7 6.0 %fusion.5 = f32[8,96,768]{2,1,0:T(8,128)} fusion(bf16[8,96,2048]{2,1,0:T(8,128)(2,1)S(1)} %bitcast.50, bf16[2048,1,768]{2,0,1:T(8,128)(2,1)} %collective-permute-done), kind=kOutput, calls=%fused_computation.6 | convolution fusion | flops 2415919104 | bytes 8650752 | tf_op jit(solution)/shard_map/dot_general | solution.py:75
  79.7 4.8 %all-to-all-start = ((f32[8,96,768]{2,1,0:T(8,128)}), f32[8,96,768]{2,1,0:T(8,128)S(1)}, u32[]{:S(2)}, u32[]{:S(2)}) async-start(f32[8,96,768]{2,1,0:T(8,128)} %fusion.5), calls=%async_computation | async-start | bytes 4718592 | tf_op jit(solution)/shard_map/all_to_all | solution.py:20
  84.5 6.8 %fusion.1 = f32[8,96,768]{2,1,0:T(8,128)} fusion(bf16[8,96,2048]{2,1,0:T(8,128)(2,1)} %bitcast.51, bf16[2048,1,768]{2,0,1:T(8,128)(2,1)} %collective-permute-done.4), kind=kOutput, calls=%fused_computation.2 | convolution fusion | flops 2415919104 | bytes 8650752 | tf_op jit(solution)/shard_map/dot_general | solution.py:75
  91.3 21.7 %all-to-all-done = f32[8,96,768]{2,1,0:T(8,128)S(1)} async-done(((f32[8,96,768]{2,1,0:T(8,128)}), f32[8,96,768]{2,1,0:T(8,128)S(1)}, u32[]{:S(2)}, u32[]{:S(2)}) %all-to-all-start) | async-done | bytes 2359328 | tf_op jit(solution)/shard_map/all_to_all | solution.py:20
  113.0 5.7 %all-to-all-start.1 = ((f32[8,96,768]{2,1,0:T(8,128)}), f32[8,96,768]{2,1,0:T(8,128)}, u32[]{:S(2)}, u32[]{:S(2)}) async-start(f32[8,96,768]{2,1,0:T(8,128)} %fusion.1), calls=%async_computation.1 | async-start | bytes 4718592 | tf_op jit(solution)/shard_map/all_to_all | solution.py:20
  118.7 34.2 %collective-permute-start.1 = (bf16[1]{0:T(256)(128)(2,1)}, bf16[1]{0:T(256)(128)(2,1)}, u32[]{:S(2)}, u32[]{:S(2)}) collective-permute-start(bf16[1]{0:T(256)(128)(2,1)} %param.4), channel_id=1, source_target_pairs={{120,0},{0,8},{8,16},{16,24},{24,32},{32,40},{40,48},{48,56},{56,6... | collective-permute-start | bytes 14 | tf_op jit(solution)/shard_map/ppermute | solution.py:60
  153.0 3.7 %collective-permute-start.5 = (bf16[1]{0:T(256)(128)(2,1)}, bf16[1]{0:T(256)(128)(2,1)}, u32[]{:S(2)}, u32[]{:S(2)}) collective-permute-start(bf16[1]{0:T(256)(128)(2,1)} %param.4), channel_id=1, source_target_pairs={{112,0},{120,8},{0,16},{8,24},{16,32},{24,40},{32,48},{40,56},{48,... | collective-permute-start | bytes 14 | tf_op jit(solution)/shard_map/ppermute | solution.py:60
  158.0 0.1 collective-permute-done.5
  158.8 0.1 reduce_sum.18
  158.9 1.8 reduce_sum.19
  160.7 0.2 divide_convert_fusion.1
  160.9 12.7 %all-gather.1 = bf16[192,768]{1,0:T(8,128)(2,1)S(1)} all-gather(bf16[48,768]{1,0:T(8,128)(2,1)S(1)} %get-tuple-element.6), channel_id=3, replica_groups=mesh['virt'=2,'occ'=16,'aux_0'=4,'aux_1'=2] {'aux_0'}, dimensions={0}, use_global_device_ids=true | all-gather | bytes 368640 | tf_op jit(solution)/shard_map/all_gather | solution.py:32
  173.6 2.2 all_gather.27
  175.9 1.9 all-gather
  177.8 13.2 %all_gather.25 = bf16[8,48,768]{2,1,0:T(8,128)(2,1)S(1)} all-gather(bf16[2,48,768]{2,1,0:T(8,128)(2,1)S(1)} %bitcast.64), channel_id=1, replica_groups=mesh['virt'=2,'occ'=16,'aux_0'=4,'aux_1'=2] {'aux_0'}, dimensions={0}, use_global_device_ids=true | all-gather | bytes 737280 | tf_op jit(solution)/shard_map/all_gather | solution.py:32
  191.1 20.4 %collective-permute-start.2 = (bf16[768,768]{1,0:T(8,128)(2,1)S(1)}, bf16[768,768]{1,0:T(8,128)(2,1)S(1)}, u32[]{:S(2)}, u32[]{:S(2)}) collective-permute-start(bf16[768,768]{1,0:T(8,128)(2,1)S(1)} %bitcast.60), channel_id=1, source_target_pairs={{8,0},{16,8},{24,16},{32,24},{40,32},{48,40},{56,48},{64,56},{72,6... | collective-permute-start | bytes 3538952 | tf_op jit(solution)/shard_map/ppermute | solution.py:60
  211.5 12.7 %all-gather.3 = bf16[192,768]{1,0:T(8,128)(2,1)S(1)} all-gather(bf16[48,768]{1,0:T(8,128)(2,1)S(1)} %get-tuple-element.8), channel_id=5, replica_groups=mesh['virt'=2,'occ'=16,'aux_0'=4,'aux_1'=2] {'aux_0'}, dimensions={0}, use_global_device_ids=true | all-gather | bytes 368640 | tf_op jit(solution)/shard_map/all_gather | solution.py:32
  224.2 2.2 all_gather.31
  226.5 1.9 all-gather.2
  228.4 12.9 %all_gather.29 = bf16[8,48,768]{2,1,0:T(8,128)(2,1)S(1)} all-gather(bf16[2,48,768]{2,1,0:T(8,128)(2,1)S(1)} %bitcast.65), channel_id=1, replica_groups=mesh['virt'=2,'occ'=16,'aux_0'=4,'aux_1'=2] {'aux_0'}, dimensions={0}, use_global_device_ids=true | all-gather | bytes 737280 | tf_op jit(solution)/shard_map/all_gather | solution.py:32
  241.4 0.4 collective-permute-start.6
  241.7 4.5 %fusion.7 = f32[768,2048]{1,0:T(8,128)S(1)} fusion(bf16[768,768]{1,0:T(8,128)(2,1)S(1)} %bitcast.61, bf16[2048,1,768]{2,0,1:T(8,128)(2,1)} %collective-permute-done), kind=kOutput, calls=%fused_computation.8 | convolution fusion | flops 2415919104 | bytes 10616832 | tf_op jit(solution)/shard_map/dot_general | solution.py:101
  246.2 4.5 %fusion.3 = f32[768,2048]{1,0:T(8,128)S(1)} fusion(bf16[768,768]{1,0:T(8,128)(2,1)S(1)} %bitcast.63, bf16[2048,1,768]{2,0,1:T(8,128)(2,1)} %collective-permute-done.4), kind=kOutput, calls=%fused_computation.4 | convolution fusion | flops 2415919104 | bytes 10616832 | tf_op jit(solution)/shard_map/dot_general | solution.py:109
  250.8 67.3 %collective-permute-done.2 = bf16[768,768]{1,0:T(8,128)(2,1)S(1)} collective-permute-done((bf16[768,768]{1,0:T(8,128)(2,1)S(1)}, bf16[768,768]{1,0:T(8,128)(2,1)S(1)}, u32[]{:S(2)}, u32[]{:S(2)}) %collective-permute-start.2) | collective-permute-done | bytes 1179680 | tf_op jit(solution)/shard_map/ppermute | solution.py:60
  318.1 4.6 %fusion.11 = f32[768,2048]{1,0:T(8,128)S(1)} fusion(bf16[768,768]{1,0:T(8,128)(2,1)S(1)} %collective-permute-done.2, bf16[2048,768]{0,1:T(8,128)(2,1)} %collective-permute-done.3), kind=kOutput, calls=%fused_computation.19 | convolution fusion | flops 2415919104 | bytes 10616832 | tf_op jit(solution)/shard_map/dot_general | solution.py:105
  322.7 22.8 %collective-permute-done.6 = bf16[768,768]{1,0:T(8,128)(2,1)} collective-permute-done((bf16[768,768]{1,0:T(8,128)(2,1)S(1)}, bf16[768,768]{1,0:T(8,128)(2,1)}, u32[]{:S(2)}, u32[]{:S(2)}) %collective-permute-start.6) | collective-permute-done | bytes 1179680 | tf_op jit(solution)/shard_map/ppermute | solution.py:60
  345.5 5.9 %fusion = bf16[2048,1,768]{0,2,1:T(8,128)(2,1)S(1)} fusion(f32[768,2048]{1,0:T(8,128)S(1)} %fusion.3, f32[768,2048]{1,0:T(8,128)S(1)} %fusion.7, f32[768,2048]{1,0:T(8,128)S(1)} %fusion.11, bf16[768,768]{1,0:T(8,128)(2,1)} %collective-permute-done.6, bf16[2048,768]{0,1:T(8,128)(2,1)} %collective-permute-done.7), kind=kOutput, calls=%fused_computation.1 | convolution fusion | flops 2422210560 | bytes 26345472 | tf_op jit(solution)/shard_map/dot_general | solution.py:113
  351.4 2.8 copy.16
  (19 shorter events, 0.4 us)
Async XLA Ops:
  0.0 73.7 %collective-permute-start = (bf16[2048,1,768]{2,0,1:T(8,128)(2,1)}, bf16[2048,1,768]{2,0,1:T(8,128)(2,1)}, u32[]{:S(2)}, u32[]{:S(2)}) collective-permute-start(bf16[2048,1,768]{2,0,1:T(8,128)(2,1)} %param.3), channel_id=1, source_target_pairs={{120,0},{0,8},{8,16},{16,24},{24,32},{32,40},{40,48},{48,56},{56,6... | collective-permute-start | bytes 9437192 | tf_op jit(solution)/shard_map/ppermute | solution.py:60
  3.2 81.3 %collective-permute-start.4 = (bf16[2048,1,768]{2,0,1:T(8,128)(2,1)}, bf16[2048,1,768]{2,0,1:T(8,128)(2,1)}, u32[]{:S(2)}, u32[]{:S(2)}) collective-permute-start(bf16[2048,1,768]{2,0,1:T(8,128)(2,1)} %param.3), channel_id=1, source_target_pairs={{112,0},{120,8},{0,16},{8,24},{16,32},{24,40},{32,48},{40,56},{48,... | collective-permute-start | bytes 9437192 | tf_op jit(solution)/shard_map/ppermute | solution.py:60
  9.5 70.1 %copy-start = (bf16[2048,1,768]{0,2,1:T(8,128)(2,1)}, bf16[2048,1,768]{0,2,1:T(8,128)(2,1)S(1)}, u32[]{:S(2)}) copy-start(bf16[2048,1,768]{0,2,1:T(8,128)(2,1)S(1)} %copy.13) | copy-start | bytes 9437188
  79.7 33.4 %all-to-all-start = ((f32[8,96,768]{2,1,0:T(8,128)}), f32[8,96,768]{2,1,0:T(8,128)S(1)}, u32[]{:S(2)}, u32[]{:S(2)}) async-start(f32[8,96,768]{2,1,0:T(8,128)} %fusion.5), calls=%async_computation | async-start | bytes 4718592 | tf_op jit(solution)/shard_map/all_to_all | solution.py:20
  91.3 67.3 %copy-start.1 = (f32[768]{0:T(1024)S(1)}, f32[768]{0:T(1024)}, u32[]{:S(2)}) copy-start(f32[768]{0:T(1024)} %param.5) | copy-start | bytes 9220
  113.0 45.9 %all-to-all-start.1 = ((f32[8,96,768]{2,1,0:T(8,128)}), f32[8,96,768]{2,1,0:T(8,128)}, u32[]{:S(2)}, u32[]{:S(2)}) async-start(f32[8,96,768]{2,1,0:T(8,128)} %fusion.1), calls=%async_computation.1 | async-start | bytes 4718592 | tf_op jit(solution)/shard_map/all_to_all | solution.py:20
  118.7 38.6 %collective-permute-start.1 = (bf16[1]{0:T(256)(128)(2,1)}, bf16[1]{0:T(256)(128)(2,1)}, u32[]{:S(2)}, u32[]{:S(2)}) collective-permute-start(bf16[1]{0:T(256)(128)(2,1)} %param.4), channel_id=1, source_target_pairs={{120,0},{0,8},{8,16},{16,24},{24,32},{32,40},{40,48},{48,56},{56,6... | collective-permute-start | bytes 14 | tf_op jit(solution)/shard_map/ppermute | solution.py:60
  153.0 5.1 %collective-permute-start.5 = (bf16[1]{0:T(256)(128)(2,1)}, bf16[1]{0:T(256)(128)(2,1)}, u32[]{:S(2)}, u32[]{:S(2)}) collective-permute-start(bf16[1]{0:T(256)(128)(2,1)} %param.4), channel_id=1, source_target_pairs={{112,0},{120,8},{0,16},{8,24},{16,32},{24,40},{32,48},{40,56},{48,... | collective-permute-start | bytes 14 | tf_op jit(solution)/shard_map/ppermute | solution.py:60
  156.7 94.1 %collective-permute-start.3 = (bf16[2048,768]{0,1:T(8,128)(2,1)}, bf16[2048,768]{0,1:T(8,128)(2,1)}, u32[]{:S(2)}, u32[]{:S(2)}) collective-permute-start(bf16[2048,768]{0,1:T(8,128)(2,1)} %bitcast.52), channel_id=1, source_target_pairs={{8,0},{16,8},{24,16},{32,24},{40,32},{48,40},{56,48},{64,56},{72,6... | collective-permute-start | bytes 9437192 | tf_op jit(solution)/shard_map/ppermute | solution.py:60
  156.7 166.0 %collective-permute-start.7 = (bf16[2048,768]{0,1:T(8,128)(2,1)}, bf16[2048,768]{0,1:T(8,128)(2,1)}, u32[]{:S(2)}, u32[]{:S(2)}) collective-permute-start(bf16[2048,768]{0,1:T(8,128)(2,1)} %bitcast.53), channel_id=1, source_target_pairs={{16,0},{24,8},{32,16},{40,24},{48,32},{56,40},{64,48},{72,56},{80,... | collective-permute-start | bytes 9437192 | tf_op jit(solution)/shard_map/ppermute | solution.py:60
  191.1 127.0 %collective-permute-start.2 = (bf16[768,768]{1,0:T(8,128)(2,1)S(1)}, bf16[768,768]{1,0:T(8,128)(2,1)S(1)}, u32[]{:S(2)}, u32[]{:S(2)}) collective-permute-start(bf16[768,768]{1,0:T(8,128)(2,1)S(1)} %bitcast.60), channel_id=1, source_target_pairs={{8,0},{16,8},{24,16},{32,24},{40,32},{48,40},{56,48},{64,56},{72,6... | collective-permute-start | bytes 3538952 | tf_op jit(solution)/shard_map/ppermute | solution.py:60
  241.4 104.1 %collective-permute-start.6 = (bf16[768,768]{1,0:T(8,128)(2,1)S(1)}, bf16[768,768]{1,0:T(8,128)(2,1)}, u32[]{:S(2)}, u32[]{:S(2)}) collective-permute-start(bf16[768,768]{1,0:T(8,128)(2,1)S(1)} %bitcast.62), channel_id=1, source_target_pairs={{16,0},{24,8},{32,16},{40,24},{48,32},{56,40},{64,48},{72,56},{80,... | collective-permute-start | bytes 3538952 | tf_op jit(solution)/shard_map/ppermute | solution.py:60
where the time goes:
time: 355 us; the launch traced here: 354 us
  waiting for transfers between devices  176 us (50%)
  starting transfers between devices  75.6 us (21%)
  blocking collectives  59.8 us (17%)
  matrix products  32.3 us (9%)
  local copies, waits for them, and re-layouts  6.2 us (2%)
    ppermute x8, waiting for transfers between devices, shifted(): return lax.ppermute(block, axis, route)  154 us
    ppermute x8, starting transfers between devices, shifted(): return lax.ppermute(block, axis, route)  65 us
    all_gather x8, blocking collectives, all_blocks(): blocks = lax.all_gather(blocks, axes[k], axis=0, tiled=True)  59.8 us
    all_to_all x2, waiting for transfers between devices, sent_and_summed(): lax.all_to_all(cut_along(value, dim, length), axis, 0, 0, tiled=True)  21.7 us
    dot_general x2, matrix products, amplitudes(): lax.dot_general(own_block, far_block, (((0,), (0,)), ((), ())), preferred...  12.8 us
    all_to_all x2, starting transfers between devices, sent_and_summed(): lax.all_to_all(cut_along(value, dim, length), axis, 0, 0, tiled=True)  10.6 us
  transfers between devices with their start and end apart: 10, of which 5 were waited for; matrix products, arithmetic and copies ran while one was open for 9% of the time, Pallas kernels for 0%

commit v1 on v0

v1 whole, which is shorter than its diff:
```python
import jax
import jax.numpy as jnp
from jax import lax
from jax.experimental import pallas as pl
from jax.experimental.pallas import tpu as pltpu
from jax.sharding import Mesh
from jax.sharding import PartitionSpec as P


SPIN_SCALE = 1.2
X, C = 4, 2
F32, BF16 = jnp.float32, jnp.bfloat16
NN = (((1,), (0,)), ((), ()))
NT = (((1,), (1,)), ((), ()))


def mm(left, right, dims):
    return lax.dot_general(left, right, dims, preferred_element_type=F32)


def on_chip(kernel, where, operands, results, scratch, flops, off_chip=()):
    vmem, anywhere = (pl.BlockSpec(memory_space=m) for m in (pltpu.VMEM, pl.ANY))
    held = [pltpu.with_memory_space_constraint(v, pltpu.VMEM) for v in operands]
    chip = off_chip == ()
    return pl.pallas_call(
        kernel,
        in_specs=[pl.BlockSpec(memory_space=pltpu.SMEM)]
        + [anywhere] * len(off_chip or ())
        + [vmem] * len(held),
        out_specs=[vmem if chip else anywhere] * len(results),
        out_shape=[pltpu.VMEM(*r) if chip else jax.ShapeDtypeStruct(*r) for r in results],
        scratch_shapes=scratch,
        compiler_params=pltpu.CompilerParams(vmem_limit_bytes=20 << 20),
        cost_estimate=pl.CostEstimate(flops=flops, bytes_accessed=flops // 1000, transcendentals=0),
    )(where, *(off_chip or ()), *held)


def ring(axis, distance):
    size = lax.axis_size(axis)
    return [(i, (i + distance) % size) for i in range(size)]


def after(value, *events):
    return lax.optimization_barrier((value, *events))[0]


def add_products(core, lefts, rights, send, keep):
    part, n = send.shape[2:]
    half, strip = part * X, 256

    def step(j, carry):
        columns = pl.ds(pl.multiple_of(j * strip, strip), strip)
        for side, out in ((1 - core, send), (core, keep)):
            rows = pl.ds(pl.multiple_of(side * half, 128), half)
            for place in range(2):
                product = mm(lefts[place][rows, :], rights[place][:, columns], NN)
                for k in range(X):
                    out[k, place, :, columns] = product[k * part : (k + 1) * part]
        return carry

    lax.fori_loop(0, n // strip, step, 0)


def turn(block, out):
    strip = 256

    def step(j, carry):
        part = pl.ds(pl.multiple_of(j * strip, strip), strip)
        out[part, :] = block[:, part].T
        return carry

    lax.fori_loop(0, block.shape[1] // strip, step, 0)


def far_pairs_kernel(where, own_high, behind, ahead, own_low, send, keep, *lefts):
    turn(own_high, lefts[0])
    turn(behind, lefts[1])
    add_products(where[1], lefts, (ahead, own_low), send, keep)


def near_pairs_kernel(where, behind, partner, ahead, own, send, keep, *lefts):
    @pl.when(where[0] == 0)
    def _():
        turn(partner, lefts[0])
        turn(behind, lefts[1])
        add_products(where[1], lefts, (own, partner), send, keep)

    @pl.when(where[0] == 1)
    def _():
        turn(own, lefts[0])
        turn(partner, lefts[1])
        add_products(where[1], lefts, (partner, ahead), send, keep)


def pair_call(kernel, where, operands):
    half, n = operands[-1].shape
    result = ((X, 2, n // (X * C), n), F32)
    lefts = [pltpu.VMEM((n, half), BF16)] * 2
    return on_chip(kernel, where, operands, [result, result], lefts, 4 * half * n * n)


def assemble(where, mine, other, full):
    part = mine.shape[2]
    core = where[1]
    for pieces, side in ((mine, core), (other, 1 - core)):
        for j in range(X):
            row = pl.multiple_of(side * (part * X) + j * part, 32)
            for place in range(2):
                full[place, pl.ds(row, part), :] = pieces[j, place]


STEP_ROWS = 256


def row_block(k):
    return pl.ds(pl.multiple_of(k * STEP_ROWS, STEP_ROWS), STEP_ROWS)


def far_terms_kernel(
    where, mine, other, ahead0, ahead1, behind0, behind1, out, full, ready, sent
):
    assemble(where, mine, other, full)
    steps = ahead0.shape[0] // STEP_ROWS

    def sending(k):
        rows = row_block(k)
        return pltpu.make_async_copy(ready.at[:, rows, :], out.at[:, rows, :], sent.at[k])

    def step(k, carry):
        rows = row_block(k)
        for place, (ahead, behind) in enumerate(((ahead0, behind0), (ahead1, behind1))):
            value = mm(ahead[rows, :], full[0], NT) + mm(behind[rows, :], full[1], NN)
            ready[place, rows, :] = value
        sending(k).start()
        return carry

    lax.fori_loop(0, steps, step, 0)
    for k in range(steps):
        sending(k).wait()


def near_terms_kernel(where, total, mine, other, *refs):
    partner_near, partner_far, near_a, near_b, far_a, far_b = refs[:6]
    out, full, loaded, ready, arrived, sent = refs[6:]
    steps = near_a.shape[0] // STEP_ROWS

    def loading(k):
        rows = row_block(k)
        return pltpu.make_async_copy(total.at[:, rows, :], loaded.at[:, rows, :], arrived.at[k])

    def sending(k):
        rows = row_block(k)
        return pltpu.make_async_copy(ready.at[:, rows, :], out.at[:, rows, :], sent.at[k])

    for k in range(2 * steps):
        loading(k).start()
    assemble(where, mine, other, full)

    def add(side, partner_dims, diagonal_dims):
        for part, diagonals in enumerate(((near_a, far_a), (near_b, far_b))):

            def step(k, carry, part=part, diagonals=diagonals):
                local, number = row_block(k), part * steps + k
                rows = row_block(number)
                loading(number).wait()
                for place, partner, diagonal in (
                    (side, partner_near, diagonals[0]),
                    (1 - side, partner_far, diagonals[1]),
                ):
                    value = loaded[place, rows, :] + mm(partner[rows, :], full[0], partner_dims)
                    value = value + mm(diagonal[local, :], full[1], diagonal_dims)
                    ready[place, rows, :] = value.astype(ready.dtype)
                sending(number).start()
                return carry

            lax.fori_loop(0, steps, step, 0)

    @pl.when(where[0] == 0)
    def _():
        add(0, NN, NT)

    @pl.when(where[0] == 1)
    def _():
        add(1, NT, NN)

    for k in range(2 * steps):
        sending(k).wait()


def core_swap(value):
    return lax.ppermute(value, "c", [(0, 1), (1, 0)])


def exchanged(blocks):
    return lax.all_to_all(blocks, "x", 0, 0, tiled=True)


def summed_rows(send, keep):
    paired = (keep + core_swap(send)).astype(BF16)
    return jnp.sum(exchanged(paired).astype(F32), axis=0)


def amplitude_rows(sums, left_levels, right_levels):
    denominator = left_levels[:, None] + right_levels[None, :]
    return (SPIN_SCALE * sums / denominator).astype(BF16)


def gathered(rows):
    mine = exchanged(jnp.broadcast_to(rows, (X, *rows.shape)))
    return mine, core_swap(mine)


def on_device(three_index, occupied_energy, virtual_energy):
    rows, _, n = three_index.shape
    half, quarter = rows // 2, rows // 4
    own = three_index.reshape(rows, n)
    h, c, x = lax.axis_index("h"), lax.axis_index("c"), lax.axis_index("x")
    where = jnp.stack([h, c, x]).astype(jnp.int32)
    even = h == 0
    zh = lax.axis_size("z") * 2
    swap_h = [(0, 1), (1, 0)]
    along_route = [(i, (i + (2 if i % 2 == 0 else -2)) % zh) for i in range(zh)]

    def ahead_of(value):
        return lax.ppermute(value, "z", ring("z", 1))

    def behind_of(value):
        return lax.ppermute(value, "z", ring("z", -1))

    def partner_of(value):
        return lax.ppermute(value, "h", swap_h)

    def along(value):
        return lax.ppermute(value, ("z", "h"), along_route)

    def energy(axis, route):
        return lax.ppermute(occupied_energy, axis, route).astype(F32)

    def cut(value, start, length):
        return lax.dynamic_slice_in_dim(value, start, length, 0)

    high = cut(own, half, half)
    low = cut(after(own, high), 0, half)
    far = cut(after(own, low), (1 - h) * half, half)
    near = cut(after(own, far), h * half, half)
    ahead1 = ahead_of(high)
    behind0 = behind_of(low)
    partner_near = partner_of(far)

    ahead0 = ahead_of(low)
    behind1 = behind_of(high)
    partner_far = partner_of(near)

    own_e = occupied_energy.astype(F32)
    ahead_e = energy("z", ring("z", 1))
    behind_e = energy("z", ring("z", -1))
    partner_e = energy("h", swap_h)
    diagonal_e = energy(("z", "h"), [(i, (i + (1 if i % 2 else -1)) % zh) for i in range(zh)])

    far_send, far_keep = pair_call(far_pairs_kernel, where, (high, behind0, ahead1, low))
    near_send, near_keep = pair_call(
        near_pairs_kernel, where, (behind0, partner_near, ahead1, near)
    )

    def facing(start):
        cuts = (v[start : start + quarter] for v in (behind0, ahead1))
        return jnp.where(even, *cuts)

    far_a = partner_of(facing(0))
    far_b = partner_of(facing(quarter))
    near_a = along(partner_near[:quarter])
    near_b = along(partner_near[quarter:])

    far_sums = summed_rows(far_send, far_keep)
    near_sums = summed_rows(near_send, near_keep)

    far_wire = far_sums.astype(BF16)
    from_ahead = ahead_of(far_wire[1])
    from_behind = behind_of(far_wire[0])
    near_wire = near_sums.astype(BF16)
    from_partner = partner_of(near_wire)
    from_along = along(near_wire[1])

    share = n // (X * C)
    my_levels = lax.dynamic_slice_in_dim(virtual_energy, c * (n // C) + x * share, share, 0)

    def levels(left_e, right_e):
        return my_levels - left_e, virtual_energy - right_e

    far_rows = jnp.stack(
        [
            amplitude_rows(far_sums[0] + from_ahead.astype(F32), *levels(own_e, ahead_e)),
            amplitude_rows(far_sums[1] + from_behind.astype(F32), *levels(behind_e, own_e)),
        ]
    )
    from_partner = after(from_partner, far_rows)
    near_rows = jnp.stack(
        [
            amplitude_rows(
                near_sums[0] + from_partner[0].astype(F32),
                *levels(jnp.where(even, partner_e, own_e), jnp.where(even, own_e, partner_e)),
            ),
            amplitude_rows(
                from_partner[1].astype(F32) + from_along.astype(F32),
                *levels(jnp.where(even, own_e, diagonal_e), jnp.where(even, diagonal_e, own_e)),
            ),
        ]
    )

    full = pltpu.VMEM((2, n, n), BF16)
    copies = pltpu.SemaphoreType.DMA((half // STEP_ROWS,))
    work = 8 * half * n * n
    (total,) = on_chip(
        far_terms_kernel,
        where,
        (*gathered(far_rows), ahead0, ahead1, behind0, behind1),
        [((2, half, n), F32)],
        [full, pltpu.VMEM((2, half, n), F32), copies],
        work,
        off_chip=None,
    )
    (density,) = on_chip(
        near_terms_kernel,
        where,
        (
            *gathered(near_rows),
            *(partner_near, partner_far, near_a, near_b, far_a, far_b),
        ),
        [((2, half, n), BF16)],
        [
            full,
            pltpu.VMEM((2, half, n), F32),
            pltpu.VMEM((2, half, n), BF16),
            copies,
            copies,
        ],
        work,
        off_chip=(total,),
    )
    return density.reshape(three_index.shape)


def solution(mesh):
    torus = Mesh(
        mesh.devices.reshape(mesh.shape["virt"], mesh.shape["occ"] // 2, 2, X, C),
        ("v", "z", "h", "x", "c"),
    )
    placed = P(("x", "c"), ("z", "h"), "v")
    return jax.shard_map(
        on_device,
        mesh=torus,
        in_specs=(placed, P(("z", "h")), P("v")),
        out_specs=placed,
        check_vma=False,
    )
```

time: 355 us -> 208 us (0.59)
  the two profiles are of different devices: /device:TPU:98 before, /device:TPU:24 now
where the time goes in v1:
time: 208 us; the launch traced here: 207 us
  waiting for transfers between devices  91.2 us (44%)
  starting transfers between devices  47.6 us (23%)
  Pallas kernels  33.1 us (16%)
  local copies, waits for them, and re-layouts  17.2 us (8%)
  other arithmetic  13.4 us (6%)
  between operations  4.87 us (2%)
    pallas_call x4, Pallas kernels, on_chip(): pl.pallas_call(kernel, in_specs=[pl.BlockSpec(memory_space=pltpu.SMEM)] +...  33.1 us
    all_to_all x4, waiting for transfers between devices, exchanged(): return lax.all_to_all(blocks, 'x', 0, 0, tiled=True)  33.1 us
    ppermute x3, waiting for transfers between devices, behind_of(): return lax.ppermute(value, 'z', ring('z', -1))  31.3 us
    ppermute x3, waiting for transfers between devices, along(): return lax.ppermute(value, ('z', 'h'), along_route)  18.2 us
    all_to_all x4, starting transfers between devices, exchanged(): return lax.all_to_all(blocks, 'x', 0, 0, tiled=True)  15.8 us
    ppermute x3, starting transfers between devices, behind_of(): return lax.ppermute(value, 'z', ring('z', -1))  11 us
    dynamic_slice x4, local copies, waits for them, and re-layouts, cut(): return lax.dynamic_slice_in_dim(value, start, length, 0)  9.48 us
    ppermute x5, starting transfers between devices, partner_of(): return lax.ppermute(value, 'h', swap_h)  7.64 us
  transfers between devices with their start and end apart: 26, of which 12 were waited for; matrix products, arithmetic and copies ran while one was open for 11% of the time, Pallas kernels for 12%

profile of v1, /device:TPU:24, one launch (start us, length us, event | category | flops | bytes accessed | tf_op | source)
XLA Modules:
  0.0 207.3 jit_solution(8971966819052614046)
XLA Ops:
  0.0 2.9 %slice_bitcast_fusion.own_high = bf16[1024,768]{1,0:T(8,128)(2,1)} fusion(bf16[2048,1,768]{2,0,1:T(8,128)(2,1)} %param.3), kind=kLoop, calls=%fused_computation.4 | loop fusion | bytes 3145728 | tf_op jit(solution)/shard_map/dynamic_slice | solution.py:240
  4.1 5.9 %collective-permute-start = (bf16[1024,768]{1,0:T(8,128)(2,1)}, bf16[1024,768]{1,0:T(8,128)(2,1)S(1)}, u32[]{:S(2)}, u32[]{:S(2)}) collective-permute-start(bf16[1024,768]{1,0:T(8,128)(2,1)} %dynamic_slice.19.own_low), channel_id=1, source_target_pairs={{0,112},{16,0},{32,16},{48,32},{64,48},{80,64},{96,80},{112,96},{1... | collective-permute-start | bytes 4718600 | tf_op jit(solution)/shard_map/ppermute | solution.py:228
  10.0 2.7 %constant_dynamic-slice_fusion.1 = bf16[1024,768]{1,0:T(8,128)(2,1)} fusion(bf16[2048,768]{1,0:T(8,128)(2,1)} %bitcast.58, s32[]{:T(128)S(6)} %select_n.42), kind=kLoop, calls=%fused_computation.39 | loop fusion | bytes 3145732 | tf_op jit(solution)/shard_map/dynamic_slice | solution.py:240
  14.0 30.0 %collective-permute-done.behind.behind0 = bf16[1024,768]{1,0:T(8,128)(2,1)S(1)} collective-permute-done((bf16[1024,768]{1,0:T(8,128)(2,1)}, bf16[1024,768]{1,0:T(8,128)(2,1)S(1)}, u32[]{:S(2)}, u32[]{:S(2)}) %collective-permute-start) | collective-permute-done | bytes 1572896 | tf_op jit(solution)/shard_map/ppermute | solution.py:228
  44.0 3.4 %collective-permute-done.1.ahead.ahead1 = bf16[1024,768]{1,0:T(8,128)(2,1)} collective-permute-done((bf16[1024,768]{1,0:T(8,128)(2,1)}, bf16[1024,768]{1,0:T(8,128)(2,1)}, u32[]{:S(2)}, u32[]{:S(2)}) %collective-permute-start.1) | collective-permute-done | bytes 1572896 | tf_op jit(solution)/shard_map/ppermute | solution.py:225
  47.4 7.6 %shard_map.37 = (f32[4,2,96,768]{3,2,1,0:T(8,128)}, f32[4,2,96,768]{3,2,1,0:T(8,128)S(1)}) custom-call(s32[3]{0:T(128)S(1)} %pad_add_fusion.where, bf16[1024,768]{1,0:T(8,128)(2,1)} %slice_bitcast_fusion.own_high, bf16[1024,768]{1,0:T(8,128)(2,1)S(1)} %collective-permute-done.behind.behind0, bf16[1024,768]{1,0:T(8,128)(2,1)} %collective-permute-done.1.ahead.ahead1, ...), custom_call_target="tpu_custom_call" | custom-call | flops 2415919104 | bytes 2415919 | tf_op jit(solution)/shard_map/pallas_call | solution.py:25
  54.9 1.4 copy-done.1
  56.4 2.7 %constant_dynamic-slice_fusion.own = bf16[1024,768]{1,0:T(8,128)(2,1)} fusion(bf16[2048,768]{1,0:T(8,128)(2,1)} %bitcast.59, s32[]{:T(128)S(6)} %select_n.43), kind=kLoop, calls=%fused_computation.38 | loop fusion | bytes 3145732 | tf_op jit(solution)/shard_map/dynamic_slice | solution.py:240
  59.1 7.7 %shard_map.39 = (f32[4,2,96,768]{3,2,1,0:T(8,128)}, f32[4,2,96,768]{3,2,1,0:T(8,128)S(1)}) custom-call(s32[3]{0:T(128)S(1)} %pad_add_fusion.where, bf16[1024,768]{1,0:T(8,128)(2,1)S(1)} %collective-permute-done.behind.behind0, bf16[1024,768]{1,0:T(8,128)(2,1)S(1)} %collective-permute-done.10.partner.refs_0_, ...), custom_call_target="tpu_custom_call" | custom-call | flops 2415919104 | bytes 2415919 | tf_op jit(solution)/shard_map/pallas_call | solution.py:25
  68.7 3.0 %add_convert_fusion.1 = bf16[4,2,96,768]{3,2,1,0:T(8,128)(2,1)} fusion(f32[4,2,96,768]{3,2,1,0:T(8,128)S(1)} %copy-done.2, f32[4,2,96,768]{3,2,1,0:T(8,128)} %collective-permute-done.2), kind=kLoop, calls=%fused_computation.3 | loop fusion | flops 1179648 | bytes 5898240 | tf_op jit(solution)/shard_map/convert_element_type | solution.py:199
  71.7 4.3 %all-to-all-start = ((bf16[4,2,96,768]{3,2,1,0:T(8,128)(2,1)}), bf16[4,2,96,768]{3,2,1,0:T(8,128)(2,1)S(1)}, u32[]{:S(2)}, u32[]{:S(2)}) async-start(bf16[4,2,96,768]{3,2,1,0:T(8,128)(2,1)} %add_convert_fusion.1), calls=%async_computation | async-start | bytes 2359296 | tf_op jit(solution)/shard_map/all_to_all | solution.py:195
  78.0 4.2 %collective-permute-start.6 = (bf16[1]{0:T(256)(128)(2,1)}, bf16[1]{0:T(256)(128)(2,1)}, u32[]{:S(2)}, u32[]{:S(2)}) collective-permute-start(bf16[1]{0:T(256)(128)(2,1)} %param.4), channel_id=1, source_target_pairs={{0,112},{16,0},{32,16},{48,32},{64,48},{80,64},{96,80},{112,96},{1... | collective-permute-start | bytes 14 | tf_op jit(solution)/shard_map/ppermute | solution.py:237
  83.5 3.7 %add_convert_fusion = bf16[4,2,96,768]{3,2,1,0:T(8,128)(2,1)} fusion(f32[4,2,96,768]{3,2,1,0:T(8,128)} %copy-done, f32[4,2,96,768]{3,2,1,0:T(8,128)} %collective-permute-done.11), kind=kLoop, calls=%fused_computation.1 | loop fusion | flops 1179648 | bytes 5898240 | tf_op jit(solution)/shard_map/convert_element_type | solution.py:199
  87.2 5.4 %all-to-all-done = bf16[4,2,96,768]{3,2,1,0:T(8,128)(2,1)S(1)} async-done(((bf16[4,2,96,768]{3,2,1,0:T(8,128)(2,1)}), bf16[4,2,96,768]{3,2,1,0:T(8,128)(2,1)S(1)}, u32[]{:S(2)}, u32[]{:S(2)}) %all-to-all-start) | async-done | bytes 1179680 | tf_op jit(solution)/shard_map/all_to_all | solution.py:195
  92.6 4.3 %all-to-all-start.2 = ((bf16[4,2,96,768]{3,2,1,0:T(8,128)(2,1)}), bf16[4,2,96,768]{3,2,1,0:T(8,128)(2,1)}, u32[]{:S(2)}, u32[]{:S(2)}) async-start(bf16[4,2,96,768]{3,2,1,0:T(8,128)(2,1)} %add_convert_fusion), calls=%async_computation.2 | async-start | bytes 2359296 | tf_op jit(solution)/shard_map/all_to_all | solution.py:195
  100.5 3.2 %collective-permute-start.5 = (bf16[96,768]{1,0:T(8,128)(2,1)S(1)}, bf16[96,768]{1,0:T(8,128)(2,1)S(1)}, u32[]{:S(2)}, u32[]{:S(2)}) collective-permute-start(bf16[96,768]{1,0:T(8,128)(2,1)S(1)} %get-tuple-element.30), channel_id=1, source_target_pairs={{0,112},{16,0},{32,16},{48,32},{64,48},{80,64},{96,80},{112,96},{1... | collective-permute-start | bytes 442376 | tf_op jit(solution)/shard_map/ppermute | solution.py:228
  103.8 9.0 %all-to-all-done.2 = bf16[4,2,96,768]{3,2,1,0:T(8,128)(2,1)} async-done(((bf16[4,2,96,768]{3,2,1,0:T(8,128)(2,1)}), bf16[4,2,96,768]{3,2,1,0:T(8,128)(2,1)}, u32[]{:S(2)}, u32[]{:S(2)}) %all-to-all-start.2) | async-done | bytes 1179680 | tf_op jit(solution)/shard_map/all_to_all | solution.py:195
  112.8 1.5 convert_reduce_fusion
  117.7 3.7 %all-to-all-start.1 = ((bf16[4,2,96,768]{3,2,1,0:T(8,128)(2,1)}), bf16[4,2,96,768]{3,2,1,0:T(8,128)(2,1)S(1)}, u32[]{:S(2)}, u32[]{:S(2)}) async-start(bf16[4,2,96,768]{3,2,1,0:T(8,128)(2,1)} %broadcast_in_dim.4), calls=%async_computation.1 | async-start | bytes 2359296 | tf_op jit(solution)/shard_map/all_to_all | solution.py:195
  124.4 2.0 collective-permute-start.9
  126.4 1.6 collective-permute-start.17
  131.2 4.8 %all-to-all-done.1.mine = bf16[4,2,96,768]{3,2,1,0:T(8,128)(2,1)S(1)} async-done(((bf16[4,2,96,768]{3,2,1,0:T(8,128)(2,1)}), bf16[4,2,96,768]{3,2,1,0:T(8,128)(2,1)S(1)}, u32[]{:S(2)}, u32[]{:S(2)}) %all-to-all-start.1) | async-done | bytes 1179680 | tf_op jit(solution)/shard_map/all_to_all | solution.py:195
  137.4 3.5 %all-to-all-start.3 = ((bf16[4,2,96,768]{3,2,1,0:T(8,128)(2,1)}), bf16[4,2,96,768]{3,2,1,0:T(8,128)(2,1)S(1)}, u32[]{:S(2)}, u32[]{:S(2)}) async-start(bf16[4,2,96,768]{3,2,1,0:T(8,128)(2,1)} %broadcast_in_dim.5), calls=%async_computation.3 | async-start | bytes 2359296 | tf_op jit(solution)/shard_map/all_to_all | solution.py:195
  141.1 13.8 %all-to-all-done.3.mine = bf16[4,2,96,768]{3,2,1,0:T(8,128)(2,1)S(1)} async-done(((bf16[4,2,96,768]{3,2,1,0:T(8,128)(2,1)}), bf16[4,2,96,768]{3,2,1,0:T(8,128)(2,1)S(1)}, u32[]{:S(2)}, u32[]{:S(2)}) %all-to-all-start.3) | async-done | bytes 1179680 | tf_op jit(solution)/shard_map/all_to_all | solution.py:195
  156.3 1.8 slice_select_fusion
  160.2 3.7 %collective-permute-start.19 = (bf16[512,768]{1,0:T(8,128)(2,1)S(1)}, bf16[512,768]{1,0:T(8,128)(2,1)S(1)}, u32[]{:S(2)}, u32[]{:S(2)}) collective-permute-start(bf16[512,768]{1,0:T(8,128)(2,1)S(1)} %get-tuple-element.25), channel_id=1, source_target_pairs={{0,16},{8,120},{16,32},{24,8},{32,48},{40,24},{48,64},{56,40},{64,... | collective-permute-start | bytes 2359304 | tf_op jit(solution)/shard_map/ppermute | solution.py:234
  163.9 3.5 %collective-permute-start.21 = (bf16[512,768]{1,0:T(8,128)(2,1)S(1)}, bf16[512,768]{1,0:T(8,128)(2,1)S(1)}, u32[]{:S(2)}, u32[]{:S(2)}) collective-permute-start(bf16[512,768]{1,0:T(8,128)(2,1)S(1)} %get-tuple-element.23), channel_id=1, source_target_pairs={{0,8},{8,0},{1,9},{9,1},{2,10},{10,2},{3,11},{11,3},{4,12},{12,4},... | collective-permute-start | bytes 2359304 | tf_op jit(solution)/shard_map/ppermute | solution.py:231
  167.4 9.1 %shard_map.38.total = f32[2,1024,768]{2,1,0:T(8,128)S(1)} custom-call(s32[3]{0:T(128)S(1)} %pad_add_fusion.where, bf16[4,2,96,768]{3,2,1,0:T(8,128)(2,1)S(1)} %copy-done.6, bf16[4,2,96,768]{3,2,1,0:T(8,128)(2,1)} %collective-permute-done.7.other, bf16[1024,768]{1,0:T(8,128)(2,1)} %collective-permute-done.8.ahead0, ...), custom_call_target="tpu_custom_call" | custom-call | flops 4831838208 | bytes 4831838 | tf_op jit(solution)/shard_map/pallas_call | solution.py:25
  176.5 2.3 %collective-permute-done.18.refs_2_ = bf16[512,768]{1,0:T(8,128)(2,1)S(1)} collective-permute-done((bf16[512,768]{1,0:T(8,128)(2,1)S(1)}, bf16[512,768]{1,0:T(8,128)(2,1)S(1)}, u32[]{:S(2)}, u32[]{:S(2)}) %collective-permute-start.18) | collective-permute-done | bytes 786464 | tf_op jit(solution)/shard_map/ppermute | solution.py:234
  178.8 14.8 %collective-permute-done.19.refs_3_ = bf16[512,768]{1,0:T(8,128)(2,1)S(1)} collective-permute-done((bf16[512,768]{1,0:T(8,128)(2,1)S(1)}, bf16[512,768]{1,0:T(8,128)(2,1)S(1)}, u32[]{:S(2)}, u32[]{:S(2)}) %collective-permute-start.19) | collective-permute-done | bytes 786464 | tf_op jit(solution)/shard_map/ppermute | solution.py:234
  193.7 4.7 %collective-permute-done.21.refs_5_ = bf16[512,768]{1,0:T(8,128)(2,1)S(1)} collective-permute-done((bf16[512,768]{1,0:T(8,128)(2,1)S(1)}, bf16[512,768]{1,0:T(8,128)(2,1)S(1)}, u32[]{:S(2)}, u32[]{:S(2)}) %collective-permute-start.21) | collective-permute-done | bytes 786464 | tf_op jit(solution)/shard_map/ppermute | solution.py:231
  198.4 8.8 %shard_map.40 = bf16[2,1024,768]{2,1,0:T(8,128)(2,1)} custom-call(s32[3]{0:T(128)S(1)} %pad_add_fusion.where, f32[2,1024,768]{2,1,0:T(8,128)S(1)} %shard_map.38.total, bf16[4,2,96,768]{3,2,1,0:T(8,128)(2,1)S(1)} %all-to-all-done.3.mine, bf16[4,2,96,768]{3,2,1,0:T(8,128)(2,1)S(1)} %collective-permute-done.16.other, ...), custom_call_target="tpu_custom_call" | custom-call | flops 4831838208 | bytes 4831838 | tf_op jit(solution)/shard_map/pallas_call | solution.py:25
  (71 shorter events, 21.6 us)
Async XLA Ops:
  0.0 2.9 %copy-start.7 = (bf16[2048,1,768]{2,0,1:T(8,128)(2,1)S(1)}, bf16[2048,1,768]{2,0,1:T(8,128)(2,1)}, u32[]{:S(2)}) copy-start(bf16[2048,1,768]{2,0,1:T(8,128)(2,1)} %param.3) | copy-start | bytes 9437188
  4.1 39.8 %collective-permute-start = (bf16[1024,768]{1,0:T(8,128)(2,1)}, bf16[1024,768]{1,0:T(8,128)(2,1)S(1)}, u32[]{:S(2)}, u32[]{:S(2)}) collective-permute-start(bf16[1024,768]{1,0:T(8,128)(2,1)} %dynamic_slice.19.own_low), channel_id=1, source_target_pairs={{0,112},{16,0},{32,16},{48,32},{64,48},{80,64},{96,80},{112,96},{1... | collective-permute-start | bytes 4718600 | tf_op jit(solution)/shard_map/ppermute | solution.py:228
  10.0 37.4 %collective-permute-start.1 = (bf16[1024,768]{1,0:T(8,128)(2,1)}, bf16[1024,768]{1,0:T(8,128)(2,1)}, u32[]{:S(2)}, u32[]{:S(2)}) collective-permute-start(bf16[1024,768]{1,0:T(8,128)(2,1)} %slice_bitcast_fusion.own_high), channel_id=1, source_target_pairs={{0,16},{16,32},{32,48},{48,64},{64,80},{80,96},{96,112},{112,0},{1... | collective-permute-start | bytes 4718600 | tf_op jit(solution)/shard_map/ppermute | solution.py:225
  12.7 46.4 %collective-permute-start.10 = (bf16[1024,768]{1,0:T(8,128)(2,1)}, bf16[1024,768]{1,0:T(8,128)(2,1)S(1)}, u32[]{:S(2)}, u32[]{:S(2)}) collective-permute-start(bf16[1024,768]{1,0:T(8,128)(2,1)} %constant_dynamic-slice_fusion.1), channel_id=1, source_target_pairs={{0,8},{8,0},{1,9},{9,1},{2,10},{10,2},{3,11},{11,3},{4,12},{12,4},... | collective-permute-start | bytes 4718600 | tf_op jit(solution)/shard_map/ppermute | solution.py:231
  43.9 15.1 %copy-start.3 = (bf16[1024,768]{1,0:T(8,128)(2,1)}, bf16[1024,768]{1,0:T(8,128)(2,1)S(1)}, u32[]{:S(2)}) copy-start(bf16[1024,768]{1,0:T(8,128)(2,1)S(1)} %collective-permute-done.behind.behind0) | copy-start | bytes 4718596
  56.4 12.3 %collective-permute-start.2 = (f32[4,2,96,768]{3,2,1,0:T(8,128)}, f32[4,2,96,768]{3,2,1,0:T(8,128)}, u32[]{:S(2)}, u32[]{:S(2)}) collective-permute-start(f32[4,2,96,768]{3,2,1,0:T(8,128)} %get-tuple-element.15), channel_id=1, source_target_pairs={{0,1},{1,0},{2,3},{3,2},{4,5},{5,4},{6,7},{7,6},{8,9},{9,8},{10,11... | collective-permute-start | bytes 7077896 | tf_op jit(solution)/shard_map/ppermute | solution.py:191
  59.1 9.6 %copy-start.2 = (f32[4,2,96,768]{3,2,1,0:T(8,128)S(1)}, f32[4,2,96,768]{3,2,1,0:T(8,128)}, u32[]{:S(2)}) copy-start(f32[4,2,96,768]{3,2,1,0:T(8,128)} %copy-done.1) | copy-start | bytes 7077892
  68.2 15.4 %collective-permute-start.11 = (f32[4,2,96,768]{3,2,1,0:T(8,128)}, f32[4,2,96,768]{3,2,1,0:T(8,128)}, u32[]{:S(2)}, u32[]{:S(2)}) collective-permute-start(f32[4,2,96,768]{3,2,1,0:T(8,128)} %get-tuple-element.19), channel_id=1, source_target_pairs={{0,1},{1,0},{2,3},{3,2},{4,5},{5,4},{6,7},{7,6},{8,9},{9,8},{10,11... | collective-permute-start | bytes 7077896 | tf_op jit(solution)/shard_map/ppermute | solution.py:191
  71.7 21.0 %all-to-all-start = ((bf16[4,2,96,768]{3,2,1,0:T(8,128)(2,1)}), bf16[4,2,96,768]{3,2,1,0:T(8,128)(2,1)S(1)}, u32[]{:S(2)}, u32[]{:S(2)}) async-start(bf16[4,2,96,768]{3,2,1,0:T(8,128)(2,1)} %add_convert_fusion.1), calls=%async_computation | async-start | bytes 2359296 | tf_op jit(solution)/shard_map/all_to_all | solution.py:195
  76.0 6.9 %collective-permute-start.13 = (bf16[1]{0:T(256)(128)(2,1)}, bf16[1]{0:T(256)(128)(2,1)}, u32[]{:S(2)}, u32[]{:S(2)}) collective-permute-start(bf16[1]{0:T(256)(128)(2,1)} %param.4), channel_id=1, source_target_pairs={{0,8},{8,0},{1,9},{9,1},{2,10},{10,2},{3,11},{11,3},{4,12},{12,4},... | collective-permute-start | bytes 14 | tf_op jit(solution)/shard_map/ppermute | solution.py:237
  77.2 19.8 %collective-permute-start.4 = (bf16[1]{0:T(256)(128)(2,1)}, bf16[1]{0:T(256)(128)(2,1)}, u32[]{:S(2)}, u32[]{:S(2)}) collective-permute-start(bf16[1]{0:T(256)(128)(2,1)} %param.4), channel_id=1, source_target_pairs={{0,16},{16,32},{32,48},{48,64},{64,80},{80,96},{96,112},{112,0},{1... | collective-permute-start | bytes 14 | tf_op jit(solution)/shard_map/ppermute | solution.py:237
  77.2 21.7 %collective-permute-start.15 = (bf16[1]{0:T(256)(128)(2,1)}, bf16[1]{0:T(256)(128)(2,1)}, u32[]{:S(2)}, u32[]{:S(2)}) collective-permute-start(bf16[1]{0:T(256)(128)(2,1)} %param.4), channel_id=1, source_target_pairs={{0,120},{8,16},{16,8},{24,32},{32,24},{40,48},{48,40},{56,64},{64,... | collective-permute-start | bytes 14 | tf_op jit(solution)/shard_map/ppermute | solution.py:237
  78.0 19.6 %collective-permute-start.6 = (bf16[1]{0:T(256)(128)(2,1)}, bf16[1]{0:T(256)(128)(2,1)}, u32[]{:S(2)}, u32[]{:S(2)}) collective-permute-start(bf16[1]{0:T(256)(128)(2,1)} %param.4), channel_id=1, source_target_pairs={{0,112},{16,0},{32,16},{48,32},{64,48},{80,64},{96,80},{112,96},{1... | collective-permute-start | bytes 14 | tf_op jit(solution)/shard_map/ppermute | solution.py:237
  87.2 9.7 %copy-start.10 = (f32[768]{0:T(1024)S(1)}, f32[768]{0:T(1024)}, u32[]{:S(2)}) copy-start(f32[768]{0:T(1024)} %param.5) | copy-start | bytes 9220
  92.6 20.2 %all-to-all-start.2 = ((bf16[4,2,96,768]{3,2,1,0:T(8,128)(2,1)}), bf16[4,2,96,768]{3,2,1,0:T(8,128)(2,1)}, u32[]{:S(2)}, u32[]{:S(2)}) async-start(bf16[4,2,96,768]{3,2,1,0:T(8,128)(2,1)} %add_convert_fusion), calls=%async_computation.2 | async-start | bytes 2359296 | tf_op jit(solution)/shard_map/all_to_all | solution.py:195
  100.4 15.9 %collective-permute-start.3 = (bf16[96,768]{1,0:T(8,128)(2,1)S(1)}, bf16[96,768]{1,0:T(8,128)(2,1)S(1)}, u32[]{:S(2)}, u32[]{:S(2)}) collective-permute-start(bf16[96,768]{1,0:T(8,128)(2,1)S(1)} %get-tuple-element.29), channel_id=1, source_target_pairs={{0,16},{16,32},{32,48},{48,64},{64,80},{80,96},{96,112},{112,0},{1... | collective-permute-start | bytes 442376 | tf_op jit(solution)/shard_map/ppermute | solution.py:225
  100.5 15.8 %collective-permute-start.5 = (bf16[96,768]{1,0:T(8,128)(2,1)S(1)}, bf16[96,768]{1,0:T(8,128)(2,1)S(1)}, u32[]{:S(2)}, u32[]{:S(2)}) collective-permute-start(bf16[96,768]{1,0:T(8,128)(2,1)S(1)} %get-tuple-element.30), channel_id=1, source_target_pairs={{0,112},{16,0},{32,16},{48,32},{64,48},{80,64},{96,80},{112,96},{1... | collective-permute-start | bytes 442376 | tf_op jit(solution)/shard_map/ppermute | solution.py:228
  115.1 12.9 %collective-permute-start.12 = (bf16[2,96,768]{2,1,0:T(8,128)(2,1)}, bf16[2,96,768]{2,1,0:T(8,128)(2,1)}, u32[]{:S(2)}, u32[]{:S(2)}) collective-permute-start(bf16[2,96,768]{2,1,0:T(8,128)(2,1)} %convert_element_type.71), channel_id=1, source_target_pairs={{0,8},{8,0},{1,9},{9,1},{2,10},{10,2},{3,11},{11,3},{4,12},{12,4},... | collective-permute-start | bytes 884744 | tf_op jit(solution)/shard_map/ppermute | solution.py:231
  117.7 12.4 %copy-start.9 = (f32[2,96,768]{2,1,0:T(8,128)S(1)}, f32[2,96,768]{2,1,0:T(8,128)}, u32[]{:S(2)}) copy-start(f32[2,96,768]{2,1,0:T(8,128)} %copy-done.8) | copy-start | bytes 1769476
  117.7 18.3 %all-to-all-start.1 = ((bf16[4,2,96,768]{3,2,1,0:T(8,128)(2,1)}), bf16[4,2,96,768]{3,2,1,0:T(8,128)(2,1)S(1)}, u32[]{:S(2)}, u32[]{:S(2)}) async-start(bf16[4,2,96,768]{3,2,1,0:T(8,128)(2,1)} %broadcast_in_dim.4), calls=%async_computation.1 | async-start | bytes 2359296 | tf_op jit(solution)/shard_map/all_to_all | solution.py:195
  122.3 6.8 %collective-permute-start.14 = (bf16[96,768]{1,0:T(8,128)(2,1)S(1)}, bf16[96,768]{1,0:T(8,128)(2,1)S(1)}, u32[]{:S(2)}, u32[]{:S(2)}) collective-permute-start(bf16[96,768]{1,0:T(8,128)(2,1)S(1)} %slice_bitcast_fusion.3), channel_id=1, source_target_pairs={{0,16},{8,120},{16,32},{24,8},{32,48},{40,24},{48,64},{56,40},{64,... | collective-permute-start | bytes 442376 | tf_op jit(solution)/shard_map/ppermute | solution.py:234
  123.1 35.3 %collective-permute-start.8 = (bf16[1024,768]{1,0:T(8,128)(2,1)}, bf16[1024,768]{1,0:T(8,128)(2,1)}, u32[]{:S(2)}, u32[]{:S(2)}) collective-permute-start(bf16[1024,768]{1,0:T(8,128)(2,1)} %dynamic_slice.19.own_low), channel_id=1, source_target_pairs={{0,16},{16,32},{32,48},{48,64},{64,80},{80,96},{96,112},{112,0},{1... | collective-permute-start | bytes 4718600 | tf_op jit(solution)/shard_map/ppermute | solution.py:225
  124.4 35.8 %collective-permute-start.9 = (bf16[1024,768]{1,0:T(8,128)(2,1)}, bf16[1024,768]{1,0:T(8,128)(2,1)}, u32[]{:S(2)}, u32[]{:S(2)}) collective-permute-start(bf16[1024,768]{1,0:T(8,128)(2,1)} %slice_bitcast_fusion.own_high), channel_id=1, source_target_pairs={{0,112},{16,0},{32,16},{48,32},{64,48},{80,64},{96,80},{112,96},{1... | collective-permute-start | bytes 4718600 | tf_op jit(solution)/shard_map/ppermute | solution.py:228
  126.4 37.5 %collective-permute-start.17 = (bf16[1024,768]{1,0:T(8,128)(2,1)}, bf16[1024,768]{1,0:T(8,128)(2,1)}, u32[]{:S(2)}, u32[]{:S(2)}) collective-permute-start(bf16[1024,768]{1,0:T(8,128)(2,1)} %constant_dynamic-slice_fusion.own), channel_id=1, source_target_pairs={{0,8},{8,0},{1,9},{9,1},{2,10},{10,2},{3,11},{11,3},{4,12},{12,4},... | collective-permute-start | bytes 4718600 | tf_op jit(solution)/shard_map/ppermute | solution.py:231
  137.4 17.4 %all-to-all-start.3 = ((bf16[4,2,96,768]{3,2,1,0:T(8,128)(2,1)}), bf16[4,2,96,768]{3,2,1,0:T(8,128)(2,1)S(1)}, u32[]{:S(2)}, u32[]{:S(2)}) async-start(bf16[4,2,96,768]{3,2,1,0:T(8,128)(2,1)} %broadcast_in_dim.5), calls=%async_computation.3 | async-start | bytes 2359296 | tf_op jit(solution)/shard_map/all_to_all | solution.py:195
  141.0 22.9 %collective-permute-start.7 = (bf16[4,2,96,768]{3,2,1,0:T(8,128)(2,1)}, bf16[4,2,96,768]{3,2,1,0:T(8,128)(2,1)}, u32[]{:S(2)}, u32[]{:S(2)}) collective-permute-start(bf16[4,2,96,768]{3,2,1,0:T(8,128)(2,1)} %copy-done.5), channel_id=1, source_target_pairs={{0,1},{1,0},{2,3},{3,2},{4,5},{5,4},{6,7},{7,6},{8,9},{9,8},{10,11... | collective-permute-start | bytes 3538952 | tf_op jit(solution)/shard_map/ppermute | solution.py:191
  154.9 43.5 %collective-permute-start.16 = (bf16[4,2,96,768]{3,2,1,0:T(8,128)(2,1)S(1)}, bf16[4,2,96,768]{3,2,1,0:T(8,128)(2,1)S(1)}, u32[]{:S(2)}, u32[]{:S(2)}) collective-permute-start(bf16[4,2,96,768]{3,2,1,0:T(8,128)(2,1)S(1)} %all-to-all-done.3.mine), channel_id=1, source_target_pairs={{0,1},{1,0},{2,3},{3,2},{4,5},{5,4},{6,7},{7,6},{8,9},{9,8},{10,11... | collective-permute-start | bytes 3538952 | tf_op jit(solution)/shard_map/ppermute | solution.py:191
  156.3 11.2 %copy-start.6 = (bf16[4,2,96,768]{3,2,1,0:T(8,128)(2,1)S(1)}, bf16[4,2,96,768]{3,2,1,0:T(8,128)(2,1)}, u32[]{:S(2)}) copy-start(bf16[4,2,96,768]{3,2,1,0:T(8,128)(2,1)} %copy-done.5) | copy-start | bytes 3538948
  158.4 20.4 %collective-permute-start.18 = (bf16[512,768]{1,0:T(8,128)(2,1)S(1)}, bf16[512,768]{1,0:T(8,128)(2,1)S(1)}, u32[]{:S(2)}, u32[]{:S(2)}) collective-permute-start(bf16[512,768]{1,0:T(8,128)(2,1)S(1)} %get-tuple-element.26), channel_id=1, source_target_pairs={{0,16},{8,120},{16,32},{24,8},{32,48},{40,24},{48,64},{56,40},{64,... | collective-permute-start | bytes 2359304 | tf_op jit(solution)/shard_map/ppermute | solution.py:234
  160.2 33.5 %collective-permute-start.19 = (bf16[512,768]{1,0:T(8,128)(2,1)S(1)}, bf16[512,768]{1,0:T(8,128)(2,1)S(1)}, u32[]{:S(2)}, u32[]{:S(2)}) collective-permute-start(bf16[512,768]{1,0:T(8,128)(2,1)S(1)} %get-tuple-element.25), channel_id=1, source_target_pairs={{0,16},{8,120},{16,32},{24,8},{32,48},{40,24},{48,64},{56,40},{64,... | collective-permute-start | bytes 2359304 | tf_op jit(solution)/shard_map/ppermute | solution.py:234
  163.9 29.8 %collective-permute-start.20 = (bf16[512,768]{1,0:T(8,128)(2,1)S(1)}, bf16[512,768]{1,0:T(8,128)(2,1)S(1)}, u32[]{:S(2)}, u32[]{:S(2)}) collective-permute-start(bf16[512,768]{1,0:T(8,128)(2,1)S(1)} %get-tuple-element.24), channel_id=1, source_target_pairs={{0,8},{8,0},{1,9},{9,1},{2,10},{10,2},{3,11},{11,3},{4,12},{12,4},... | collective-permute-start | bytes 2359304 | tf_op jit(solution)/shard_map/ppermute | solution.py:231
  163.9 34.5 %collective-permute-start.21 = (bf16[512,768]{1,0:T(8,128)(2,1)S(1)}, bf16[512,768]{1,0:T(8,128)(2,1)S(1)}, u32[]{:S(2)}, u32[]{:S(2)}) collective-permute-start(bf16[512,768]{1,0:T(8,128)(2,1)S(1)} %get-tuple-element.23), channel_id=1, source_target_pairs={{0,8},{8,0},{1,9},{9,1},{2,10},{10,2},{3,11},{11,3},{4,12},{12,4},... | collective-permute-start | bytes 2359304 | tf_op jit(solution)/shard_map/ppermute | solution.py:231
  (5 other events, 8.0 us)

commit v2 on v1

--- a/solution.py
+++ b/solution.py
@@ -19,20 +19,20 @@
 
 
 def on_chip(kernel, where, operands, results, scratch, flops, off_chip=()):
-    vmem, anywhere = (pl.BlockSpec(memory_space=m) for m in (pltpu.VMEM, pl.ANY))
+    vmem, hbm = (pl.BlockSpec(memory_space=m) for m in (pltpu.VMEM, pltpu.HBM))
     held = [pltpu.with_memory_space_constraint(v, pltpu.VMEM) for v in operands]
-    chip = off_chip == ()
+    far_away = [pltpu.with_memory_space_constraint(v, pltpu.HBM) for v in off_chip]
     return pl.pallas_call(
         kernel,
         in_specs=[pl.BlockSpec(memory_space=pltpu.SMEM)]
-        + [anywhere] * len(off_chip or ())
+        + [hbm] * len(far_away)
         + [vmem] * len(held),
-        out_specs=[vmem if chip else anywhere] * len(results),
-        out_shape=[pltpu.VMEM(*r) if chip else jax.ShapeDtypeStruct(*r) for r in results],
+        out_specs=[hbm] * len(results),
+        out_shape=[pltpu.HBM(*r) for r in results],
         scratch_shapes=scratch,
         compiler_params=pltpu.CompilerParams(vmem_limit_bytes=20 << 20),
         cost_estimate=pl.CostEstimate(flops=flops, bytes_accessed=flops // 1000, transcendentals=0),
-    )(where, *(off_chip or ()), *held)
+    )(where, *far_away, *held)
 
 
 def ring(axis, distance):
@@ -40,25 +40,42 @@
     return [(i, (i + distance) % size) for i in range(size)]
 
 
+def moved(value, axis, distance):
+    return lax.ppermute(value, axis, ring(axis, distance))
+
+
 def after(value, *events):
     return lax.optimization_barrier((value, *events))[0]
 
 
-def add_products(core, lefts, rights, send, keep):
-    part, n = send.shape[2:]
-    half, strip = part * X, 256
+STRIP = 256
+
+
+def add_products(core, first, lefts, rights, outs, ready, sent):
+    part, n = ready.shape[3:]
+    half = part * X
+
+    def sending(j, number):
+        columns = pl.ds(pl.multiple_of(j * STRIP, STRIP), STRIP)
+        source = ready.at[number, :, :, :, columns]
+        return pltpu.make_async_copy(source, outs[number].at[:, :, :, columns], sent.at[j, number])
 
     def step(j, carry):
-        columns = pl.ds(pl.multiple_of(j * strip, strip), strip)
-        for side, out in ((1 - core, send), (core, keep)):
+        columns = pl.ds(pl.multiple_of(j * STRIP, STRIP), STRIP)
+        for number, side in enumerate((1 - core, core)):
             rows = pl.ds(pl.multiple_of(side * half, 128), half)
             for place in range(2):
                 product = mm(lefts[place][rows, :], rights[place][:, columns], NN)
                 for k in range(X):
-                    out[k, place, :, columns] = product[k * part : (k + 1) * part]
+                    chunk = lax.rem(k - first + X, X)
+                    ready[number, chunk, place, :, columns] = product[k * part : (k + 1) * part]
+            sending(j, number).start()
         return carry
 
-    lax.fori_loop(0, n // strip, step, 0)
+    lax.fori_loop(0, n // STRIP, step, 0)
+    for j in range(n // STRIP):
+        for number in range(2):
+            sending(j, number).wait()
 
 
 def turn(block, out):
@@ -72,31 +89,36 @@
     lax.fori_loop(0, block.shape[1] // strip, step, 0)
 
 
-def far_pairs_kernel(where, own_high, behind, ahead, own_low, send, keep, *lefts):
+def far_pairs_kernel(where, own_high, behind, ahead, own_low, *refs):
+    outs, lefts, (ready, sent) = refs[:2], refs[2:4], refs[4:]
     turn(own_high, lefts[0])
     turn(behind, lefts[1])
-    add_products(where[1], lefts, (ahead, own_low), send, keep)
-
-
-def near_pairs_kernel(where, behind, partner, ahead, own, send, keep, *lefts):
+    add_products(where[1], 0, lefts, (ahead, own_low), outs, ready, sent)
+
+
+def near_pairs_kernel(where, behind, partner, ahead, own, *refs):
+    outs, lefts, (ready, sent) = refs[:2], refs[2:4], refs[4:]
+    core, x = where[1], where[2]
+
     @pl.when(where[0] == 0)
     def _():
         turn(partner, lefts[0])
         turn(behind, lefts[1])
-        add_products(where[1], lefts, (own, partner), send, keep)
+        add_products(core, x, lefts, (own, partner), outs, ready, sent)
 
     @pl.when(where[0] == 1)
     def _():
         turn(own, lefts[0])
         turn(partner, lefts[1])
-        add_products(where[1], lefts, (partner, ahead), send, keep)
+        add_products(core, x, lefts, (partner, ahead), outs, ready, sent)
 
 
 def pair_call(kernel, where, operands):
     half, n = operands[-1].shape
-    result = ((X, 2, n // (X * C), n), F32)
-    lefts = [pltpu.VMEM((n, half), BF16)] * 2
-    return on_chip(kernel, where, operands, [result, result], lefts, 4 * half * n * n)
+    shape = (X, 2, n // (X * C), n)
+    scratch = [pltpu.VMEM((n, half), BF16)] * 2
+    scratch += [pltpu.VMEM((2, *shape), F32), pltpu.SemaphoreType.DMA((n // STRIP, 2))]
+    return on_chip(kernel, where, operands, [(shape, F32)] * 2, scratch, 4 * half * n * n)
 
 
 def assemble(where, mine, other, full):
@@ -139,7 +161,18 @@
         sending(k).wait()
 
 
-def near_terms_kernel(where, total, mine, other, *refs):
+def assemble_turned(where, pieces, full):
+    part = pieces[0].shape[1]
+    core, x = where[1], where[2]
+    for number, piece in enumerate(pieces):
+        turn_by, other = number % X, number // X
+        row = lax.rem(core + other, C) * (part * X) + lax.rem(x - turn_by + X, X) * part
+        for place in range(2):
+            full[place, pl.ds(pl.multiple_of(row, 32), part), :] = piece[place]
+
+
+def near_terms_kernel(where, total, *refs):
+    pieces, refs = refs[: X * C], refs[X * C :]
     partner_near, partner_far, near_a, near_b, far_a, far_b = refs[:6]
     out, full, loaded, ready, arrived, sent = refs[6:]
     steps = near_a.shape[0] // STEP_ROWS
@@ -154,7 +187,7 @@
 
     for k in range(2 * steps):
         loading(k).start()
-    assemble(where, mine, other, full)
+    assemble_turned(where, pieces, full)
 
     def add(side, partner_dims, diagonal_dims):
         for part, diagonals in enumerate(((near_a, far_a), (near_b, far_b))):
@@ -195,9 +228,28 @@
     return lax.all_to_all(blocks, "x", 0, 0, tiled=True)
 
 
-def summed_rows(send, keep):
-    paired = (keep + core_swap(send)).astype(BF16)
+def summed_rows(paired):
     return jnp.sum(exchanged(paired).astype(F32), axis=0)
+
+
+def turned_in(values):
+    results = []
+    for t, value in enumerate(values):
+        results.append(moved(value, "x", t + 1))
+    return results
+
+
+def turned_sum(send, keep):
+    other = core_swap(send)
+    mine, *rest = (keep[t] + other[t] for t in range(X))
+    for piece in turned_in([r.astype(BF16) for r in rest]):
+        mine = mine + piece.astype(F32)
+    return mine
+
+
+def turned_gather(rows):
+    pieces = [rows, *turned_in([rows] * (X - 1))]
+    return pieces + [core_swap(p) for p in pieces]
 
 
 def amplitude_rows(sums, left_levels, right_levels):
@@ -234,7 +286,7 @@
         return lax.ppermute(value, ("z", "h"), along_route)
 
     def energy(axis, route):
-        return lax.ppermute(occupied_energy, axis, route).astype(F32)
+        return lax.ppermute(occupied_energy, axis, route)
 
     def cut(value, start, length):
         return lax.dynamic_slice_in_dim(value, start, length, 0)
@@ -271,8 +323,12 @@
     near_a = along(partner_near[:quarter])
     near_b = along(partner_near[quarter:])
 
-    far_sums = summed_rows(far_send, far_keep)
-    near_sums = summed_rows(near_send, near_keep)
+    paired = (far_keep + core_swap(far_send)).astype(BF16)
+    far_sums = summed_rows(paired)
+    near_sums = turned_sum(near_send, near_keep)
+    ahead_e, behind_e, partner_e, diagonal_e = (
+        after(e, paired).astype(F32) for e in (ahead_e, behind_e, partner_e, diagonal_e)
+    )
 
     far_wire = far_sums.astype(BF16)
     from_ahead = ahead_of(far_wire[1])
@@ -317,13 +373,12 @@
         [((2, half, n), F32)],
         [full, pltpu.VMEM((2, half, n), F32), copies],
         work,
-        off_chip=None,
     )
     (density,) = on_chip(
         near_terms_kernel,
         where,
         (
-            *gathered(near_rows),
+            *turned_gather(near_rows),
             *(partner_near, partner_far, near_a, near_b, far_a, far_b),
         ),
         [((2, half, n), BF16)],

time: 208 us -> 235 us (1.13)
  the two profiles are of different devices: /device:TPU:24 before, /device:TPU:1 now
where the time goes in v2:
time: 235 us; the launch traced here: 234 us
  waiting for transfers between devices  114 us (49%)
  starting transfers between devices  56.1 us (24%)
  Pallas kernels  34.3 us (15%)
  other arithmetic  15.1 us (6%)
  local copies, waits for them, and re-layouts  10.2 us (4%)
  between operations  5.02 us (2%)
    pallas_call x4, Pallas kernels, on_chip(): pl.pallas_call(kernel, in_specs=[pl.BlockSpec(memory_space=pltpu.SMEM)] +...  34.3 us
    ppermute x3, waiting for transfers between devices, behind_of(): return lax.ppermute(value, 'z', ring('z', -1))  28.9 us
    ppermute x3, waiting for transfers between devices, along(): return lax.ppermute(value, ('z', 'h'), along_route)  28.7 us
    ppermute x6, waiting for transfers between devices, moved(): return lax.ppermute(value, axis, ring(axis, distance))  26.7 us
    ppermute x3, waiting for transfers between devices, ahead_of(): return lax.ppermute(value, 'z', ring('z', 1))  25.8 us
    ppermute x7, starting transfers between devices, core_swap(): return lax.ppermute(value, 'c', [(0, 1), (1, 0)])  12.3 us
    ppermute x3, starting transfers between devices, behind_of(): return lax.ppermute(value, 'z', ring('z', -1))  10.5 us
    ppermute x5, starting transfers between devices, partner_of(): return lax.ppermute(value, 'h', swap_h)  9.33 us
  transfers between devices with their start and end apart: 33, of which 13 were waited for; matrix products, arithmetic and copies ran while one was open for 9% of the time, Pallas kernels for 11%

profile of v2, /device:TPU:1, one launch (start us, length us, event | category | flops | bytes accessed | tf_op | source)
XLA Modules:
  0.0 234.2 jit_solution(5619969005809579096)
XLA Ops:
  0.0 2.8 %slice_bitcast_fusion.own_high = bf16[1024,768]{1,0:T(8,128)(2,1)} fusion(bf16[2048,1,768]{2,0,1:T(8,128)(2,1)} %param.3), kind=kLoop, calls=%fused_computation.2 | loop fusion | bytes 3145728 | tf_op jit(solution)/shard_map/dynamic_slice | solution.py:292
  4.0 6.4 %collective-permute-start = (bf16[1024,768]{1,0:T(8,128)(2,1)}, bf16[1024,768]{1,0:T(8,128)(2,1)S(1)}, u32[]{:S(2)}, u32[]{:S(2)}) collective-permute-start(bf16[1024,768]{1,0:T(8,128)(2,1)} %dynamic_slice.19.own_low), channel_id=1, source_target_pairs={{0,112},{16,0},{32,16},{48,32},{64,48},{80,64},{96,80},{112,96},{1... | collective-permute-start | bytes 4718600 | tf_op jit(solution)/shard_map/ppermute | solution.py:280
  10.4 2.7 %constant_dynamic-slice_fusion.1 = bf16[1024,768]{1,0:T(8,128)(2,1)} fusion(bf16[2048,768]{1,0:T(8,128)(2,1)} %bitcast.73, s32[]{:T(128)S(6)} %select_n.42), kind=kLoop, calls=%fused_computation.51 | loop fusion | bytes 3145732 | tf_op jit(solution)/shard_map/dynamic_slice | solution.py:292
  13.1 2.9 %collective-permute-start.10 = (bf16[1024,768]{1,0:T(8,128)(2,1)}, bf16[1024,768]{1,0:T(8,128)(2,1)S(1)}, u32[]{:S(2)}, u32[]{:S(2)}) collective-permute-start(bf16[1024,768]{1,0:T(8,128)(2,1)} %constant_dynamic-slice_fusion.1), channel_id=1, source_target_pairs={{0,8},{8,0},{1,9},{9,1},{2,10},{10,2},{3,11},{11,3},{4,12},{12,4},... | collective-permute-start | bytes 4718600 | tf_op jit(solution)/shard_map/ppermute | solution.py:283
  16.1 27.7 %collective-permute-done.behind.behind0 = bf16[1024,768]{1,0:T(8,128)(2,1)S(1)} collective-permute-done((bf16[1024,768]{1,0:T(8,128)(2,1)}, bf16[1024,768]{1,0:T(8,128)(2,1)S(1)}, u32[]{:S(2)}, u32[]{:S(2)}) %collective-permute-start) | collective-permute-done | bytes 1572896 | tf_op jit(solution)/shard_map/ppermute | solution.py:280
  43.8 3.1 %collective-permute-done.1.ahead.ahead1 = bf16[1024,768]{1,0:T(8,128)(2,1)} collective-permute-done((bf16[1024,768]{1,0:T(8,128)(2,1)}, bf16[1024,768]{1,0:T(8,128)(2,1)}, u32[]{:S(2)}, u32[]{:S(2)}) %collective-permute-start.1) | collective-permute-done | bytes 1572896 | tf_op jit(solution)/shard_map/ppermute | solution.py:277
  47.0 7.5 %shard_map.37 = (f32[4,2,96,768]{3,2,1,0:T(8,128)}, f32[4,2,96,768]{3,2,1,0:T(8,128)}) custom-call(s32[3]{0:T(128)S(1)} %pad_add_fusion.where, bf16[1024,768]{1,0:T(8,128)(2,1)} %slice_bitcast_fusion.own_high, bf16[1024,768]{1,0:T(8,128)(2,1)S(1)} %collective-permute-done.behind.behind0, bf16[1024,768]{1,0:T(8,128)(2,1)} %collective-permute-done.1.ahead.ahead1, ...), custom_call_target="tpu_custom_call" | custom-call | flops 2415919104 | bytes 2415919 | tf_op jit(solution)/shard_map/pallas_call | solution.py:25
  58.0 7.5 %shard_map.39 = (f32[4,2,96,768]{3,2,1,0:T(8,128)}, f32[4,2,96,768]{3,2,1,0:T(8,128)}) custom-call(s32[3]{0:T(128)S(1)} %pad_add_fusion.where, bf16[1024,768]{1,0:T(8,128)(2,1)S(1)} %collective-permute-done.behind.behind0, bf16[1024,768]{1,0:T(8,128)(2,1)S(1)} %collective-permute-done.10.partner.refs_8_, ...), custom_call_target="tpu_custom_call" | custom-call | flops 2415919104 | bytes 2415919 | tf_op jit(solution)/shard_map/pallas_call | solution.py:25
  65.6 3.1 %add_convert_fusion = bf16[4,2,96,768]{3,2,1,0:T(8,128)(2,1)} fusion(f32[4,2,96,768]{3,2,1,0:T(8,128)S(1)} %copy-done.2, f32[4,2,96,768]{3,2,1,0:T(8,128)} %collective-permute-done.2), kind=kLoop, calls=%fused_computation.1 | loop fusion | flops 1179648 | bytes 5898240 | tf_op jit(solution)/shard_map/convert_element_type | solution.py:326
  68.6 4.3 %all-to-all-start = ((bf16[4,2,96,768]{3,2,1,0:T(8,128)(2,1)}), bf16[4,2,96,768]{3,2,1,0:T(8,128)(2,1)}, u32[]{:S(2)}, u32[]{:S(2)}) async-start(bf16[4,2,96,768]{3,2,1,0:T(8,128)(2,1)} %add_convert_fusion), calls=%async_computation | async-start | bytes 2359296 | tf_op jit(solution)/shard_map/all_to_all | solution.py:228
  72.9 3.0 %collective-permute-start.16 = (bf16[1]{0:T(256)(128)(2,1)}, bf16[1]{0:T(256)(128)(2,1)}, u32[]{:S(2)}, u32[]{:S(2)}) collective-permute-start(bf16[1]{0:T(256)(128)(2,1)} %param.4), channel_id=1, source_target_pairs={{0,8},{8,0},{1,9},{9,1},{2,10},{10,2},{3,11},{11,3},{4,12},{12,4},... | collective-permute-start | bytes 14 | tf_op jit(solution)/shard_map/ppermute | solution.py:289
  75.9 2.5 %collective-permute-start.18 = (bf16[1]{0:T(256)(128)(2,1)}, bf16[1]{0:T(256)(128)(2,1)}, u32[]{:S(2)}, u32[]{:S(2)}) collective-permute-start(bf16[1]{0:T(256)(128)(2,1)} %param.4), channel_id=1, source_target_pairs={{0,120},{8,16},{16,8},{24,32},{32,24},{40,48},{48,40},{56,64},{64,... | collective-permute-start | bytes 14 | tf_op jit(solution)/shard_map/ppermute | solution.py:289
  86.2 2.9 %fusion.7 = (bf16[2,96,768]{2,1,0:T(8,128)(2,1)}, bf16[2,96,768]{2,1,0:T(8,128)(2,1)}, bf16[2,96,768]{2,1,0:T(8,128)(2,1)}) fusion(f32[4,2,96,768]{3,2,1,0:T(8,128)} %collective-permute-done.11, f32[4,2,96,768]{3,2,1,0:T(8,128)} %get-tuple-element.24), kind=kLoop, calls=%fused_computation.16 | loop fusion | flops 884736 | bytes 4423680 | tf_op jit(solution)/shard_map/convert_element_type | solution.py:245
  89.1 2.5 %collective-permute-start.14 = (bf16[2,96,768]{2,1,0:T(8,128)(2,1)}, bf16[2,96,768]{2,1,0:T(8,128)(2,1)S(1)}, u32[]{:S(2)}, u32[]{:S(2)}) collective-permute-start(bf16[2,96,768]{2,1,0:T(8,128)(2,1)} %get-tuple-element.34), channel_id=1, source_target_pairs={{0,6},{2,0},{4,2},{6,4},{1,7},{3,1},{5,3},{7,5},{8,14},{10,8},{12,... | collective-permute-start | bytes 884744 | tf_op jit(solution)/shard_map/ppermute | solution.py:44
  93.4 2.7 %collective-permute-start.5 = (bf16[96,768]{1,0:T(8,128)(2,1)S(1)}, bf16[96,768]{1,0:T(8,128)(2,1)S(1)}, u32[]{:S(2)}, u32[]{:S(2)}) collective-permute-start(bf16[96,768]{1,0:T(8,128)(2,1)S(1)} %get-tuple-element.43), channel_id=1, source_target_pairs={{0,112},{16,0},{32,16},{48,32},{64,48},{80,64},{96,80},{112,96},{1... | collective-permute-start | bytes 442376 | tf_op jit(solution)/shard_map/ppermute | solution.py:280
  96.1 22.6 %collective-permute-done.3 = bf16[96,768]{1,0:T(8,128)(2,1)S(1)} collective-permute-done((bf16[96,768]{1,0:T(8,128)(2,1)S(1)}, bf16[96,768]{1,0:T(8,128)(2,1)S(1)}, u32[]{:S(2)}, u32[]{:S(2)}) %collective-permute-start.3) | collective-permute-done | bytes 147488 | tf_op jit(solution)/shard_map/ppermute | solution.py:277
  121.2 4.3 %all-to-all-start.1 = ((bf16[4,2,96,768]{3,2,1,0:T(8,128)(2,1)}), bf16[4,2,96,768]{3,2,1,0:T(8,128)(2,1)}, u32[]{:S(2)}, u32[]{:S(2)}) async-start(bf16[4,2,96,768]{3,2,1,0:T(8,128)(2,1)} %broadcast_in_dim.2), calls=%async_computation.1 | async-start | bytes 2359296 | tf_op jit(solution)/shard_map/all_to_all | solution.py:228
  127.4 2.8 %collective-permute-start.13 = (bf16[2,96,768]{2,1,0:T(8,128)(2,1)}, bf16[2,96,768]{2,1,0:T(8,128)(2,1)S(1)}, u32[]{:S(2)}, u32[]{:S(2)}) collective-permute-start(bf16[2,96,768]{2,1,0:T(8,128)(2,1)} %get-tuple-element.35), channel_id=1, source_target_pairs={{0,4},{2,6},{4,0},{6,2},{1,5},{3,7},{5,1},{7,3},{8,12},{10,14},{12... | collective-permute-start | bytes 884744 | tf_op jit(solution)/shard_map/ppermute | solution.py:44
  130.6 2.7 %slice_select_fusion = (bf16[512,768]{1,0:T(8,128)(2,1)}, bf16[512,768]{1,0:T(8,128)(2,1)}) fusion(bf16[1024,768]{1,0:T(8,128)(2,1)} %collective-permute-done.1.ahead.ahead1, bf16[1024,768]{1,0:T(8,128)(2,1)S(1)} %collective-permute-done.behind.behind0, pred[]{:T(512)} %eq.3), kind=kLoop, calls=%fused_computation.3 | loop fusion | flops 786432 | bytes 4718593 | tf_op jit(solution)/shard_map/jit(_where)/select_n | solution.py:319
  133.3 12.6 %collective-permute-done.13 = bf16[2,96,768]{2,1,0:T(8,128)(2,1)S(1)} collective-permute-done((bf16[2,96,768]{2,1,0:T(8,128)(2,1)}, bf16[2,96,768]{2,1,0:T(8,128)(2,1)S(1)}, u32[]{:S(2)}, u32[]{:S(2)}) %collective-permute-start.13) | collective-permute-done | bytes 294944 | tf_op jit(solution)/shard_map/ppermute | solution.py:44
  145.9 6.9 %collective-permute-done.12 = bf16[2,96,768]{2,1,0:T(8,128)(2,1)S(1)} collective-permute-done((bf16[2,96,768]{2,1,0:T(8,128)(2,1)}, bf16[2,96,768]{2,1,0:T(8,128)(2,1)S(1)}, u32[]{:S(2)}, u32[]{:S(2)}) %collective-permute-start.12) | collective-permute-done | bytes 294944 | tf_op jit(solution)/shard_map/ppermute | solution.py:44
  152.8 2.3 fusion.27
  157.2 3.3 %collective-permute-start.7 = (bf16[4,2,96,768]{3,2,1,0:T(8,128)(2,1)}, bf16[4,2,96,768]{3,2,1,0:T(8,128)(2,1)S(1)}, u32[]{:S(2)}, u32[]{:S(2)}) collective-permute-start(bf16[4,2,96,768]{3,2,1,0:T(8,128)(2,1)} %all-to-all-done.1.mine), channel_id=1, source_target_pairs={{0,1},{1,0},{2,3},{3,2},{4,5},{5,4},{6,7},{7,6},{8,9},{9,8},{10,11... | collective-permute-start | bytes 3538952 | tf_op jit(solution)/shard_map/ppermute | solution.py:224
  164.0 3.2 %collective-permute-done.15 = bf16[2,96,768]{2,1,0:T(8,128)(2,1)} collective-permute-done((bf16[2,96,768]{2,1,0:T(8,128)(2,1)S(1)}, bf16[2,96,768]{2,1,0:T(8,128)(2,1)}, u32[]{:S(2)}, u32[]{:S(2)}) %collective-permute-start.15) | collective-permute-done | bytes 294944 | tf_op jit(solution)/shard_map/ppermute | solution.py:283
  172.4 9.8 %collective-permute-done.27.refs_10_ = bf16[512,768]{1,0:T(8,128)(2,1)S(1)} collective-permute-done((bf16[512,768]{1,0:T(8,128)(2,1)S(1)}, bf16[512,768]{1,0:T(8,128)(2,1)S(1)}, u32[]{:S(2)}, u32[]{:S(2)}) %collective-permute-start.27) | collective-permute-done | bytes 786464 | tf_op jit(solution)/shard_map/ppermute | solution.py:286
  182.2 16.8 %collective-permute-done.28.refs_11_ = bf16[512,768]{1,0:T(8,128)(2,1)S(1)} collective-permute-done((bf16[512,768]{1,0:T(8,128)(2,1)S(1)}, bf16[512,768]{1,0:T(8,128)(2,1)S(1)}, u32[]{:S(2)}, u32[]{:S(2)}) %collective-permute-start.28) | collective-permute-done | bytes 786464 | tf_op jit(solution)/shard_map/ppermute | solution.py:286
  200.3 2.6 %collective-permute-start.22 = (bf16[2,96,768]{2,1,0:T(8,128)(2,1)S(1)}, bf16[2,96,768]{2,1,0:T(8,128)(2,1)S(1)}, u32[]{:S(2)}, u32[]{:S(2)}) collective-permute-start(bf16[2,96,768]{2,1,0:T(8,128)(2,1)S(1)} %pad_maximum_fusion.1.refs_0_), channel_id=1, source_target_pairs={{0,1},{1,0},{2,3},{3,2},{4,5},{5,4},{6,7},{7,6},{8,9},{9,8},{10,11... | collective-permute-start | bytes 884744 | tf_op jit(solution)/shard_map/ppermute | solution.py:224
  202.9 4.2 %collective-permute-done.20.refs_2_ = bf16[2,96,768]{2,1,0:T(8,128)(2,1)S(1)} collective-permute-done((bf16[2,96,768]{2,1,0:T(8,128)(2,1)S(1)}, bf16[2,96,768]{2,1,0:T(8,128)(2,1)S(1)}, u32[]{:S(2)}, u32[]{:S(2)}) %collective-permute-start.20) | collective-permute-done | bytes 294944 | tf_op jit(solution)/shard_map/ppermute | solution.py:44
  207.1 2.9 %collective-permute-start.23 = (bf16[2,96,768]{2,1,0:T(8,128)(2,1)S(1)}, bf16[2,96,768]{2,1,0:T(8,128)(2,1)S(1)}, u32[]{:S(2)}, u32[]{:S(2)}) collective-permute-start(bf16[2,96,768]{2,1,0:T(8,128)(2,1)S(1)} %collective-permute-done.19.refs_1_), channel_id=1, source_target_pairs={{0,1},{1,0},{2,3},{3,2},{4,5},{5,4},{6,7},{7,6},{8,9},{9,8},{10,11... | collective-permute-start | bytes 884744 | tf_op jit(solution)/shard_map/ppermute | solution.py:224
  210.0 3.0 %collective-permute-done.21.refs_3_ = bf16[2,96,768]{2,1,0:T(8,128)(2,1)S(1)} collective-permute-done((bf16[2,96,768]{2,1,0:T(8,128)(2,1)S(1)}, bf16[2,96,768]{2,1,0:T(8,128)(2,1)S(1)}, u32[]{:S(2)}, u32[]{:S(2)}) %collective-permute-start.21) | collective-permute-done | bytes 294944 | tf_op jit(solution)/shard_map/ppermute | solution.py:44
  214.6 9.7 %shard_map.38.total = f32[2,1024,768]{2,1,0:T(8,128)} custom-call(s32[3]{0:T(128)S(1)} %pad_add_fusion.where, bf16[4,2,96,768]{3,2,1,0:T(8,128)(2,1)} %all-to-all-done.1.mine, bf16[4,2,96,768]{3,2,1,0:T(8,128)(2,1)S(1)} %collective-permute-done.7.other, bf16[1024,768]{1,0:T(8,128)(2,1)} %collective-permute-done.8.ahead0, ...), custom_call_target="tpu_custom_call" | custom-call | flops 4831838208 | bytes 4831838 | tf_op jit(solution)/shard_map/pallas_call | solution.py:25
  224.4 9.6 %shard_map.40 = bf16[2,1024,768]{2,1,0:T(8,128)(2,1)} custom-call(s32[3]{0:T(128)S(1)} %pad_add_fusion.where, f32[2,1024,768]{2,1,0:T(8,128)} %shard_map.38.total, bf16[2,96,768]{2,1,0:T(8,128)(2,1)S(1)} %pad_maximum_fusion.1.refs_0_, bf16[2,96,768]{2,1,0:T(8,128)(2,1)S(1)} %collective-permute-done.19.refs_1_, ...), custom_call_target="tpu_custom_call" | custom-call | flops 4831838208 | bytes 4831838 | tf_op jit(solution)/shard_map/pallas_call | solution.py:25
  (77 shorter events, 28.1 us)
Async XLA Ops:
  4.0 39.8 %collective-permute-start = (bf16[1024,768]{1,0:T(8,128)(2,1)}, bf16[1024,768]{1,0:T(8,128)(2,1)S(1)}, u32[]{:S(2)}, u32[]{:S(2)}) collective-permute-start(bf16[1024,768]{1,0:T(8,128)(2,1)} %dynamic_slice.19.own_low), channel_id=1, source_target_pairs={{0,112},{16,0},{32,16},{48,32},{64,48},{80,64},{96,80},{112,96},{1... | collective-permute-start | bytes 4718600 | tf_op jit(solution)/shard_map/ppermute | solution.py:280
  10.4 36.5 %collective-permute-start.1 = (bf16[1024,768]{1,0:T(8,128)(2,1)}, bf16[1024,768]{1,0:T(8,128)(2,1)}, u32[]{:S(2)}, u32[]{:S(2)}) collective-permute-start(bf16[1024,768]{1,0:T(8,128)(2,1)} %slice_bitcast_fusion.own_high), channel_id=1, source_target_pairs={{0,16},{16,32},{32,48},{48,64},{64,80},{80,96},{96,112},{112,0},{1... | collective-permute-start | bytes 4718600 | tf_op jit(solution)/shard_map/ppermute | solution.py:277
  13.1 44.8 %collective-permute-start.10 = (bf16[1024,768]{1,0:T(8,128)(2,1)}, bf16[1024,768]{1,0:T(8,128)(2,1)S(1)}, u32[]{:S(2)}, u32[]{:S(2)}) collective-permute-start(bf16[1024,768]{1,0:T(8,128)(2,1)} %constant_dynamic-slice_fusion.1), channel_id=1, source_target_pairs={{0,8},{8,0},{1,9},{9,1},{2,10},{10,2},{3,11},{11,3},{4,12},{12,4},... | collective-permute-start | bytes 4718600 | tf_op jit(solution)/shard_map/ppermute | solution.py:283
  54.5 11.0 %collective-permute-start.2 = (f32[4,2,96,768]{3,2,1,0:T(8,128)}, f32[4,2,96,768]{3,2,1,0:T(8,128)}, u32[]{:S(2)}, u32[]{:S(2)}) collective-permute-start(f32[4,2,96,768]{3,2,1,0:T(8,128)} %get-tuple-element.19), channel_id=1, source_target_pairs={{0,1},{1,0},{2,3},{3,2},{4,5},{5,4},{6,7},{7,6},{8,9},{9,8},{10,11... | collective-permute-start | bytes 7077896 | tf_op jit(solution)/shard_map/ppermute | solution.py:224
  65.4 20.7 %collective-permute-start.11 = (f32[4,2,96,768]{3,2,1,0:T(8,128)}, f32[4,2,96,768]{3,2,1,0:T(8,128)}, u32[]{:S(2)}, u32[]{:S(2)}) collective-permute-start(f32[4,2,96,768]{3,2,1,0:T(8,128)} %get-tuple-element.25), channel_id=1, source_target_pairs={{0,1},{1,0},{2,3},{3,2},{4,5},{5,4},{6,7},{7,6},{8,9},{9,8},{10,11... | collective-permute-start | bytes 7077896 | tf_op jit(solution)/shard_map/ppermute | solution.py:224
  68.6 23.1 %all-to-all-start = ((bf16[4,2,96,768]{3,2,1,0:T(8,128)(2,1)}), bf16[4,2,96,768]{3,2,1,0:T(8,128)(2,1)}, u32[]{:S(2)}, u32[]{:S(2)}) async-start(bf16[4,2,96,768]{3,2,1,0:T(8,128)(2,1)} %add_convert_fusion), calls=%async_computation | async-start | bytes 2359296 | tf_op jit(solution)/shard_map/all_to_all | solution.py:228
  72.9 6.4 %collective-permute-start.16 = (bf16[1]{0:T(256)(128)(2,1)}, bf16[1]{0:T(256)(128)(2,1)}, u32[]{:S(2)}, u32[]{:S(2)}) collective-permute-start(bf16[1]{0:T(256)(128)(2,1)} %param.4), channel_id=1, source_target_pairs={{0,8},{8,0},{1,9},{9,1},{2,10},{10,2},{3,11},{11,3},{4,12},{12,4},... | collective-permute-start | bytes 14 | tf_op jit(solution)/shard_map/ppermute | solution.py:289
  75.9 9.0 %collective-permute-start.4 = (bf16[1]{0:T(256)(128)(2,1)}, bf16[1]{0:T(256)(128)(2,1)}, u32[]{:S(2)}, u32[]{:S(2)}) collective-permute-start(bf16[1]{0:T(256)(128)(2,1)} %param.4), channel_id=1, source_target_pairs={{0,16},{16,32},{32,48},{48,64},{64,80},{80,96},{96,112},{112,0},{1... | collective-permute-start | bytes 14 | tf_op jit(solution)/shard_map/ppermute | solution.py:289
  75.9 6.3 %collective-permute-start.18 = (bf16[1]{0:T(256)(128)(2,1)}, bf16[1]{0:T(256)(128)(2,1)}, u32[]{:S(2)}, u32[]{:S(2)}) collective-permute-start(bf16[1]{0:T(256)(128)(2,1)} %param.4), channel_id=1, source_target_pairs={{0,120},{8,16},{16,8},{24,32},{32,24},{40,48},{48,40},{56,64},{64,... | collective-permute-start | bytes 14 | tf_op jit(solution)/shard_map/ppermute | solution.py:289
  78.4 7.2 %collective-permute-start.6 = (bf16[1]{0:T(256)(128)(2,1)}, bf16[1]{0:T(256)(128)(2,1)}, u32[]{:S(2)}, u32[]{:S(2)}) collective-permute-start(bf16[1]{0:T(256)(128)(2,1)} %param.4), channel_id=1, source_target_pairs={{0,112},{16,0},{32,16},{48,32},{64,48},{80,64},{96,80},{112,96},{1... | collective-permute-start | bytes 14 | tf_op jit(solution)/shard_map/ppermute | solution.py:289
  79.3 77.9 %collective-permute-start.8 = (bf16[1024,768]{1,0:T(8,128)(2,1)}, bf16[1024,768]{1,0:T(8,128)(2,1)}, u32[]{:S(2)}, u32[]{:S(2)}) collective-permute-start(bf16[1024,768]{1,0:T(8,128)(2,1)} %dynamic_slice.19.own_low), channel_id=1, source_target_pairs={{0,16},{16,32},{32,48},{48,64},{64,80},{80,96},{96,112},{112,0},{1... | collective-permute-start | bytes 4718600 | tf_op jit(solution)/shard_map/ppermute | solution.py:277
  82.2 78.4 %collective-permute-start.9 = (bf16[1024,768]{1,0:T(8,128)(2,1)}, bf16[1024,768]{1,0:T(8,128)(2,1)}, u32[]{:S(2)}, u32[]{:S(2)}) collective-permute-start(bf16[1024,768]{1,0:T(8,128)(2,1)} %slice_bitcast_fusion.own_high), channel_id=1, source_target_pairs={{0,112},{16,0},{32,16},{48,32},{64,48},{80,64},{96,80},{112,96},{1... | collective-permute-start | bytes 4718600 | tf_op jit(solution)/shard_map/ppermute | solution.py:280
  89.1 41.2 %collective-permute-start.14 = (bf16[2,96,768]{2,1,0:T(8,128)(2,1)}, bf16[2,96,768]{2,1,0:T(8,128)(2,1)S(1)}, u32[]{:S(2)}, u32[]{:S(2)}) collective-permute-start(bf16[2,96,768]{2,1,0:T(8,128)(2,1)} %get-tuple-element.34), channel_id=1, source_target_pairs={{0,6},{2,0},{4,2},{6,4},{1,7},{3,1},{5,3},{7,5},{8,14},{10,8},{12,... | collective-permute-start | bytes 884744 | tf_op jit(solution)/shard_map/ppermute | solution.py:44
  93.3 25.4 %collective-permute-start.3 = (bf16[96,768]{1,0:T(8,128)(2,1)S(1)}, bf16[96,768]{1,0:T(8,128)(2,1)S(1)}, u32[]{:S(2)}, u32[]{:S(2)}) collective-permute-start(bf16[96,768]{1,0:T(8,128)(2,1)S(1)} %get-tuple-element.42), channel_id=1, source_target_pairs={{0,16},{16,32},{32,48},{48,64},{64,80},{80,96},{96,112},{112,0},{1... | collective-permute-start | bytes 442376 | tf_op jit(solution)/shard_map/ppermute | solution.py:277
  93.4 26.5 %collective-permute-start.5 = (bf16[96,768]{1,0:T(8,128)(2,1)S(1)}, bf16[96,768]{1,0:T(8,128)(2,1)S(1)}, u32[]{:S(2)}, u32[]{:S(2)}) collective-permute-start(bf16[96,768]{1,0:T(8,128)(2,1)S(1)} %get-tuple-element.43), channel_id=1, source_target_pairs={{0,112},{16,0},{32,16},{48,32},{64,48},{80,64},{96,80},{112,96},{1... | collective-permute-start | bytes 442376 | tf_op jit(solution)/shard_map/ppermute | solution.py:280
  121.2 36.0 %all-to-all-start.1 = ((bf16[4,2,96,768]{3,2,1,0:T(8,128)(2,1)}), bf16[4,2,96,768]{3,2,1,0:T(8,128)(2,1)}, u32[]{:S(2)}, u32[]{:S(2)}) async-start(bf16[4,2,96,768]{3,2,1,0:T(8,128)(2,1)} %broadcast_in_dim.2), calls=%async_computation.1 | async-start | bytes 2359296 | tf_op jit(solution)/shard_map/all_to_all | solution.py:228
  125.5 45.7 %collective-permute-start.26 = (bf16[1024,768]{1,0:T(8,128)(2,1)}, bf16[1024,768]{1,0:T(8,128)(2,1)}, u32[]{:S(2)}, u32[]{:S(2)}) collective-permute-start(bf16[1024,768]{1,0:T(8,128)(2,1)} %copy-done), channel_id=1, source_target_pairs={{0,8},{8,0},{1,9},{9,1},{2,10},{10,2},{3,11},{11,3},{4,12},{12,4},... | collective-permute-start | bytes 4718600 | tf_op jit(solution)/shard_map/ppermute | solution.py:283
  127.4 18.4 %collective-permute-start.13 = (bf16[2,96,768]{2,1,0:T(8,128)(2,1)}, bf16[2,96,768]{2,1,0:T(8,128)(2,1)S(1)}, u32[]{:S(2)}, u32[]{:S(2)}) collective-permute-start(bf16[2,96,768]{2,1,0:T(8,128)(2,1)} %get-tuple-element.35), channel_id=1, source_target_pairs={{0,4},{2,6},{4,0},{6,2},{1,5},{3,7},{5,1},{7,3},{8,12},{10,14},{12... | collective-permute-start | bytes 884744 | tf_op jit(solution)/shard_map/ppermute | solution.py:44
  130.3 22.5 %collective-permute-start.12 = (bf16[2,96,768]{2,1,0:T(8,128)(2,1)}, bf16[2,96,768]{2,1,0:T(8,128)(2,1)S(1)}, u32[]{:S(2)}, u32[]{:S(2)}) collective-permute-start(bf16[2,96,768]{2,1,0:T(8,128)(2,1)} %get-tuple-element.33), channel_id=1, source_target_pairs={{0,2},{2,4},{4,6},{6,0},{1,3},{3,5},{5,7},{7,1},{8,10},{10,12},{12... | collective-permute-start | bytes 884744 | tf_op jit(solution)/shard_map/ppermute | solution.py:44
  155.1 12.0 %collective-permute-start.15 = (bf16[2,96,768]{2,1,0:T(8,128)(2,1)S(1)}, bf16[2,96,768]{2,1,0:T(8,128)(2,1)}, u32[]{:S(2)}, u32[]{:S(2)}) collective-permute-start(bf16[2,96,768]{2,1,0:T(8,128)(2,1)S(1)} %get-tuple-element.31), channel_id=1, source_target_pairs={{0,8},{8,0},{1,9},{9,1},{2,10},{10,2},{3,11},{11,3},{4,12},{12,4},... | collective-permute-start | bytes 884744 | tf_op jit(solution)/shard_map/ppermute | solution.py:283
  157.2 57.4 %collective-permute-start.7 = (bf16[4,2,96,768]{3,2,1,0:T(8,128)(2,1)}, bf16[4,2,96,768]{3,2,1,0:T(8,128)(2,1)S(1)}, u32[]{:S(2)}, u32[]{:S(2)}) collective-permute-start(bf16[4,2,96,768]{3,2,1,0:T(8,128)(2,1)} %all-to-all-done.1.mine), channel_id=1, source_target_pairs={{0,1},{1,0},{2,3},{3,2},{4,5},{5,4},{6,7},{7,6},{8,9},{9,8},{10,11... | collective-permute-start | bytes 3538952 | tf_op jit(solution)/shard_map/ppermute | solution.py:224
  160.6 21.6 %collective-permute-start.27 = (bf16[512,768]{1,0:T(8,128)(2,1)S(1)}, bf16[512,768]{1,0:T(8,128)(2,1)S(1)}, u32[]{:S(2)}, u32[]{:S(2)}) collective-permute-start(bf16[512,768]{1,0:T(8,128)(2,1)S(1)} %get-tuple-element.39), channel_id=1, source_target_pairs={{0,16},{8,120},{16,32},{24,8},{32,48},{40,24},{48,64},{56,40},{64,... | collective-permute-start | bytes 2359304 | tf_op jit(solution)/shard_map/ppermute | solution.py:286
  163.4 35.7 %collective-permute-start.28 = (bf16[512,768]{1,0:T(8,128)(2,1)S(1)}, bf16[512,768]{1,0:T(8,128)(2,1)S(1)}, u32[]{:S(2)}, u32[]{:S(2)}) collective-permute-start(bf16[512,768]{1,0:T(8,128)(2,1)S(1)} %get-tuple-element.38), channel_id=1, source_target_pairs={{0,16},{8,120},{16,32},{24,8},{32,48},{40,24},{48,64},{56,40},{64,... | collective-permute-start | bytes 2359304 | tf_op jit(solution)/shard_map/ppermute | solution.py:286
  167.1 32.5 %collective-permute-start.29 = (bf16[512,768]{1,0:T(8,128)(2,1)S(1)}, bf16[512,768]{1,0:T(8,128)(2,1)S(1)}, u32[]{:S(2)}, u32[]{:S(2)}) collective-permute-start(bf16[512,768]{1,0:T(8,128)(2,1)S(1)} %copy-done.5), channel_id=1, source_target_pairs={{0,8},{8,0},{1,9},{9,1},{2,10},{10,2},{3,11},{11,3},{4,12},{12,4},... | collective-permute-start | bytes 2359304 | tf_op jit(solution)/shard_map/ppermute | solution.py:283
  171.2 53.1 %collective-permute-start.30 = (bf16[512,768]{1,0:T(8,128)(2,1)S(1)}, bf16[512,768]{1,0:T(8,128)(2,1)S(1)}, u32[]{:S(2)}, u32[]{:S(2)}) collective-permute-start(bf16[512,768]{1,0:T(8,128)(2,1)S(1)} %copy-done.4), channel_id=1, source_target_pairs={{0,8},{8,0},{1,9},{9,1},{2,10},{10,2},{3,11},{11,3},{4,12},{12,4},... | collective-permute-start | bytes 2359304 | tf_op jit(solution)/shard_map/ppermute | solution.py:283
  182.2 18.1 %collective-permute-start.19 = (bf16[2,96,768]{2,1,0:T(8,128)(2,1)S(1)}, bf16[2,96,768]{2,1,0:T(8,128)(2,1)S(1)}, u32[]{:S(2)}, u32[]{:S(2)}) collective-permute-start(bf16[2,96,768]{2,1,0:T(8,128)(2,1)S(1)} %pad_maximum_fusion.1.refs_0_), channel_id=1, source_target_pairs={{0,2},{2,4},{4,6},{6,0},{1,3},{3,5},{5,7},{7,1},{8,10},{10,12},{12... | collective-permute-start | bytes 884744 | tf_op jit(solution)/shard_map/ppermute | solution.py:44
  199.1 8.0 %collective-permute-start.20 = (bf16[2,96,768]{2,1,0:T(8,128)(2,1)S(1)}, bf16[2,96,768]{2,1,0:T(8,128)(2,1)S(1)}, u32[]{:S(2)}, u32[]{:S(2)}) collective-permute-start(bf16[2,96,768]{2,1,0:T(8,128)(2,1)S(1)} %pad_maximum_fusion.1.refs_0_), channel_id=1, source_target_pairs={{0,4},{2,6},{4,0},{6,2},{1,5},{3,7},{5,1},{7,3},{8,12},{10,14},{12... | collective-permute-start | bytes 884744 | tf_op jit(solution)/shard_map/ppermute | solution.py:44
  199.7 13.4 %collective-permute-start.21 = (bf16[2,96,768]{2,1,0:T(8,128)(2,1)S(1)}, bf16[2,96,768]{2,1,0:T(8,128)(2,1)S(1)}, u32[]{:S(2)}, u32[]{:S(2)}) collective-permute-start(bf16[2,96,768]{2,1,0:T(8,128)(2,1)S(1)} %pad_maximum_fusion.1.refs_0_), channel_id=1, source_target_pairs={{0,6},{2,0},{4,2},{6,4},{1,7},{3,1},{5,3},{7,5},{8,14},{10,8},{12,... | collective-permute-start | bytes 884744 | tf_op jit(solution)/shard_map/ppermute | solution.py:44
  200.3 24.0 %collective-permute-start.22 = (bf16[2,96,768]{2,1,0:T(8,128)(2,1)S(1)}, bf16[2,96,768]{2,1,0:T(8,128)(2,1)S(1)}, u32[]{:S(2)}, u32[]{:S(2)}) collective-permute-start(bf16[2,96,768]{2,1,0:T(8,128)(2,1)S(1)} %pad_maximum_fusion.1.refs_0_), channel_id=1, source_target_pairs={{0,1},{1,0},{2,3},{3,2},{4,5},{5,4},{6,7},{7,6},{8,9},{9,8},{10,11... | collective-permute-start | bytes 884744 | tf_op jit(solution)/shard_map/ppermute | solution.py:224
  207.1 17.3 %collective-permute-start.23 = (bf16[2,96,768]{2,1,0:T(8,128)(2,1)S(1)}, bf16[2,96,768]{2,1,0:T(8,128)(2,1)S(1)}, u32[]{:S(2)}, u32[]{:S(2)}) collective-permute-start(bf16[2,96,768]{2,1,0:T(8,128)(2,1)S(1)} %collective-permute-done.19.refs_1_), channel_id=1, source_target_pairs={{0,1},{1,0},{2,3},{3,2},{4,5},{5,4},{6,7},{7,6},{8,9},{9,8},{10,11... | collective-permute-start | bytes 884744 | tf_op jit(solution)/shard_map/ppermute | solution.py:224
  213.1 11.3 %collective-permute-start.24 = (bf16[2,96,768]{2,1,0:T(8,128)(2,1)S(1)}, bf16[2,96,768]{2,1,0:T(8,128)(2,1)S(1)}, u32[]{:S(2)}, u32[]{:S(2)}) collective-permute-start(bf16[2,96,768]{2,1,0:T(8,128)(2,1)S(1)} %collective-permute-done.20.refs_2_), channel_id=1, source_target_pairs={{0,1},{1,0},{2,3},{3,2},{4,5},{5,4},{6,7},{7,6},{8,9},{9,8},{10,11... | collective-permute-start | bytes 884744 | tf_op jit(solution)/shard_map/ppermute | solution.py:224
  214.6 9.8 %collective-permute-start.25 = (bf16[2,96,768]{2,1,0:T(8,128)(2,1)S(1)}, bf16[2,96,768]{2,1,0:T(8,128)(2,1)S(1)}, u32[]{:S(2)}, u32[]{:S(2)}) collective-permute-start(bf16[2,96,768]{2,1,0:T(8,128)(2,1)S(1)} %collective-permute-done.21.refs_3_), channel_id=1, source_target_pairs={{0,1},{1,0},{2,3},{3,2},{4,5},{5,4},{6,7},{7,6},{8,9},{9,8},{10,11... | collective-permute-start | bytes 884744 | tf_op jit(solution)/shard_map/ppermute | solution.py:224
  (9 other events, 69.5 us)

commit v3 on v2

--- a/solution.py
+++ b/solution.py
@@ -113,6 +113,21 @@
         add_products(core, x, lefts, (partner, ahead), outs, ready, sent)
 
 
+def copy_kernel(value, out):
+    for k in range(value.shape[0]):
+        out[k] = value[k]
+
+
+def copied(value):
+    table = pl.BlockSpec(memory_space=pltpu.SMEM)
+    return pl.pallas_call(
+        copy_kernel,
+        in_specs=[table],
+        out_specs=table,
+        out_shape=jax.ShapeDtypeStruct(value.shape, value.dtype),
+    )(value)
+
+
 def pair_call(kernel, where, operands):
     half, n = operands[-1].shape
     shape = (X, 2, n // (X * C), n)
@@ -242,7 +257,9 @@
 def turned_sum(send, keep):
     other = core_swap(send)
     mine, *rest = (keep[t] + other[t] for t in range(X))
-    for piece in turned_in([r.astype(BF16) for r in rest]):
+    rest = [r.astype(BF16) for r in rest]
+    pieces = turned_in(rest)
+    for piece in pieces:
         mine = mine + piece.astype(F32)
     return mine
 
@@ -368,7 +385,7 @@
     work = 8 * half * n * n
     (total,) = on_chip(
         far_terms_kernel,
-        where,
+        copied(where),
         (*gathered(far_rows), ahead0, ahead1, behind0, behind1),
         [((2, half, n), F32)],
         [full, pltpu.VMEM((2, half, n), F32), copies],

time: 235 us -> 237 us (level)
  waiting for transfers between devices: 114 us -> 110 us
  local copies, waits for them, and re-layouts: 10.2 us -> 13.5 us
    unnamed x16 -> x32, local copies, waits for them, and re-layouts: 0.03 us -> 3.37 us
where the time goes in v3:
time: 237 us; the launch traced here: 236 us
  waiting for transfers between devices  110 us (46%)
  starting transfers between devices  56.5 us (24%)
  Pallas kernels  36 us (15%)
  other arithmetic  15 us (6%)
  local copies, waits for them, and re-layouts  13.5 us (6%)
  between operations  4.81 us (2%)
    pallas_call x4, Pallas kernels, on_chip(): pl.pallas_call(kernel, in_specs=[pl.BlockSpec(memory_space=pltpu.SMEM)] +...  34.8 us
    ppermute x3, waiting for transfers between devices, along(): return lax.ppermute(value, ('z', 'h'), along_route)  28.6 us
    ppermute x3, waiting for transfers between devices, behind_of(): return lax.ppermute(value, 'z', ring('z', -1))  28.4 us
    ppermute x3, waiting for transfers between devices, ahead_of(): return lax.ppermute(value, 'z', ring('z', 1))  25.9 us
    ppermute x6, waiting for transfers between devices, moved(): return lax.ppermute(value, axis, ring(axis, distance))  24.5 us
    ppermute x7, starting transfers between devices, core_swap(): return lax.ppermute(value, 'c', [(0, 1), (1, 0)])  12.4 us
    ppermute x3, starting transfers between devices, behind_of(): return lax.ppermute(value, 'z', ring('z', -1))  10.5 us
    ppermute x5, starting transfers between devices, partner_of(): return lax.ppermute(value, 'h', swap_h)  9.68 us
  transfers between devices with their start and end apart: 33, of which 13 were waited for; matrix products, arithmetic and copies ran while one was open for 9% of the time, Pallas kernels for 11%

profile of v3, /device:TPU:1, one launch (start us, length us, event | category | flops | bytes accessed | tf_op | source)
XLA Modules:
  0.0 236.1 jit_solution(9993059644479138348)
XLA Ops:
  0.0 2.8 %slice_bitcast_fusion.own_high = bf16[1024,768]{1,0:T(8,128)(2,1)} fusion(bf16[2048,1,768]{2,0,1:T(8,128)(2,1)} %param.3), kind=kLoop, calls=%fused_computation.2 | loop fusion | bytes 3145728 | tf_op jit(solution)/shard_map/dynamic_slice | solution.py:309
  4.0 6.4 %collective-permute-start = (bf16[1024,768]{1,0:T(8,128)(2,1)}, bf16[1024,768]{1,0:T(8,128)(2,1)S(1)}, u32[]{:S(2)}, u32[]{:S(2)}) collective-permute-start(bf16[1024,768]{1,0:T(8,128)(2,1)} %dynamic_slice.19.own_low), channel_id=1, source_target_pairs={{0,112},{16,0},{32,16},{48,32},{64,48},{80,64},{96,80},{112,96},{1... | collective-permute-start | bytes 4718600 | tf_op jit(solution)/shard_map/ppermute | solution.py:297
  10.4 2.7 %constant_dynamic-slice_fusion.1 = bf16[1024,768]{1,0:T(8,128)(2,1)} fusion(bf16[2048,768]{1,0:T(8,128)(2,1)} %bitcast.73, s32[]{:T(128)S(6)} %select_n.42), kind=kLoop, calls=%fused_computation.51 | loop fusion | bytes 3145732 | tf_op jit(solution)/shard_map/dynamic_slice | solution.py:309
  13.1 2.9 %collective-permute-start.10 = (bf16[1024,768]{1,0:T(8,128)(2,1)}, bf16[1024,768]{1,0:T(8,128)(2,1)S(1)}, u32[]{:S(2)}, u32[]{:S(2)}) collective-permute-start(bf16[1024,768]{1,0:T(8,128)(2,1)} %constant_dynamic-slice_fusion.1), channel_id=1, source_target_pairs={{0,8},{8,0},{1,9},{9,1},{2,10},{10,2},{3,11},{11,3},{4,12},{12,4},... | collective-permute-start | bytes 4718600 | tf_op jit(solution)/shard_map/ppermute | solution.py:300
  16.1 27.7 %collective-permute-done.behind.behind0 = bf16[1024,768]{1,0:T(8,128)(2,1)S(1)} collective-permute-done((bf16[1024,768]{1,0:T(8,128)(2,1)}, bf16[1024,768]{1,0:T(8,128)(2,1)S(1)}, u32[]{:S(2)}, u32[]{:S(2)}) %collective-permute-start) | collective-permute-done | bytes 1572896 | tf_op jit(solution)/shard_map/ppermute | solution.py:297
  43.8 3.1 %collective-permute-done.1.ahead.ahead1 = bf16[1024,768]{1,0:T(8,128)(2,1)} collective-permute-done((bf16[1024,768]{1,0:T(8,128)(2,1)}, bf16[1024,768]{1,0:T(8,128)(2,1)}, u32[]{:S(2)}, u32[]{:S(2)}) %collective-permute-start.1) | collective-permute-done | bytes 1572896 | tf_op jit(solution)/shard_map/ppermute | solution.py:294
  47.0 7.5 %shard_map.38 = (f32[4,2,96,768]{3,2,1,0:T(8,128)}, f32[4,2,96,768]{3,2,1,0:T(8,128)}) custom-call(s32[3]{0:T(128)S(1)} %pad_add_fusion.value.where, bf16[1024,768]{1,0:T(8,128)(2,1)} %slice_bitcast_fusion.own_high, bf16[1024,768]{1,0:T(8,128)(2,1)S(1)} %collective-permute-done.behind.behind0, bf16[1024,768]{1,0:T(8,128)(2,1)} %collective-permute-done.1.ahead.ahead1, ...), custom_call_target="tpu_custom_call" | custom-call | flops 2415919104 | bytes 2415919 | tf_op jit(solution)/shard_map/pallas_call | solution.py:25
  57.9 7.4 %shard_map.40 = (f32[4,2,96,768]{3,2,1,0:T(8,128)}, f32[4,2,96,768]{3,2,1,0:T(8,128)}) custom-call(s32[3]{0:T(128)S(1)} %pad_add_fusion.value.where, bf16[1024,768]{1,0:T(8,128)(2,1)S(1)} %collective-permute-done.behind.behind0, bf16[1024,768]{1,0:T(8,128)(2,1)S(1)} %collective-permute-done.10.partner.refs_8_, ...), custom_call_target="tpu_custom_call" | custom-call | flops 2415919104 | bytes 2415919 | tf_op jit(solution)/shard_map/pallas_call | solution.py:25
  65.5 2.9 %add_convert_fusion = bf16[4,2,96,768]{3,2,1,0:T(8,128)(2,1)} fusion(f32[4,2,96,768]{3,2,1,0:T(8,128)S(1)} %copy-done.11, f32[4,2,96,768]{3,2,1,0:T(8,128)} %collective-permute-done.2), kind=kLoop, calls=%fused_computation.1 | loop fusion | flops 1179648 | bytes 5898240 | tf_op jit(solution)/shard_map/convert_element_type | solution.py:343
  68.4 4.3 %all-to-all-start = ((bf16[4,2,96,768]{3,2,1,0:T(8,128)(2,1)}), bf16[4,2,96,768]{3,2,1,0:T(8,128)(2,1)}, u32[]{:S(2)}, u32[]{:S(2)}) async-start(bf16[4,2,96,768]{3,2,1,0:T(8,128)(2,1)} %add_convert_fusion), calls=%async_computation | async-start | bytes 2359296 | tf_op jit(solution)/shard_map/all_to_all | solution.py:243
  72.7 3.0 %collective-permute-start.16 = (bf16[1]{0:T(256)(128)(2,1)}, bf16[1]{0:T(256)(128)(2,1)}, u32[]{:S(2)}, u32[]{:S(2)}) collective-permute-start(bf16[1]{0:T(256)(128)(2,1)} %param.4), channel_id=1, source_target_pairs={{0,8},{8,0},{1,9},{9,1},{2,10},{10,2},{3,11},{11,3},{4,12},{12,4},... | collective-permute-start | bytes 14 | tf_op jit(solution)/shard_map/ppermute | solution.py:306
  75.7 2.5 %collective-permute-start.18 = (bf16[1]{0:T(256)(128)(2,1)}, bf16[1]{0:T(256)(128)(2,1)}, u32[]{:S(2)}, u32[]{:S(2)}) collective-permute-start(bf16[1]{0:T(256)(128)(2,1)} %param.4), channel_id=1, source_target_pairs={{0,120},{8,16},{16,8},{24,32},{32,24},{40,48},{48,40},{56,64},{64,... | collective-permute-start | bytes 14 | tf_op jit(solution)/shard_map/ppermute | solution.py:306
  85.8 3.0 %fusion.7 = (bf16[2,96,768]{2,1,0:T(8,128)(2,1)}, bf16[2,96,768]{2,1,0:T(8,128)(2,1)}, bf16[2,96,768]{2,1,0:T(8,128)(2,1)}) fusion(f32[4,2,96,768]{3,2,1,0:T(8,128)} %collective-permute-done.11, f32[4,2,96,768]{3,2,1,0:T(8,128)} %get-tuple-element.24), kind=kLoop, calls=%fused_computation.16 | loop fusion | flops 884736 | bytes 4423680 | tf_op jit(solution)/shard_map/convert_element_type | solution.py:260
  88.7 2.5 %collective-permute-start.14 = (bf16[2,96,768]{2,1,0:T(8,128)(2,1)}, bf16[2,96,768]{2,1,0:T(8,128)(2,1)S(1)}, u32[]{:S(2)}, u32[]{:S(2)}) collective-permute-start(bf16[2,96,768]{2,1,0:T(8,128)(2,1)} %get-tuple-element.34), channel_id=1, source_target_pairs={{0,6},{2,0},{4,2},{6,4},{1,7},{3,1},{5,3},{7,5},{8,14},{10,8},{12,... | collective-permute-start | bytes 884744 | tf_op jit(solution)/shard_map/ppermute | solution.py:44
  93.0 2.7 %collective-permute-start.5 = (bf16[96,768]{1,0:T(8,128)(2,1)S(1)}, bf16[96,768]{1,0:T(8,128)(2,1)S(1)}, u32[]{:S(2)}, u32[]{:S(2)}) collective-permute-start(bf16[96,768]{1,0:T(8,128)(2,1)S(1)} %get-tuple-element.43), channel_id=1, source_target_pairs={{0,112},{16,0},{32,16},{48,32},{64,48},{80,64},{96,80},{112,96},{1... | collective-permute-start | bytes 442376 | tf_op jit(solution)/shard_map/ppermute | solution.py:297
  95.7 22.8 %collective-permute-done.3 = bf16[96,768]{1,0:T(8,128)(2,1)S(1)} collective-permute-done((bf16[96,768]{1,0:T(8,128)(2,1)S(1)}, bf16[96,768]{1,0:T(8,128)(2,1)S(1)}, u32[]{:S(2)}, u32[]{:S(2)}) %collective-permute-start.3) | collective-permute-done | bytes 147488 | tf_op jit(solution)/shard_map/ppermute | solution.py:294
  120.5 4.3 %all-to-all-start.1 = ((bf16[4,2,96,768]{3,2,1,0:T(8,128)(2,1)}), bf16[4,2,96,768]{3,2,1,0:T(8,128)(2,1)}, u32[]{:S(2)}, u32[]{:S(2)}) async-start(bf16[4,2,96,768]{3,2,1,0:T(8,128)(2,1)} %broadcast_in_dim.2), calls=%async_computation.1 | async-start | bytes 2359296 | tf_op jit(solution)/shard_map/all_to_all | solution.py:243
  126.9 2.8 %collective-permute-start.13 = (bf16[2,96,768]{2,1,0:T(8,128)(2,1)}, bf16[2,96,768]{2,1,0:T(8,128)(2,1)S(1)}, u32[]{:S(2)}, u32[]{:S(2)}) collective-permute-start(bf16[2,96,768]{2,1,0:T(8,128)(2,1)} %get-tuple-element.35), channel_id=1, source_target_pairs={{0,4},{2,6},{4,0},{6,2},{1,5},{3,7},{5,1},{7,3},{8,12},{10,14},{12... | collective-permute-start | bytes 884744 | tf_op jit(solution)/shard_map/ppermute | solution.py:44
  130.1 2.7 %slice_select_fusion = (bf16[512,768]{1,0:T(8,128)(2,1)}, bf16[512,768]{1,0:T(8,128)(2,1)}) fusion(bf16[1024,768]{1,0:T(8,128)(2,1)} %collective-permute-done.1.ahead.ahead1, bf16[1024,768]{1,0:T(8,128)(2,1)S(1)} %collective-permute-done.behind.behind0, pred[]{:T(512)} %eq.3), kind=kLoop, calls=%fused_computation.3 | loop fusion | flops 786432 | bytes 4718593 | tf_op jit(solution)/shard_map/jit(_where)/select_n | solution.py:336
  132.8 12.0 %collective-permute-done.13 = bf16[2,96,768]{2,1,0:T(8,128)(2,1)S(1)} collective-permute-done((bf16[2,96,768]{2,1,0:T(8,128)(2,1)}, bf16[2,96,768]{2,1,0:T(8,128)(2,1)S(1)}, u32[]{:S(2)}, u32[]{:S(2)}) %collective-permute-start.13) | collective-permute-done | bytes 294944 | tf_op jit(solution)/shard_map/ppermute | solution.py:44
  144.8 7.2 %collective-permute-done.12 = bf16[2,96,768]{2,1,0:T(8,128)(2,1)S(1)} collective-permute-done((bf16[2,96,768]{2,1,0:T(8,128)(2,1)}, bf16[2,96,768]{2,1,0:T(8,128)(2,1)S(1)}, u32[]{:S(2)}, u32[]{:S(2)}) %collective-permute-start.12) | collective-permute-done | bytes 294944 | tf_op jit(solution)/shard_map/ppermute | solution.py:44
  152.0 2.4 %fusion.27 = (bf16[2,96,768]{2,1,0:T(8,128)(2,1)S(1)}, f32[2,96,768]{2,1,0:T(8,128)}) fusion(bf16[2,96,768]{2,1,0:T(8,128)(2,1)} %copy-done.14, bf16[2,96,768]{2,1,0:T(8,128)(2,1)S(1)} %collective-permute-done.13, bf16[2,96,768]{2,1,0:T(8,128)(2,1)S(1)} %collective-permute-done.12, f32[4,2,96,768]{3,2,1,0:T(8,128)} %collective-permute-done.11, ...), kind=kLoop, calls=%fused_computation.56 | loop fusion | flops 1179648 | bytes 2949120 | tf_op jit(solution)/shard_map/convert_element_type | solution.py:353
  156.7 3.4 %collective-permute-start.7 = (bf16[4,2,96,768]{3,2,1,0:T(8,128)(2,1)}, bf16[4,2,96,768]{3,2,1,0:T(8,128)(2,1)}, u32[]{:S(2)}, u32[]{:S(2)}) collective-permute-start(bf16[4,2,96,768]{3,2,1,0:T(8,128)(2,1)} %all-to-all-done.1.mine), channel_id=1, source_target_pairs={{0,1},{1,0},{2,3},{3,2},{4,5},{5,4},{6,7},{7,6},{8,9},{9,8},{10,11... | collective-permute-start | bytes 3538952 | tf_op jit(solution)/shard_map/ppermute | solution.py:239
  163.5 2.6 %collective-permute-done.15 = bf16[2,96,768]{2,1,0:T(8,128)(2,1)} collective-permute-done((bf16[2,96,768]{2,1,0:T(8,128)(2,1)S(1)}, bf16[2,96,768]{2,1,0:T(8,128)(2,1)}, u32[]{:S(2)}, u32[]{:S(2)}) %collective-permute-start.15) | collective-permute-done | bytes 294944 | tf_op jit(solution)/shard_map/ppermute | solution.py:300
  166.1 2.4 %collective-permute-start.29 = (bf16[512,768]{1,0:T(8,128)(2,1)S(1)}, bf16[512,768]{1,0:T(8,128)(2,1)S(1)}, u32[]{:S(2)}, u32[]{:S(2)}) collective-permute-start(bf16[512,768]{1,0:T(8,128)(2,1)S(1)} %copy-done.13), channel_id=1, source_target_pairs={{0,8},{8,0},{1,9},{9,1},{2,10},{10,2},{3,11},{11,3},{4,12},{12,4},... | collective-permute-start | bytes 2359304 | tf_op jit(solution)/shard_map/ppermute | solution.py:300
  171.4 10.4 %collective-permute-done.27.refs_10_ = bf16[512,768]{1,0:T(8,128)(2,1)S(1)} collective-permute-done((bf16[512,768]{1,0:T(8,128)(2,1)S(1)}, bf16[512,768]{1,0:T(8,128)(2,1)S(1)}, u32[]{:S(2)}, u32[]{:S(2)}) %collective-permute-start.27) | collective-permute-done | bytes 786464 | tf_op jit(solution)/shard_map/ppermute | solution.py:303
  182.7 16.1 %collective-permute-done.28.refs_11_ = bf16[512,768]{1,0:T(8,128)(2,1)S(1)} collective-permute-done((bf16[512,768]{1,0:T(8,128)(2,1)S(1)}, bf16[512,768]{1,0:T(8,128)(2,1)S(1)}, u32[]{:S(2)}, u32[]{:S(2)}) %collective-permute-start.28) | collective-permute-done | bytes 786464 | tf_op jit(solution)/shard_map/ppermute | solution.py:303
  203.0 2.6 %collective-permute-start.22 = (bf16[2,96,768]{2,1,0:T(8,128)(2,1)S(1)}, bf16[2,96,768]{2,1,0:T(8,128)(2,1)S(1)}, u32[]{:S(2)}, u32[]{:S(2)}) collective-permute-start(bf16[2,96,768]{2,1,0:T(8,128)(2,1)S(1)} %pad_maximum_fusion.1.refs_0_), channel_id=1, source_target_pairs={{0,1},{1,0},{2,3},{3,2},{4,5},{5,4},{6,7},{7,6},{8,9},{9,8},{10,11... | collective-permute-start | bytes 884744 | tf_op jit(solution)/shard_map/ppermute | solution.py:239
  207.8 2.8 %collective-permute-start.23 = (bf16[2,96,768]{2,1,0:T(8,128)(2,1)}, bf16[2,96,768]{2,1,0:T(8,128)(2,1)S(1)}, u32[]{:S(2)}, u32[]{:S(2)}) collective-permute-start(bf16[2,96,768]{2,1,0:T(8,128)(2,1)} %collective-permute-done.19.refs_1_), channel_id=1, source_target_pairs={{0,1},{1,0},{2,3},{3,2},{4,5},{5,4},{6,7},{7,6},{8,9},{9,8},{10,11... | collective-permute-start | bytes 884744 | tf_op jit(solution)/shard_map/ppermute | solution.py:239
  210.7 2.9 %collective-permute-done.21.refs_3_ = bf16[2,96,768]{2,1,0:T(8,128)(2,1)} collective-permute-done((bf16[2,96,768]{2,1,0:T(8,128)(2,1)S(1)}, bf16[2,96,768]{2,1,0:T(8,128)(2,1)}, u32[]{:S(2)}, u32[]{:S(2)}) %collective-permute-start.21) | collective-permute-done | bytes 294944 | tf_op jit(solution)/shard_map/ppermute | solution.py:44
  215.9 10.0 %shard_map.39.total = f32[2,1024,768]{2,1,0:T(8,128)} custom-call(s32[3]{0:T(128)S(1)} %copy-done.9, bf16[4,2,96,768]{3,2,1,0:T(8,128)(2,1)} %all-to-all-done.1.mine, bf16[4,2,96,768]{3,2,1,0:T(8,128)(2,1)} %collective-permute-done.7.other, bf16[1024,768]{1,0:T(8,128)(2,1)} %collective-permute-done.8.ahead0, ...), custom_call_target="tpu_custom_call" | custom-call | flops 4831838208 | bytes 4831838 | tf_op jit(solution)/shard_map/pallas_call | solution.py:25
  226.0 9.9 %shard_map.41 = bf16[2,1024,768]{2,1,0:T(8,128)(2,1)} custom-call(s32[3]{0:T(128)S(1)} %copy-done.8, f32[2,1024,768]{2,1,0:T(8,128)} %shard_map.39.total, bf16[2,96,768]{2,1,0:T(8,128)(2,1)S(1)} %pad_maximum_fusion.1.refs_0_, bf16[2,96,768]{2,1,0:T(8,128)(2,1)} %collective-permute-done.19.refs_1_, bf16[2,96,768]{2,1,0:T(8,128)(2,1)} %collective-permute-done.20.refs_2_, ...), custom_call_target="tpu_custom_call" | custom-call | flops 4831838208 | bytes 4831838 | tf_op jit(solution)/shard_map/pallas_call | solution.py:25
  (94 shorter events, 32.5 us)
Async XLA Ops:
  4.0 39.8 %collective-permute-start = (bf16[1024,768]{1,0:T(8,128)(2,1)}, bf16[1024,768]{1,0:T(8,128)(2,1)S(1)}, u32[]{:S(2)}, u32[]{:S(2)}) collective-permute-start(bf16[1024,768]{1,0:T(8,128)(2,1)} %dynamic_slice.19.own_low), channel_id=1, source_target_pairs={{0,112},{16,0},{32,16},{48,32},{64,48},{80,64},{96,80},{112,96},{1... | collective-permute-start | bytes 4718600 | tf_op jit(solution)/shard_map/ppermute | solution.py:297
  10.4 36.5 %collective-permute-start.1 = (bf16[1024,768]{1,0:T(8,128)(2,1)}, bf16[1024,768]{1,0:T(8,128)(2,1)}, u32[]{:S(2)}, u32[]{:S(2)}) collective-permute-start(bf16[1024,768]{1,0:T(8,128)(2,1)} %slice_bitcast_fusion.own_high), channel_id=1, source_target_pairs={{0,16},{16,32},{32,48},{48,64},{64,80},{80,96},{96,112},{112,0},{1... | collective-permute-start | bytes 4718600 | tf_op jit(solution)/shard_map/ppermute | solution.py:294
  13.1 44.8 %collective-permute-start.10 = (bf16[1024,768]{1,0:T(8,128)(2,1)}, bf16[1024,768]{1,0:T(8,128)(2,1)S(1)}, u32[]{:S(2)}, u32[]{:S(2)}) collective-permute-start(bf16[1024,768]{1,0:T(8,128)(2,1)} %constant_dynamic-slice_fusion.1), channel_id=1, source_target_pairs={{0,8},{8,0},{1,9},{9,1},{2,10},{10,2},{3,11},{11,3},{4,12},{12,4},... | collective-permute-start | bytes 4718600 | tf_op jit(solution)/shard_map/ppermute | solution.py:300
  54.5 11.0 %collective-permute-start.2 = (f32[4,2,96,768]{3,2,1,0:T(8,128)}, f32[4,2,96,768]{3,2,1,0:T(8,128)}, u32[]{:S(2)}, u32[]{:S(2)}) collective-permute-start(f32[4,2,96,768]{3,2,1,0:T(8,128)} %get-tuple-element.19), channel_id=1, source_target_pairs={{0,1},{1,0},{2,3},{3,2},{4,5},{5,4},{6,7},{7,6},{8,9},{9,8},{10,11... | collective-permute-start | bytes 7077896 | tf_op jit(solution)/shard_map/ppermute | solution.py:239
  65.4 20.4 %collective-permute-start.11 = (f32[4,2,96,768]{3,2,1,0:T(8,128)}, f32[4,2,96,768]{3,2,1,0:T(8,128)}, u32[]{:S(2)}, u32[]{:S(2)}) collective-permute-start(f32[4,2,96,768]{3,2,1,0:T(8,128)} %get-tuple-element.25), channel_id=1, source_target_pairs={{0,1},{1,0},{2,3},{3,2},{4,5},{5,4},{6,7},{7,6},{8,9},{9,8},{10,11... | collective-permute-start | bytes 7077896 | tf_op jit(solution)/shard_map/ppermute | solution.py:239
  68.4 23.0 %all-to-all-start = ((bf16[4,2,96,768]{3,2,1,0:T(8,128)(2,1)}), bf16[4,2,96,768]{3,2,1,0:T(8,128)(2,1)}, u32[]{:S(2)}, u32[]{:S(2)}) async-start(bf16[4,2,96,768]{3,2,1,0:T(8,128)(2,1)} %add_convert_fusion), calls=%async_computation | async-start | bytes 2359296 | tf_op jit(solution)/shard_map/all_to_all | solution.py:243
  72.7 6.4 %collective-permute-start.16 = (bf16[1]{0:T(256)(128)(2,1)}, bf16[1]{0:T(256)(128)(2,1)}, u32[]{:S(2)}, u32[]{:S(2)}) collective-permute-start(bf16[1]{0:T(256)(128)(2,1)} %param.4), channel_id=1, source_target_pairs={{0,8},{8,0},{1,9},{9,1},{2,10},{10,2},{3,11},{11,3},{4,12},{12,4},... | collective-permute-start | bytes 14 | tf_op jit(solution)/shard_map/ppermute | solution.py:306
  75.7 8.8 %collective-permute-start.4 = (bf16[1]{0:T(256)(128)(2,1)}, bf16[1]{0:T(256)(128)(2,1)}, u32[]{:S(2)}, u32[]{:S(2)}) collective-permute-start(bf16[1]{0:T(256)(128)(2,1)} %param.4), channel_id=1, source_target_pairs={{0,16},{16,32},{32,48},{48,64},{64,80},{80,96},{96,112},{112,0},{1... | collective-permute-start | bytes 14 | tf_op jit(solution)/shard_map/ppermute | solution.py:306
  78.2 6.9 %collective-permute-start.6 = (bf16[1]{0:T(256)(128)(2,1)}, bf16[1]{0:T(256)(128)(2,1)}, u32[]{:S(2)}, u32[]{:S(2)}) collective-permute-start(bf16[1]{0:T(256)(128)(2,1)} %param.4), channel_id=1, source_target_pairs={{0,112},{16,0},{32,16},{48,32},{64,48},{80,64},{96,80},{112,96},{1... | collective-permute-start | bytes 14 | tf_op jit(solution)/shard_map/ppermute | solution.py:306
  79.1 77.6 %collective-permute-start.8 = (bf16[1024,768]{1,0:T(8,128)(2,1)}, bf16[1024,768]{1,0:T(8,128)(2,1)}, u32[]{:S(2)}, u32[]{:S(2)}) collective-permute-start(bf16[1024,768]{1,0:T(8,128)(2,1)} %dynamic_slice.19.own_low), channel_id=1, source_target_pairs={{0,16},{16,32},{32,48},{48,64},{64,80},{80,96},{96,112},{112,0},{1... | collective-permute-start | bytes 4718600 | tf_op jit(solution)/shard_map/ppermute | solution.py:294
  81.8 78.3 %collective-permute-start.9 = (bf16[1024,768]{1,0:T(8,128)(2,1)}, bf16[1024,768]{1,0:T(8,128)(2,1)}, u32[]{:S(2)}, u32[]{:S(2)}) collective-permute-start(bf16[1024,768]{1,0:T(8,128)(2,1)} %slice_bitcast_fusion.own_high), channel_id=1, source_target_pairs={{0,112},{16,0},{32,16},{48,32},{64,48},{80,64},{96,80},{112,96},{1... | collective-permute-start | bytes 4718600 | tf_op jit(solution)/shard_map/ppermute | solution.py:297
  88.7 41.0 %collective-permute-start.14 = (bf16[2,96,768]{2,1,0:T(8,128)(2,1)}, bf16[2,96,768]{2,1,0:T(8,128)(2,1)S(1)}, u32[]{:S(2)}, u32[]{:S(2)}) collective-permute-start(bf16[2,96,768]{2,1,0:T(8,128)(2,1)} %get-tuple-element.34), channel_id=1, source_target_pairs={{0,6},{2,0},{4,2},{6,4},{1,7},{3,1},{5,3},{7,5},{8,14},{10,8},{12,... | collective-permute-start | bytes 884744 | tf_op jit(solution)/shard_map/ppermute | solution.py:44
  92.9 25.6 %collective-permute-start.3 = (bf16[96,768]{1,0:T(8,128)(2,1)S(1)}, bf16[96,768]{1,0:T(8,128)(2,1)S(1)}, u32[]{:S(2)}, u32[]{:S(2)}) collective-permute-start(bf16[96,768]{1,0:T(8,128)(2,1)S(1)} %get-tuple-element.42), channel_id=1, source_target_pairs={{0,16},{16,32},{32,48},{48,64},{64,80},{80,96},{96,112},{112,0},{1... | collective-permute-start | bytes 442376 | tf_op jit(solution)/shard_map/ppermute | solution.py:294
  93.0 26.2 %collective-permute-start.5 = (bf16[96,768]{1,0:T(8,128)(2,1)S(1)}, bf16[96,768]{1,0:T(8,128)(2,1)S(1)}, u32[]{:S(2)}, u32[]{:S(2)}) collective-permute-start(bf16[96,768]{1,0:T(8,128)(2,1)S(1)} %get-tuple-element.43), channel_id=1, source_target_pairs={{0,112},{16,0},{32,16},{48,32},{64,48},{80,64},{96,80},{112,96},{1... | collective-permute-start | bytes 442376 | tf_op jit(solution)/shard_map/ppermute | solution.py:297
  120.5 36.1 %all-to-all-start.1 = ((bf16[4,2,96,768]{3,2,1,0:T(8,128)(2,1)}), bf16[4,2,96,768]{3,2,1,0:T(8,128)(2,1)}, u32[]{:S(2)}, u32[]{:S(2)}) async-start(bf16[4,2,96,768]{3,2,1,0:T(8,128)(2,1)} %broadcast_in_dim.2), calls=%async_computation.1 | async-start | bytes 2359296 | tf_op jit(solution)/shard_map/all_to_all | solution.py:243
  124.8 45.9 %collective-permute-start.26 = (bf16[1024,768]{1,0:T(8,128)(2,1)}, bf16[1024,768]{1,0:T(8,128)(2,1)}, u32[]{:S(2)}, u32[]{:S(2)}) collective-permute-start(bf16[1024,768]{1,0:T(8,128)(2,1)} %copy-done), channel_id=1, source_target_pairs={{0,8},{8,0},{1,9},{9,1},{2,10},{10,2},{3,11},{11,3},{4,12},{12,4},... | collective-permute-start | bytes 4718600 | tf_op jit(solution)/shard_map/ppermute | solution.py:300
  126.9 17.9 %collective-permute-start.13 = (bf16[2,96,768]{2,1,0:T(8,128)(2,1)}, bf16[2,96,768]{2,1,0:T(8,128)(2,1)S(1)}, u32[]{:S(2)}, u32[]{:S(2)}) collective-permute-start(bf16[2,96,768]{2,1,0:T(8,128)(2,1)} %get-tuple-element.35), channel_id=1, source_target_pairs={{0,4},{2,6},{4,0},{6,2},{1,5},{3,7},{5,1},{7,3},{8,12},{10,14},{12... | collective-permute-start | bytes 884744 | tf_op jit(solution)/shard_map/ppermute | solution.py:44
  129.8 22.3 %collective-permute-start.12 = (bf16[2,96,768]{2,1,0:T(8,128)(2,1)}, bf16[2,96,768]{2,1,0:T(8,128)(2,1)S(1)}, u32[]{:S(2)}, u32[]{:S(2)}) collective-permute-start(bf16[2,96,768]{2,1,0:T(8,128)(2,1)} %get-tuple-element.33), channel_id=1, source_target_pairs={{0,2},{2,4},{4,6},{6,0},{1,3},{3,5},{5,7},{7,1},{8,10},{10,12},{12... | collective-permute-start | bytes 884744 | tf_op jit(solution)/shard_map/ppermute | solution.py:44
  154.4 11.7 %collective-permute-start.15 = (bf16[2,96,768]{2,1,0:T(8,128)(2,1)S(1)}, bf16[2,96,768]{2,1,0:T(8,128)(2,1)}, u32[]{:S(2)}, u32[]{:S(2)}) collective-permute-start(bf16[2,96,768]{2,1,0:T(8,128)(2,1)S(1)} %get-tuple-element.31), channel_id=1, source_target_pairs={{0,8},{8,0},{1,9},{9,1},{2,10},{10,2},{3,11},{11,3},{4,12},{12,4},... | collective-permute-start | bytes 884744 | tf_op jit(solution)/shard_map/ppermute | solution.py:300
  156.6 6.3 %collective-permute-start.17 = (bf16[96,768]{1,0:T(8,128)(2,1)}, bf16[96,768]{1,0:T(8,128)(2,1)}, u32[]{:S(2)}, u32[]{:S(2)}) collective-permute-start(bf16[96,768]{1,0:T(8,128)(2,1)} %slice_bitcast_fusion.3), channel_id=1, source_target_pairs={{0,16},{8,120},{16,32},{24,8},{32,48},{40,24},{48,64},{56,40},{64,... | collective-permute-start | bytes 442376 | tf_op jit(solution)/shard_map/ppermute | solution.py:303
  156.7 58.6 %collective-permute-start.7 = (bf16[4,2,96,768]{3,2,1,0:T(8,128)(2,1)}, bf16[4,2,96,768]{3,2,1,0:T(8,128)(2,1)}, u32[]{:S(2)}, u32[]{:S(2)}) collective-permute-start(bf16[4,2,96,768]{3,2,1,0:T(8,128)(2,1)} %all-to-all-done.1.mine), channel_id=1, source_target_pairs={{0,1},{1,0},{2,3},{3,2},{4,5},{5,4},{6,7},{7,6},{8,9},{9,8},{10,11... | collective-permute-start | bytes 3538952 | tf_op jit(solution)/shard_map/ppermute | solution.py:239
  160.2 21.6 %collective-permute-start.27 = (bf16[512,768]{1,0:T(8,128)(2,1)S(1)}, bf16[512,768]{1,0:T(8,128)(2,1)S(1)}, u32[]{:S(2)}, u32[]{:S(2)}) collective-permute-start(bf16[512,768]{1,0:T(8,128)(2,1)S(1)} %get-tuple-element.39), channel_id=1, source_target_pairs={{0,16},{8,120},{16,32},{24,8},{32,48},{40,24},{48,64},{56,40},{64,... | collective-permute-start | bytes 2359304 | tf_op jit(solution)/shard_map/ppermute | solution.py:303
  162.9 35.8 %collective-permute-start.28 = (bf16[512,768]{1,0:T(8,128)(2,1)S(1)}, bf16[512,768]{1,0:T(8,128)(2,1)S(1)}, u32[]{:S(2)}, u32[]{:S(2)}) collective-permute-start(bf16[512,768]{1,0:T(8,128)(2,1)S(1)} %get-tuple-element.38), channel_id=1, source_target_pairs={{0,16},{8,120},{16,32},{24,8},{32,48},{40,24},{48,64},{56,40},{64,... | collective-permute-start | bytes 2359304 | tf_op jit(solution)/shard_map/ppermute | solution.py:303
  166.1 34.1 %collective-permute-start.29 = (bf16[512,768]{1,0:T(8,128)(2,1)S(1)}, bf16[512,768]{1,0:T(8,128)(2,1)S(1)}, u32[]{:S(2)}, u32[]{:S(2)}) collective-permute-start(bf16[512,768]{1,0:T(8,128)(2,1)S(1)} %copy-done.13), channel_id=1, source_target_pairs={{0,8},{8,0},{1,9},{9,1},{2,10},{10,2},{3,11},{11,3},{4,12},{12,4},... | collective-permute-start | bytes 2359304 | tf_op jit(solution)/shard_map/ppermute | solution.py:300
  170.7 55.2 %collective-permute-start.30 = (bf16[512,768]{1,0:T(8,128)(2,1)}, bf16[512,768]{1,0:T(8,128)(2,1)}, u32[]{:S(2)}, u32[]{:S(2)}) collective-permute-start(bf16[512,768]{1,0:T(8,128)(2,1)} %get-tuple-element.36), channel_id=1, source_target_pairs={{0,8},{8,0},{1,9},{9,1},{2,10},{10,2},{3,11},{11,3},{4,12},{12,4},... | collective-permute-start | bytes 2359304 | tf_op jit(solution)/shard_map/ppermute | solution.py:300
  182.7 20.3 %collective-permute-start.19 = (bf16[2,96,768]{2,1,0:T(8,128)(2,1)S(1)}, bf16[2,96,768]{2,1,0:T(8,128)(2,1)}, u32[]{:S(2)}, u32[]{:S(2)}) collective-permute-start(bf16[2,96,768]{2,1,0:T(8,128)(2,1)S(1)} %pad_maximum_fusion.1.refs_0_), channel_id=1, source_target_pairs={{0,2},{2,4},{4,6},{6,0},{1,3},{3,5},{5,7},{7,1},{8,10},{10,12},{12... | collective-permute-start | bytes 884744 | tf_op jit(solution)/shard_map/ppermute | solution.py:44
  199.6 8.2 %collective-permute-start.20 = (bf16[2,96,768]{2,1,0:T(8,128)(2,1)S(1)}, bf16[2,96,768]{2,1,0:T(8,128)(2,1)}, u32[]{:S(2)}, u32[]{:S(2)}) collective-permute-start(bf16[2,96,768]{2,1,0:T(8,128)(2,1)S(1)} %pad_maximum_fusion.1.refs_0_), channel_id=1, source_target_pairs={{0,4},{2,6},{4,0},{6,2},{1,5},{3,7},{5,1},{7,3},{8,12},{10,14},{12... | collective-permute-start | bytes 884744 | tf_op jit(solution)/shard_map/ppermute | solution.py:44
  201.1 12.5 %collective-permute-start.21 = (bf16[2,96,768]{2,1,0:T(8,128)(2,1)S(1)}, bf16[2,96,768]{2,1,0:T(8,128)(2,1)}, u32[]{:S(2)}, u32[]{:S(2)}) collective-permute-start(bf16[2,96,768]{2,1,0:T(8,128)(2,1)S(1)} %pad_maximum_fusion.1.refs_0_), channel_id=1, source_target_pairs={{0,6},{2,0},{4,2},{6,4},{1,7},{3,1},{5,3},{7,5},{8,14},{10,8},{12,... | collective-permute-start | bytes 884744 | tf_op jit(solution)/shard_map/ppermute | solution.py:44
  203.0 23.0 %collective-permute-start.22 = (bf16[2,96,768]{2,1,0:T(8,128)(2,1)S(1)}, bf16[2,96,768]{2,1,0:T(8,128)(2,1)S(1)}, u32[]{:S(2)}, u32[]{:S(2)}) collective-permute-start(bf16[2,96,768]{2,1,0:T(8,128)(2,1)S(1)} %pad_maximum_fusion.1.refs_0_), channel_id=1, source_target_pairs={{0,1},{1,0},{2,3},{3,2},{4,5},{5,4},{6,7},{7,6},{8,9},{9,8},{10,11... | collective-permute-start | bytes 884744 | tf_op jit(solution)/shard_map/ppermute | solution.py:239
  207.8 18.1 %collective-permute-start.23 = (bf16[2,96,768]{2,1,0:T(8,128)(2,1)}, bf16[2,96,768]{2,1,0:T(8,128)(2,1)S(1)}, u32[]{:S(2)}, u32[]{:S(2)}) collective-permute-start(bf16[2,96,768]{2,1,0:T(8,128)(2,1)} %collective-permute-done.19.refs_1_), channel_id=1, source_target_pairs={{0,1},{1,0},{2,3},{3,2},{4,5},{5,4},{6,7},{7,6},{8,9},{9,8},{10,11... | collective-permute-start | bytes 884744 | tf_op jit(solution)/shard_map/ppermute | solution.py:239
  213.6 12.4 %collective-permute-start.24 = (bf16[2,96,768]{2,1,0:T(8,128)(2,1)}, bf16[2,96,768]{2,1,0:T(8,128)(2,1)S(1)}, u32[]{:S(2)}, u32[]{:S(2)}) collective-permute-start(bf16[2,96,768]{2,1,0:T(8,128)(2,1)} %collective-permute-done.20.refs_2_), channel_id=1, source_target_pairs={{0,1},{1,0},{2,3},{3,2},{4,5},{5,4},{6,7},{7,6},{8,9},{9,8},{10,11... | collective-permute-start | bytes 884744 | tf_op jit(solution)/shard_map/ppermute | solution.py:239
  215.2 10.7 %collective-permute-start.25 = (bf16[2,96,768]{2,1,0:T(8,128)(2,1)}, bf16[2,96,768]{2,1,0:T(8,128)(2,1)S(1)}, u32[]{:S(2)}, u32[]{:S(2)}) collective-permute-start(bf16[2,96,768]{2,1,0:T(8,128)(2,1)} %collective-permute-done.21.refs_3_), channel_id=1, source_target_pairs={{0,1},{1,0},{2,3},{3,2},{4,5},{5,4},{6,7},{7,6},{8,9},{9,8},{10,11... | collective-permute-start | bytes 884744 | tf_op jit(solution)/shard_map/ppermute | solution.py:239
  (17 other events, 192.3 us)

commit v4 on v3

--- a/solution.py
+++ b/solution.py
@@ -190,7 +190,8 @@
     pieces, refs = refs[: X * C], refs[X * C :]
     partner_near, partner_far, near_a, near_b, far_a, far_b = refs[:6]
     out, full, loaded, ready, arrived, sent = refs[6:]
-    steps = near_a.shape[0] // STEP_ROWS
+    steps = loaded.shape[1] // STEP_ROWS
+    cuts = near_a.shape[0] // STEP_ROWS, far_a.shape[0] // STEP_ROWS
 
     def loading(k):
         rows = row_block(k)
@@ -200,28 +201,33 @@
         rows = row_block(k)
         return pltpu.make_async_copy(ready.at[:, rows, :], out.at[:, rows, :], sent.at[k])
 
-    for k in range(2 * steps):
+    for k in range(steps):
         loading(k).start()
     assemble_turned(where, pieces, full)
 
     def add(side, partner_dims, diagonal_dims):
-        for part, diagonals in enumerate(((near_a, far_a), (near_b, far_b))):
-
-            def step(k, carry, part=part, diagonals=diagonals):
-                local, number = row_block(k), part * steps + k
+        edges = sorted({0, *cuts, steps})
+        for start, end in zip(edges, edges[1:]):
+            sources = [
+                (first, 0) if start < cut else (second, cut)
+                for cut, first, second in zip(cuts, (near_a, far_a), (near_b, far_b))
+            ]
+
+            def step(number, carry, sources=sources):
                 rows = row_block(number)
                 loading(number).wait()
-                for place, partner, diagonal in (
-                    (side, partner_near, diagonals[0]),
-                    (1 - side, partner_far, diagonals[1]),
+                for place, partner, (diagonal, offset) in (
+                    (side, partner_near, sources[0]),
+                    (1 - side, partner_far, sources[1]),
                 ):
                     value = loaded[place, rows, :] + mm(partner[rows, :], full[0], partner_dims)
+                    local = row_block(number - offset)
                     value = value + mm(diagonal[local, :], full[1], diagonal_dims)
                     ready[place, rows, :] = value.astype(ready.dtype)
                 sending(number).start()
                 return carry
 
-            lax.fori_loop(0, steps, step, 0)
+            lax.fori_loop(start, end, step, 0)
 
     @pl.when(where[0] == 0)
     def _():
@@ -231,7 +237,7 @@
     def _():
         add(1, NT, NN)
 
-    for k in range(2 * steps):
+    for k in range(steps):
         sending(k).wait()
 
 
@@ -337,8 +343,8 @@
 
     far_a = partner_of(facing(0))
     far_b = partner_of(facing(quarter))
-    near_a = along(partner_near[:quarter])
-    near_b = along(partner_near[quarter:])
+    near_a = along(partner_near[:STEP_ROWS])
+    near_b = along(cut(partner_near, STEP_ROWS, half - STEP_ROWS))
 
     paired = (far_keep + core_swap(far_send)).astype(BF16)
     far_sums = summed_rows(paired)

time: 237 us -> 227 us (0.958)
  the two profiles are of different devices: /device:TPU:1 before, /device:TPU:7 now
where the time goes in v4:
time: 227 us
  waiting for transfers between devices  100 us (44%)
  starting transfers between devices  57 us (25%)
  Pallas kernels  36.6 us (16%)
  other arithmetic  15 us (7%)
  local copies, waits for them, and re-layouts  13.1 us (6%)
  between operations  4.87 us (2%)
    pallas_call x4, Pallas kernels, on_chip(): pl.pallas_call(kernel, in_specs=[pl.BlockSpec(memory_space=pltpu.SMEM)] +...  35.4 us
    ppermute x5, waiting for transfers between devices, partner_of(): return lax.ppermute(value, 'h', swap_h)  32.5 us
    ppermute x3, waiting for transfers between devices, behind_of(): return lax.ppermute(value, 'z', ring('z', -1))  27.7 us
    ppermute x3, waiting for transfers between devices, ahead_of(): return lax.ppermute(value, 'z', ring('z', 1))  27.3 us
    ppermute x7, starting transfers between devices, core_swap(): return lax.ppermute(value, 'c', [(0, 1), (1, 0)])  16.3 us
    dynamic_slice x5, local copies, waits for them, and re-layouts, cut(): return lax.dynamic_slice_in_dim(value, start, length, 0)  10.5 us
    ppermute x3, starting transfers between devices, behind_of(): return lax.ppermute(value, 'z', ring('z', -1))  9.7 us
    all_to_all x2, starting transfers between devices, exchanged(): return lax.all_to_all(blocks, 'x', 0, 0, tiled=True)  8.96 us
  transfers between devices with their start and end apart: 33, of which 11 were waited for; matrix products, arithmetic and copies ran while one was open for 10% of the time, Pallas kernels for 12%

profile of v4, /device:TPU:7, one launch (start us, length us, event | category | flops | bytes accessed | tf_op | source)
XLA Modules:
  0.0 226.7 jit_solution(10248552227961814585)
XLA Ops:
  0.0 2.8 %slice_bitcast_fusion.own_high = bf16[1024,768]{1,0:T(8,128)(2,1)} fusion(bf16[2048,1,768]{2,0,1:T(8,128)(2,1)} %param.3), kind=kLoop, calls=%fused_computation.2 | loop fusion | bytes 3145728 | tf_op jit(solution)/shard_map/dynamic_slice | solution.py:315
  4.1 5.6 %collective-permute-start = (bf16[1024,768]{1,0:T(8,128)(2,1)}, bf16[1024,768]{1,0:T(8,128)(2,1)S(1)}, u32[]{:S(2)}, u32[]{:S(2)}) collective-permute-start(bf16[1024,768]{1,0:T(8,128)(2,1)} %dynamic_slice.22.own_low), channel_id=1, source_target_pairs={{0,112},{16,0},{32,16},{48,32},{64,48},{80,64},{96,80},{112,96},{1... | collective-permute-start | bytes 4718600 | tf_op jit(solution)/shard_map/ppermute | solution.py:303
  9.6 2.7 %constant_dynamic-slice_fusion.1 = bf16[1024,768]{1,0:T(8,128)(2,1)} fusion(bf16[2048,768]{1,0:T(8,128)(2,1)} %bitcast.73, s32[]{:T(128)S(6)} %select_n.42), kind=kLoop, calls=%fused_computation.51 | loop fusion | bytes 3145732 | tf_op jit(solution)/shard_map/dynamic_slice | solution.py:315
  12.3 2.9 %collective-permute-start.10 = (bf16[1024,768]{1,0:T(8,128)(2,1)}, bf16[1024,768]{1,0:T(8,128)(2,1)S(1)}, u32[]{:S(2)}, u32[]{:S(2)}) collective-permute-start(bf16[1024,768]{1,0:T(8,128)(2,1)} %constant_dynamic-slice_fusion.1), channel_id=1, source_target_pairs={{0,8},{8,0},{1,9},{9,1},{2,10},{10,2},{3,11},{11,3},{4,12},{12,4},... | collective-permute-start | bytes 4718600 | tf_op jit(solution)/shard_map/ppermute | solution.py:306
  15.3 27.7 %collective-permute-done.behind.behind0 = bf16[1024,768]{1,0:T(8,128)(2,1)S(1)} collective-permute-done((bf16[1024,768]{1,0:T(8,128)(2,1)}, bf16[1024,768]{1,0:T(8,128)(2,1)S(1)}, u32[]{:S(2)}, u32[]{:S(2)}) %collective-permute-start) | collective-permute-done | bytes 1572896 | tf_op jit(solution)/shard_map/ppermute | solution.py:303
  43.0 3.1 %collective-permute-done.1.ahead.ahead1 = bf16[1024,768]{1,0:T(8,128)(2,1)} collective-permute-done((bf16[1024,768]{1,0:T(8,128)(2,1)}, bf16[1024,768]{1,0:T(8,128)(2,1)}, u32[]{:S(2)}, u32[]{:S(2)}) %collective-permute-start.1) | collective-permute-done | bytes 1572896 | tf_op jit(solution)/shard_map/ppermute | solution.py:300
  46.2 7.5 %shard_map.38 = (f32[4,2,96,768]{3,2,1,0:T(8,128)}, f32[4,2,96,768]{3,2,1,0:T(8,128)}) custom-call(s32[3]{0:T(128)S(1)} %pad_add_fusion.value.where, bf16[1024,768]{1,0:T(8,128)(2,1)} %slice_bitcast_fusion.own_high, bf16[1024,768]{1,0:T(8,128)(2,1)S(1)} %collective-permute-done.behind.behind0, bf16[1024,768]{1,0:T(8,128)(2,1)} %collective-permute-done.1.ahead.ahead1, ...), custom_call_target="tpu_custom_call" | custom-call | flops 2415919104 | bytes 2415919 | tf_op jit(solution)/shard_map/pallas_call | solution.py:25
  55.6 2.7 %constant_dynamic-slice_fusion.own = bf16[1024,768]{1,0:T(8,128)(2,1)} fusion(bf16[2048,768]{1,0:T(8,128)(2,1)} %bitcast.74, s32[]{:T(128)S(6)} %select_n.43), kind=kLoop, calls=%fused_computation.50 | loop fusion | bytes 3145732 | tf_op jit(solution)/shard_map/dynamic_slice | solution.py:315
  58.3 7.4 %shard_map.40 = (f32[4,2,96,768]{3,2,1,0:T(8,128)}, f32[4,2,96,768]{3,2,1,0:T(8,128)}) custom-call(s32[3]{0:T(128)S(1)} %pad_add_fusion.value.where, bf16[1024,768]{1,0:T(8,128)(2,1)S(1)} %collective-permute-done.behind.behind0, bf16[1024,768]{1,0:T(8,128)(2,1)S(1)} %collective-permute-done.10.partner.refs_8_, ...), custom_call_target="tpu_custom_call" | custom-call | flops 2415919104 | bytes 2415919 | tf_op jit(solution)/shard_map/pallas_call | solution.py:25
  65.9 2.9 %add_convert_fusion = bf16[4,2,96,768]{3,2,1,0:T(8,128)(2,1)} fusion(f32[4,2,96,768]{3,2,1,0:T(8,128)S(1)} %copy-done.6, f32[4,2,96,768]{3,2,1,0:T(8,128)} %collective-permute-done.2), kind=kLoop, calls=%fused_computation.1 | loop fusion | flops 1179648 | bytes 5898240 | tf_op jit(solution)/shard_map/convert_element_type | solution.py:349
  68.8 4.4 %all-to-all-start = ((bf16[4,2,96,768]{3,2,1,0:T(8,128)(2,1)}), bf16[4,2,96,768]{3,2,1,0:T(8,128)(2,1)}, u32[]{:S(2)}, u32[]{:S(2)}) async-start(bf16[4,2,96,768]{3,2,1,0:T(8,128)(2,1)} %add_convert_fusion), calls=%async_computation | async-start | bytes 2359296 | tf_op jit(solution)/shard_map/all_to_all | solution.py:249
  73.2 2.9 %collective-permute-start.16 = (bf16[1]{0:T(256)(128)(2,1)}, bf16[1]{0:T(256)(128)(2,1)}, u32[]{:S(2)}, u32[]{:S(2)}) collective-permute-start(bf16[1]{0:T(256)(128)(2,1)} %param.4), channel_id=1, source_target_pairs={{0,8},{8,0},{1,9},{9,1},{2,10},{10,2},{3,11},{11,3},{4,12},{12,4},... | collective-permute-start | bytes 14 | tf_op jit(solution)/shard_map/ppermute | solution.py:312
  76.1 2.4 %collective-permute-start.18 = (bf16[1]{0:T(256)(128)(2,1)}, bf16[1]{0:T(256)(128)(2,1)}, u32[]{:S(2)}, u32[]{:S(2)}) collective-permute-start(bf16[1]{0:T(256)(128)(2,1)} %param.4), channel_id=1, source_target_pairs={{0,120},{8,16},{16,8},{24,32},{32,24},{40,48},{48,40},{56,64},{64,... | collective-permute-start | bytes 14 | tf_op jit(solution)/shard_map/ppermute | solution.py:312
  86.5 3.0 %fusion.7 = (bf16[2,96,768]{2,1,0:T(8,128)(2,1)}, bf16[2,96,768]{2,1,0:T(8,128)(2,1)}, bf16[2,96,768]{2,1,0:T(8,128)(2,1)}) fusion(f32[4,2,96,768]{3,2,1,0:T(8,128)} %collective-permute-done.11, f32[4,2,96,768]{3,2,1,0:T(8,128)} %get-tuple-element.24), kind=kLoop, calls=%fused_computation.16 | loop fusion | flops 884736 | bytes 4423680 | tf_op jit(solution)/shard_map/convert_element_type | solution.py:266
  91.7 2.7 %collective-permute-start.5 = (bf16[96,768]{1,0:T(8,128)(2,1)S(1)}, bf16[96,768]{1,0:T(8,128)(2,1)S(1)}, u32[]{:S(2)}, u32[]{:S(2)}) collective-permute-start(bf16[96,768]{1,0:T(8,128)(2,1)S(1)} %get-tuple-element.41), channel_id=1, source_target_pairs={{0,112},{16,0},{32,16},{48,32},{64,48},{80,64},{96,80},{112,96},{1... | collective-permute-start | bytes 442376 | tf_op jit(solution)/shard_map/ppermute | solution.py:303
  94.4 24.2 %collective-permute-done.3 = bf16[96,768]{1,0:T(8,128)(2,1)S(1)} collective-permute-done((bf16[96,768]{1,0:T(8,128)(2,1)S(1)}, bf16[96,768]{1,0:T(8,128)(2,1)S(1)}, u32[]{:S(2)}, u32[]{:S(2)}) %collective-permute-start.3) | collective-permute-done | bytes 147488 | tf_op jit(solution)/shard_map/ppermute | solution.py:300
  118.6 2.7 %collective-permute-start.26 = (bf16[1024,768]{1,0:T(8,128)(2,1)}, bf16[1024,768]{1,0:T(8,128)(2,1)}, u32[]{:S(2)}, u32[]{:S(2)}) collective-permute-start(bf16[1024,768]{1,0:T(8,128)(2,1)} %constant_dynamic-slice_fusion.own), channel_id=1, source_target_pairs={{0,8},{8,0},{1,9},{9,1},{2,10},{10,2},{3,11},{11,3},{4,12},{12,4},... | collective-permute-start | bytes 4718600 | tf_op jit(solution)/shard_map/ppermute | solution.py:306
  125.7 4.5 %all-to-all-start.1 = ((bf16[4,2,96,768]{3,2,1,0:T(8,128)(2,1)}), bf16[4,2,96,768]{3,2,1,0:T(8,128)(2,1)}, u32[]{:S(2)}, u32[]{:S(2)}) async-start(bf16[4,2,96,768]{3,2,1,0:T(8,128)(2,1)} %broadcast_in_dim.2), calls=%async_computation.1 | async-start | bytes 2359296 | tf_op jit(solution)/shard_map/all_to_all | solution.py:249
  130.2 4.1 %collective-permute-done.12 = bf16[2,96,768]{2,1,0:T(8,128)(2,1)} collective-permute-done((bf16[2,96,768]{2,1,0:T(8,128)(2,1)}, bf16[2,96,768]{2,1,0:T(8,128)(2,1)}, u32[]{:S(2)}, u32[]{:S(2)}) %collective-permute-start.12) | collective-permute-done | bytes 294944 | tf_op jit(solution)/shard_map/ppermute | solution.py:44
  134.3 2.5 %fusion.27 = (bf16[2,96,768]{2,1,0:T(8,128)(2,1)S(1)}, f32[2,96,768]{2,1,0:T(8,128)}) fusion(bf16[2,96,768]{2,1,0:T(8,128)(2,1)} %copy-done.8, bf16[2,96,768]{2,1,0:T(8,128)(2,1)} %collective-permute-done.13, bf16[2,96,768]{2,1,0:T(8,128)(2,1)} %collective-permute-done.12, f32[4,2,96,768]{3,2,1,0:T(8,128)} %collective-permute-done.11, ...), kind=kLoop, calls=%fused_computation.56 | loop fusion | flops 1179648 | bytes 2949120 | tf_op jit(solution)/shard_map/convert_element_type | solution.py:359
  137.1 2.7 %slice_select_fusion = (bf16[512,768]{1,0:T(8,128)(2,1)}, bf16[512,768]{1,0:T(8,128)(2,1)}) fusion(bf16[1024,768]{1,0:T(8,128)(2,1)} %collective-permute-done.1.ahead.ahead1, bf16[1024,768]{1,0:T(8,128)(2,1)S(1)} %collective-permute-done.behind.behind0, pred[]{:T(512)} %eq.3), kind=kLoop, calls=%fused_computation.3 | loop fusion | flops 786432 | bytes 4718593 | tf_op jit(solution)/shard_map/jit(_where)/select_n | solution.py:342
  139.8 2.7 %collective-permute-start.29 = (bf16[512,768]{1,0:T(8,128)(2,1)}, bf16[512,768]{1,0:T(8,128)(2,1)}, u32[]{:S(2)}, u32[]{:S(2)}) collective-permute-start(bf16[512,768]{1,0:T(8,128)(2,1)} %get-tuple-element.37), channel_id=1, source_target_pairs={{0,8},{8,0},{1,9},{9,1},{2,10},{10,2},{3,11},{11,3},{4,12},{12,4},... | collective-permute-start | bytes 2359304 | tf_op jit(solution)/shard_map/ppermute | solution.py:306
  142.8 6.3 %collective-permute-start.7 = (bf16[4,2,96,768]{3,2,1,0:T(8,128)(2,1)}, bf16[4,2,96,768]{3,2,1,0:T(8,128)(2,1)}, u32[]{:S(2)}, u32[]{:S(2)}) collective-permute-start(bf16[4,2,96,768]{3,2,1,0:T(8,128)(2,1)} %all-to-all-done.1.mine), channel_id=1, source_target_pairs={{0,1},{1,0},{2,3},{3,2},{4,5},{5,4},{6,7},{7,6},{8,9},{9,8},{10,11... | collective-permute-start | bytes 3538952 | tf_op jit(solution)/shard_map/ppermute | solution.py:245
  149.0 11.3 %collective-permute-done.15 = bf16[2,96,768]{2,1,0:T(8,128)(2,1)} collective-permute-done((bf16[2,96,768]{2,1,0:T(8,128)(2,1)S(1)}, bf16[2,96,768]{2,1,0:T(8,128)(2,1)}, u32[]{:S(2)}, u32[]{:S(2)}) %collective-permute-start.15) | collective-permute-done | bytes 294944 | tf_op jit(solution)/shard_map/ppermute | solution.py:306
  161.4 4.5 %collective-permute-done.17 = bf16[96,768]{1,0:T(8,128)(2,1)S(1)} collective-permute-done((bf16[96,768]{1,0:T(8,128)(2,1)S(1)}, bf16[96,768]{1,0:T(8,128)(2,1)S(1)}, u32[]{:S(2)}, u32[]{:S(2)}) %collective-permute-start.17) | collective-permute-done | bytes 147488 | tf_op jit(solution)/shard_map/ppermute | solution.py:309
  168.0 2.1 collective-permute-done.27.refs_10_
  171.6 5.5 %collective-permute-done.29.refs_12_ = bf16[512,768]{1,0:T(8,128)(2,1)} collective-permute-done((bf16[512,768]{1,0:T(8,128)(2,1)}, bf16[512,768]{1,0:T(8,128)(2,1)}, u32[]{:S(2)}, u32[]{:S(2)}) %collective-permute-start.29) | collective-permute-done | bytes 786464 | tf_op jit(solution)/shard_map/ppermute | solution.py:306
  178.3 15.7 %collective-permute-done.30.refs_13_ = bf16[512,768]{1,0:T(8,128)(2,1)} collective-permute-done((bf16[512,768]{1,0:T(8,128)(2,1)}, bf16[512,768]{1,0:T(8,128)(2,1)}, u32[]{:S(2)}, u32[]{:S(2)}) %collective-permute-start.30) | collective-permute-done | bytes 786464 | tf_op jit(solution)/shard_map/ppermute | solution.py:306
  195.8 3.6 %collective-permute-start.22 = (bf16[2,96,768]{2,1,0:T(8,128)(2,1)S(1)}, bf16[2,96,768]{2,1,0:T(8,128)(2,1)S(1)}, u32[]{:S(2)}, u32[]{:S(2)}) collective-permute-start(bf16[2,96,768]{2,1,0:T(8,128)(2,1)S(1)} %pad_maximum_fusion.1.refs_0_), channel_id=1, source_target_pairs={{0,1},{1,0},{2,3},{3,2},{4,5},{5,4},{6,7},{7,6},{8,9},{9,8},{10,11... | collective-permute-start | bytes 884744 | tf_op jit(solution)/shard_map/ppermute | solution.py:245
  201.2 4.1 %collective-permute-start.24 = (bf16[2,96,768]{2,1,0:T(8,128)(2,1)}, bf16[2,96,768]{2,1,0:T(8,128)(2,1)S(1)}, u32[]{:S(2)}, u32[]{:S(2)}) collective-permute-start(bf16[2,96,768]{2,1,0:T(8,128)(2,1)} %collective-permute-done.20.refs_2_), channel_id=1, source_target_pairs={{0,1},{1,0},{2,3},{3,2},{4,5},{5,4},{6,7},{7,6},{8,9},{9,8},{10,11... | collective-permute-start | bytes 884744 | tf_op jit(solution)/shard_map/ppermute | solution.py:245
  206.0 10.0 %shard_map.39.total = f32[2,1024,768]{2,1,0:T(8,128)} custom-call(s32[3]{0:T(128)S(1)} %copy-done.4, bf16[4,2,96,768]{3,2,1,0:T(8,128)(2,1)} %all-to-all-done.1.mine, bf16[4,2,96,768]{3,2,1,0:T(8,128)(2,1)} %collective-permute-done.7.other, bf16[1024,768]{1,0:T(8,128)(2,1)} %collective-permute-done.8.ahead0, ...), custom_call_target="tpu_custom_call" | custom-call | flops 4831838208 | bytes 4831838 | tf_op jit(solution)/shard_map/pallas_call | solution.py:25
  216.0 10.5 %shard_map.41 = bf16[2,1024,768]{2,1,0:T(8,128)(2,1)} custom-call(s32[3]{0:T(128)S(1)} %copy-done.3, f32[2,1024,768]{2,1,0:T(8,128)} %shard_map.39.total, bf16[2,96,768]{2,1,0:T(8,128)(2,1)S(1)} %pad_maximum_fusion.1.refs_0_, bf16[2,96,768]{2,1,0:T(8,128)(2,1)} %collective-permute-done.19.refs_1_, bf16[2,96,768]{2,1,0:T(8,128)(2,1)} %collective-permute-done.20.refs_2_, ...), custom_call_target="tpu_custom_call" | custom-call | flops 4831838208 | bytes 4831838 | tf_op jit(solution)/shard_map/pallas_call | solution.py:25
  (83 shorter events, 24.2 us)
Async XLA Ops:
  4.1 39.0 %collective-permute-start = (bf16[1024,768]{1,0:T(8,128)(2,1)}, bf16[1024,768]{1,0:T(8,128)(2,1)S(1)}, u32[]{:S(2)}, u32[]{:S(2)}) collective-permute-start(bf16[1024,768]{1,0:T(8,128)(2,1)} %dynamic_slice.22.own_low), channel_id=1, source_target_pairs={{0,112},{16,0},{32,16},{48,32},{64,48},{80,64},{96,80},{112,96},{1... | collective-permute-start | bytes 4718600 | tf_op jit(solution)/shard_map/ppermute | solution.py:303
  9.6 36.5 %collective-permute-start.1 = (bf16[1024,768]{1,0:T(8,128)(2,1)}, bf16[1024,768]{1,0:T(8,128)(2,1)}, u32[]{:S(2)}, u32[]{:S(2)}) collective-permute-start(bf16[1024,768]{1,0:T(8,128)(2,1)} %slice_bitcast_fusion.own_high), channel_id=1, source_target_pairs={{0,16},{16,32},{32,48},{48,64},{64,80},{80,96},{96,112},{112,0},{1... | collective-permute-start | bytes 4718600 | tf_op jit(solution)/shard_map/ppermute | solution.py:300
  12.3 46.0 %collective-permute-start.10 = (bf16[1024,768]{1,0:T(8,128)(2,1)}, bf16[1024,768]{1,0:T(8,128)(2,1)S(1)}, u32[]{:S(2)}, u32[]{:S(2)}) collective-permute-start(bf16[1024,768]{1,0:T(8,128)(2,1)} %constant_dynamic-slice_fusion.1), channel_id=1, source_target_pairs={{0,8},{8,0},{1,9},{9,1},{2,10},{10,2},{3,11},{11,3},{4,12},{12,4},... | collective-permute-start | bytes 4718600 | tf_op jit(solution)/shard_map/ppermute | solution.py:306
  53.7 12.1 %collective-permute-start.2 = (f32[4,2,96,768]{3,2,1,0:T(8,128)}, f32[4,2,96,768]{3,2,1,0:T(8,128)}, u32[]{:S(2)}, u32[]{:S(2)}) collective-permute-start(f32[4,2,96,768]{3,2,1,0:T(8,128)} %get-tuple-element.19), channel_id=1, source_target_pairs={{0,1},{1,0},{2,3},{3,2},{4,5},{5,4},{6,7},{7,6},{8,9},{9,8},{10,11... | collective-permute-start | bytes 7077896 | tf_op jit(solution)/shard_map/ppermute | solution.py:245
  65.7 20.7 %collective-permute-start.11 = (f32[4,2,96,768]{3,2,1,0:T(8,128)}, f32[4,2,96,768]{3,2,1,0:T(8,128)}, u32[]{:S(2)}, u32[]{:S(2)}) collective-permute-start(f32[4,2,96,768]{3,2,1,0:T(8,128)} %get-tuple-element.25), channel_id=1, source_target_pairs={{0,1},{1,0},{2,3},{3,2},{4,5},{5,4},{6,7},{7,6},{8,9},{9,8},{10,11... | collective-permute-start | bytes 7077896 | tf_op jit(solution)/shard_map/ppermute | solution.py:245
  68.8 21.3 %all-to-all-start = ((bf16[4,2,96,768]{3,2,1,0:T(8,128)(2,1)}), bf16[4,2,96,768]{3,2,1,0:T(8,128)(2,1)}, u32[]{:S(2)}, u32[]{:S(2)}) async-start(bf16[4,2,96,768]{3,2,1,0:T(8,128)(2,1)} %add_convert_fusion), calls=%async_computation | async-start | bytes 2359296 | tf_op jit(solution)/shard_map/all_to_all | solution.py:249
  73.2 6.3 %collective-permute-start.16 = (bf16[1]{0:T(256)(128)(2,1)}, bf16[1]{0:T(256)(128)(2,1)}, u32[]{:S(2)}, u32[]{:S(2)}) collective-permute-start(bf16[1]{0:T(256)(128)(2,1)} %param.4), channel_id=1, source_target_pairs={{0,8},{8,0},{1,9},{9,1},{2,10},{10,2},{3,11},{11,3},{4,12},{12,4},... | collective-permute-start | bytes 14 | tf_op jit(solution)/shard_map/ppermute | solution.py:312
  76.1 9.1 %collective-permute-start.4 = (bf16[1]{0:T(256)(128)(2,1)}, bf16[1]{0:T(256)(128)(2,1)}, u32[]{:S(2)}, u32[]{:S(2)}) collective-permute-start(bf16[1]{0:T(256)(128)(2,1)} %param.4), channel_id=1, source_target_pairs={{0,16},{16,32},{32,48},{48,64},{64,80},{80,96},{96,112},{112,0},{1... | collective-permute-start | bytes 14 | tf_op jit(solution)/shard_map/ppermute | solution.py:312
  76.1 6.3 %collective-permute-start.18 = (bf16[1]{0:T(256)(128)(2,1)}, bf16[1]{0:T(256)(128)(2,1)}, u32[]{:S(2)}, u32[]{:S(2)}) collective-permute-start(bf16[1]{0:T(256)(128)(2,1)} %param.4), channel_id=1, source_target_pairs={{0,120},{8,16},{16,8},{24,32},{32,24},{40,48},{48,40},{56,64},{64,... | collective-permute-start | bytes 14 | tf_op jit(solution)/shard_map/ppermute | solution.py:312
  78.6 7.2 %collective-permute-start.6 = (bf16[1]{0:T(256)(128)(2,1)}, bf16[1]{0:T(256)(128)(2,1)}, u32[]{:S(2)}, u32[]{:S(2)}) collective-permute-start(bf16[1]{0:T(256)(128)(2,1)} %param.4), channel_id=1, source_target_pairs={{0,112},{16,0},{32,16},{48,32},{64,48},{80,64},{96,80},{112,96},{1... | collective-permute-start | bytes 14 | tf_op jit(solution)/shard_map/ppermute | solution.py:312
  79.5 62.9 %collective-permute-start.8 = (bf16[1024,768]{1,0:T(8,128)(2,1)}, bf16[1024,768]{1,0:T(8,128)(2,1)}, u32[]{:S(2)}, u32[]{:S(2)}) collective-permute-start(bf16[1024,768]{1,0:T(8,128)(2,1)} %dynamic_slice.22.own_low), channel_id=1, source_target_pairs={{0,16},{16,32},{32,48},{48,64},{64,80},{80,96},{96,112},{112,0},{1... | collective-permute-start | bytes 4718600 | tf_op jit(solution)/shard_map/ppermute | solution.py:300
  82.4 60.3 %collective-permute-start.9 = (bf16[1024,768]{1,0:T(8,128)(2,1)}, bf16[1024,768]{1,0:T(8,128)(2,1)}, u32[]{:S(2)}, u32[]{:S(2)}) collective-permute-start(bf16[1024,768]{1,0:T(8,128)(2,1)} %slice_bitcast_fusion.own_high), channel_id=1, source_target_pairs={{0,112},{16,0},{32,16},{48,32},{64,48},{80,64},{96,80},{112,96},{1... | collective-permute-start | bytes 4718600 | tf_op jit(solution)/shard_map/ppermute | solution.py:303
  89.4 33.2 %collective-permute-start.14 = (bf16[2,96,768]{2,1,0:T(8,128)(2,1)}, bf16[2,96,768]{2,1,0:T(8,128)(2,1)S(1)}, u32[]{:S(2)}, u32[]{:S(2)}) collective-permute-start(bf16[2,96,768]{2,1,0:T(8,128)(2,1)} %get-tuple-element.34), channel_id=1, source_target_pairs={{0,6},{2,0},{4,2},{6,4},{1,7},{3,1},{5,3},{7,5},{8,14},{10,8},{12,... | collective-permute-start | bytes 884744 | tf_op jit(solution)/shard_map/ppermute | solution.py:44
  91.7 26.9 %collective-permute-start.3 = (bf16[96,768]{1,0:T(8,128)(2,1)S(1)}, bf16[96,768]{1,0:T(8,128)(2,1)S(1)}, u32[]{:S(2)}, u32[]{:S(2)}) collective-permute-start(bf16[96,768]{1,0:T(8,128)(2,1)S(1)} %get-tuple-element.40), channel_id=1, source_target_pairs={{0,16},{16,32},{32,48},{48,64},{64,80},{80,96},{96,112},{112,0},{1... | collective-permute-start | bytes 442376 | tf_op jit(solution)/shard_map/ppermute | solution.py:300
  91.7 29.5 %collective-permute-start.5 = (bf16[96,768]{1,0:T(8,128)(2,1)S(1)}, bf16[96,768]{1,0:T(8,128)(2,1)S(1)}, u32[]{:S(2)}, u32[]{:S(2)}) collective-permute-start(bf16[96,768]{1,0:T(8,128)(2,1)S(1)} %get-tuple-element.41), channel_id=1, source_target_pairs={{0,112},{16,0},{32,16},{48,32},{64,48},{80,64},{96,80},{112,96},{1... | collective-permute-start | bytes 442376 | tf_op jit(solution)/shard_map/ppermute | solution.py:303
  118.6 42.8 %collective-permute-start.26 = (bf16[1024,768]{1,0:T(8,128)(2,1)}, bf16[1024,768]{1,0:T(8,128)(2,1)}, u32[]{:S(2)}, u32[]{:S(2)}) collective-permute-start(bf16[1024,768]{1,0:T(8,128)(2,1)} %constant_dynamic-slice_fusion.own), channel_id=1, source_target_pairs={{0,8},{8,0},{1,9},{9,1},{2,10},{10,2},{3,11},{11,3},{4,12},{12,4},... | collective-permute-start | bytes 4718600 | tf_op jit(solution)/shard_map/ppermute | solution.py:306
  121.3 8.9 %collective-permute-start.13 = (bf16[2,96,768]{2,1,0:T(8,128)(2,1)}, bf16[2,96,768]{2,1,0:T(8,128)(2,1)}, u32[]{:S(2)}, u32[]{:S(2)}) collective-permute-start(bf16[2,96,768]{2,1,0:T(8,128)(2,1)} %get-tuple-element.35), channel_id=1, source_target_pairs={{0,4},{2,6},{4,0},{6,2},{1,5},{3,7},{5,1},{7,3},{8,12},{10,14},{12... | collective-permute-start | bytes 884744 | tf_op jit(solution)/shard_map/ppermute | solution.py:44
  122.7 11.6 %collective-permute-start.12 = (bf16[2,96,768]{2,1,0:T(8,128)(2,1)}, bf16[2,96,768]{2,1,0:T(8,128)(2,1)}, u32[]{:S(2)}, u32[]{:S(2)}) collective-permute-start(bf16[2,96,768]{2,1,0:T(8,128)(2,1)} %get-tuple-element.33), channel_id=1, source_target_pairs={{0,2},{2,4},{4,6},{6,0},{1,3},{3,5},{5,7},{7,1},{8,10},{10,12},{12... | collective-permute-start | bytes 884744 | tf_op jit(solution)/shard_map/ppermute | solution.py:44
  125.7 17.1 %all-to-all-start.1 = ((bf16[4,2,96,768]{3,2,1,0:T(8,128)(2,1)}), bf16[4,2,96,768]{3,2,1,0:T(8,128)(2,1)}, u32[]{:S(2)}, u32[]{:S(2)}) async-start(bf16[4,2,96,768]{3,2,1,0:T(8,128)(2,1)} %broadcast_in_dim.2), calls=%async_computation.1 | async-start | bytes 2359296 | tf_op jit(solution)/shard_map/all_to_all | solution.py:249
  136.8 23.5 %collective-permute-start.15 = (bf16[2,96,768]{2,1,0:T(8,128)(2,1)S(1)}, bf16[2,96,768]{2,1,0:T(8,128)(2,1)}, u32[]{:S(2)}, u32[]{:S(2)}) collective-permute-start(bf16[2,96,768]{2,1,0:T(8,128)(2,1)S(1)} %get-tuple-element.31), channel_id=1, source_target_pairs={{0,8},{8,0},{1,9},{9,1},{2,10},{10,2},{3,11},{11,3},{4,12},{12,4},... | collective-permute-start | bytes 884744 | tf_op jit(solution)/shard_map/ppermute | solution.py:306
  139.8 37.4 %collective-permute-start.29 = (bf16[512,768]{1,0:T(8,128)(2,1)}, bf16[512,768]{1,0:T(8,128)(2,1)}, u32[]{:S(2)}, u32[]{:S(2)}) collective-permute-start(bf16[512,768]{1,0:T(8,128)(2,1)} %get-tuple-element.37), channel_id=1, source_target_pairs={{0,8},{8,0},{1,9},{9,1},{2,10},{10,2},{3,11},{11,3},{4,12},{12,4},... | collective-permute-start | bytes 2359304 | tf_op jit(solution)/shard_map/ppermute | solution.py:306
  142.5 51.5 %collective-permute-start.30 = (bf16[512,768]{1,0:T(8,128)(2,1)}, bf16[512,768]{1,0:T(8,128)(2,1)}, u32[]{:S(2)}, u32[]{:S(2)}) collective-permute-start(bf16[512,768]{1,0:T(8,128)(2,1)} %get-tuple-element.36), channel_id=1, source_target_pairs={{0,8},{8,0},{1,9},{9,1},{2,10},{10,2},{3,11},{11,3},{4,12},{12,4},... | collective-permute-start | bytes 2359304 | tf_op jit(solution)/shard_map/ppermute | solution.py:306
  142.8 62.5 %collective-permute-start.7 = (bf16[4,2,96,768]{3,2,1,0:T(8,128)(2,1)}, bf16[4,2,96,768]{3,2,1,0:T(8,128)(2,1)}, u32[]{:S(2)}, u32[]{:S(2)}) collective-permute-start(bf16[4,2,96,768]{3,2,1,0:T(8,128)(2,1)} %all-to-all-done.1.mine), channel_id=1, source_target_pairs={{0,1},{1,0},{2,3},{3,2},{4,5},{5,4},{6,7},{7,6},{8,9},{9,8},{10,11... | collective-permute-start | bytes 3538952 | tf_op jit(solution)/shard_map/ppermute | solution.py:245
  161.4 8.7 %collective-permute-start.27 = (bf16[256,768]{1,0:T(8,128)(2,1)S(1)}, bf16[256,768]{1,0:T(8,128)(2,1)S(1)}, u32[]{:S(2)}, u32[]{:S(2)}) collective-permute-start(bf16[256,768]{1,0:T(8,128)(2,1)S(1)} %slice.95), channel_id=1, source_target_pairs={{0,16},{8,120},{16,32},{24,8},{32,48},{40,24},{48,64},{56,40},{64,... | collective-permute-start | bytes 1179656 | tf_op jit(solution)/shard_map/ppermute | solution.py:309
  165.9 50.1 %collective-permute-start.28 = (bf16[768,768]{1,0:T(8,128)(2,1)}, bf16[768,768]{1,0:T(8,128)(2,1)}, u32[]{:S(2)}, u32[]{:S(2)}) collective-permute-start(bf16[768,768]{1,0:T(8,128)(2,1)} %dynamic_slice.27), channel_id=1, source_target_pairs={{0,16},{8,120},{16,32},{24,8},{32,48},{40,24},{48,64},{56,40},{64,... | collective-permute-start | bytes 3538952 | tf_op jit(solution)/shard_map/ppermute | solution.py:309
  170.9 24.9 %collective-permute-start.19 = (bf16[2,96,768]{2,1,0:T(8,128)(2,1)S(1)}, bf16[2,96,768]{2,1,0:T(8,128)(2,1)}, u32[]{:S(2)}, u32[]{:S(2)}) collective-permute-start(bf16[2,96,768]{2,1,0:T(8,128)(2,1)S(1)} %pad_maximum_fusion.1.refs_0_), channel_id=1, source_target_pairs={{0,2},{2,4},{4,6},{6,0},{1,3},{3,5},{5,7},{7,1},{8,10},{10,12},{12... | collective-permute-start | bytes 884744 | tf_op jit(solution)/shard_map/ppermute | solution.py:44
  177.1 22.3 %collective-permute-start.20 = (bf16[2,96,768]{2,1,0:T(8,128)(2,1)S(1)}, bf16[2,96,768]{2,1,0:T(8,128)(2,1)}, u32[]{:S(2)}, u32[]{:S(2)}) collective-permute-start(bf16[2,96,768]{2,1,0:T(8,128)(2,1)S(1)} %pad_maximum_fusion.1.refs_0_), channel_id=1, source_target_pairs={{0,4},{2,6},{4,0},{6,2},{1,5},{3,7},{5,1},{7,3},{8,12},{10,14},{12... | collective-permute-start | bytes 884744 | tf_op jit(solution)/shard_map/ppermute | solution.py:44
  194.0 7.2 %collective-permute-start.21 = (bf16[2,96,768]{2,1,0:T(8,128)(2,1)S(1)}, bf16[2,96,768]{2,1,0:T(8,128)(2,1)}, u32[]{:S(2)}, u32[]{:S(2)}) collective-permute-start(bf16[2,96,768]{2,1,0:T(8,128)(2,1)S(1)} %pad_maximum_fusion.1.refs_0_), channel_id=1, source_target_pairs={{0,6},{2,0},{4,2},{6,4},{1,7},{3,1},{5,3},{7,5},{8,14},{10,8},{12,... | collective-permute-start | bytes 884744 | tf_op jit(solution)/shard_map/ppermute | solution.py:44
  195.8 20.2 %collective-permute-start.22 = (bf16[2,96,768]{2,1,0:T(8,128)(2,1)S(1)}, bf16[2,96,768]{2,1,0:T(8,128)(2,1)S(1)}, u32[]{:S(2)}, u32[]{:S(2)}) collective-permute-start(bf16[2,96,768]{2,1,0:T(8,128)(2,1)S(1)} %pad_maximum_fusion.1.refs_0_), channel_id=1, source_target_pairs={{0,1},{1,0},{2,3},{3,2},{4,5},{5,4},{6,7},{7,6},{8,9},{9,8},{10,11... | collective-permute-start | bytes 884744 | tf_op jit(solution)/shard_map/ppermute | solution.py:245
  199.4 16.6 %collective-permute-start.23 = (bf16[2,96,768]{2,1,0:T(8,128)(2,1)}, bf16[2,96,768]{2,1,0:T(8,128)(2,1)S(1)}, u32[]{:S(2)}, u32[]{:S(2)}) collective-permute-start(bf16[2,96,768]{2,1,0:T(8,128)(2,1)} %collective-permute-done.19.refs_1_), channel_id=1, source_target_pairs={{0,1},{1,0},{2,3},{3,2},{4,5},{5,4},{6,7},{7,6},{8,9},{9,8},{10,11... | collective-permute-start | bytes 884744 | tf_op jit(solution)/shard_map/ppermute | solution.py:245
  201.2 14.8 %collective-permute-start.24 = (bf16[2,96,768]{2,1,0:T(8,128)(2,1)}, bf16[2,96,768]{2,1,0:T(8,128)(2,1)S(1)}, u32[]{:S(2)}, u32[]{:S(2)}) collective-permute-start(bf16[2,96,768]{2,1,0:T(8,128)(2,1)} %collective-permute-done.20.refs_2_), channel_id=1, source_target_pairs={{0,1},{1,0},{2,3},{3,2},{4,5},{5,4},{6,7},{7,6},{8,9},{9,8},{10,11... | collective-permute-start | bytes 884744 | tf_op jit(solution)/shard_map/ppermute | solution.py:245
  205.3 10.7 %collective-permute-start.25 = (bf16[2,96,768]{2,1,0:T(8,128)(2,1)}, bf16[2,96,768]{2,1,0:T(8,128)(2,1)S(1)}, u32[]{:S(2)}, u32[]{:S(2)}) collective-permute-start(bf16[2,96,768]{2,1,0:T(8,128)(2,1)} %collective-permute-done.21.refs_3_), channel_id=1, source_target_pairs={{0,1},{1,0},{2,3},{3,2},{4,5},{5,4},{6,7},{7,6},{8,9},{9,8},{10,11... | collective-permute-start | bytes 884744 | tf_op jit(solution)/shard_map/ppermute | solution.py:245
  (11 other events, 114.0 us)
